TPU v7x, 256 devices: a whole 4x4x8 slice. The times are simulated.
256 devices in a mesh: replica: 16 (over x_hi, z), tensor: 16 (over y, x_lo, core).
Axes of the slice: x: 4 (x_hi: 2, x_lo: 2; x = x_hi * 2 + x_lo), y: 4, z: 8, core: 2. Of those that a mesh axis runs over, the one named last changes fastest.
Arguments:
- hidden: bfloat16 [512, 8192], P('replica'), may hold values from -16 to 16
- q_weight: bfloat16 [8192, 4096], P(None, 'tensor'), may hold values from -0.0625 to 0.0625
- q_gain: float32 [128], replicated, may hold values from 0.1 to 1.9
- o_weight: bfloat16 [4096, 8192], P('tensor'), may hold values from -0.125 to 0.125
- attn_gate: float32 [1], replicated, may hold values from 0.5 to 1.5
- key_codes: bfloat16 [128, 512, 1024], P('replica', 'tensor'), may hold values from -96 to 96
- value_codes: bfloat16 [128, 512, 1024], P('replica', 'tensor'), may hold values from -96 to 96
- key_scales: bfloat16 [128, 16, 8], P('replica', 'tensor'), may hold values from 0.02 to 8
- value_scales: bfloat16 [128, 16, 8], P('replica', 'tensor'), may hold values from 0.019897461 to 0.119628906
- lengths: int32 [128], P('replica'), may hold values from 128 to 512
- dest_replica: int32 [16, 6], replicated, may hold values from 0 to 15, as said below
- move_slot: int32 [16, 6], P('replica'), may hold values from 0 to 7, as said below
Outputs:
- mixed: bfloat16 [512, 8192], P('replica', 'tensor')
- new_keys: bfloat16 [128, 512, 1024], P('replica', 'tensor')
- new_values: bfloat16 [128, 512, 1024], P('replica', 'tensor')
- new_key_scales: bfloat16 [128, 16, 8], P('replica', 'tensor')
- new_value_scales: bfloat16 [128, 16, 8], P('replica', 'tensor')
Inputs may be any that keep to these rules, and one draw needn't show every extreme that they name: For each j the column dest_replica[:, j] names every replica once, so each replica receives exactly 6 requests, at most one from each replica; a request may stay on its own replica. `move_slot`: the 6 slots of one replica are different.
All inputs are finite; a program needn't handle non-finite values.
Results may differ from a plain program's by a relative error of at most 0.0065.
Values may be sent and summed in bfloat16 or wider, within the bound.
No kernel may reach another device: no remote copies, remote signals or barrier semaphores. Data moves between devices by JAX's collectives and lax.ppermute only.
A program may use at most 64 MiB of HBM per device.

v0:
```python
import jax
import jax.numpy as jnp
from jax import lax
from jax.sharding import PartitionSpec as P

NEGATIVE = -1e30
EPSILON = 1e-06


def laid_out(tiles, dim):
    tiles = jnp.moveaxis(tiles, 0, dim)
    shape = tiles.shape
    return tiles.reshape(*shape[:dim], shape[dim] * shape[dim + 1], *shape[dim + 2 :])


def from_everyone(array, axis):
    copies = jnp.broadcast_to(array, (lax.axis_size(axis), *array.shape))
    return lax.all_to_all(copies, axis, split_axis=0, concat_axis=0, tiled=True)


def gather_directly(array, axis, dim):
    return laid_out(from_everyone(array, axis), dim)


def sent_together(arrays, axis, split_dim, concat_dim, along):
    columns = [a.reshape(*a.shape[:along], -1) for a in arrays]
    both = jnp.concatenate(columns, axis=along)
    result, at, done = (
        lax.all_to_all(both, axis, split_axis=split_dim, concat_axis=concat_dim, tiled=True),
        0,
        [],
    )
    for a, column in zip(arrays, columns):
        share = result[..., at : at + column.shape[along]]
        done.append(share.reshape(*share.shape[:along], *a.shape[along:]))
        at += column.shape[along]
    return tuple(done)


def cut_along(array, dim, count):
    before, after = (array.shape[:dim], array.shape[dim + 1 :])
    return jnp.moveaxis(array.reshape(*before, count, -1, *after), dim, 0)


def sent_and_summed(array, axis, dim):
    count = lax.axis_size(axis)
    tiles = lax.all_to_all(cut_along(array, dim, count), axis, 0, 0, tiled=True)
    return jnp.sum(tiles, axis=0)


def outgoing(send_table, codes):
    flat = codes.reshape(codes.shape[0], -1)
    moved = jnp.dot(send_table, flat, preferred_element_type=jnp.float32)
    return moved.astype(jnp.bfloat16).reshape((send_table.shape[0],) + codes.shape[1:])


def incoming(select, keep, received, codes):
    flat = received.reshape(received.shape[0], -1)
    placed = jnp.dot(select, flat, preferred_element_type=jnp.float32).astype(jnp.bfloat16)
    former = codes.reshape(codes.shape[0], -1)
    return jnp.where(keep[:, None], former, placed).reshape(codes.shape)


def attend(
    hidden,
    q_weight,
    q_gain,
    o_weight,
    attn_gate,
    key_codes,
    value_codes,
    key_scales,
    value_scales,
    lengths,
):
    tensors = lax.axis_size("tensor")
    rank = lax.axis_index("tensor")
    held, span, kv_width = key_codes.shape
    kv_heads = key_scales.shape[2]
    head_dim = kv_width // kv_heads
    rows = hidden.shape[0]
    drafts = rows // held
    local_heads = q_weight.shape[1] // head_dim
    projected = jnp.dot(hidden, q_weight, preferred_element_type=jnp.float32).reshape(
        rows, local_heads, head_dim
    )
    projected = projected * lax.rsqrt(
        jnp.mean(projected * projected, axis=-1, keepdims=True) + EPSILON
    )
    query = (projected * q_gain * head_dim ** (-0.5)).astype(jnp.bfloat16)
    every_head = gather_directly(query, "tensor", 1)
    heads = every_head.shape[1]
    grouped = every_head.reshape(held, drafts, kv_heads, heads // kv_heads, head_dim)
    keys = key_codes.reshape(held, span, kv_heads, head_dim)
    values = value_codes.reshape(held, span, kv_heads, head_dim)
    scores = jnp.einsum("rsngd,rtnd->rsngt", grouped, keys, preferred_element_type=jnp.float32)
    scores = scores * key_scales[:, 0, :].astype(jnp.float32)[:, None, :, None, None]
    position = rank * span + jnp.arange(span, dtype=jnp.int32)
    valid = (position[None, :] < lengths[:, None])[:, None, None, None, :]
    block_max = jnp.max(jnp.where(valid, scores, NEGATIVE), axis=-1)
    weights = jnp.where(valid, jnp.exp(scores - block_max[..., None]), 0.0)
    block_sum = jnp.sum(weights, axis=-1)
    block_out = jnp.einsum(
        "rsngt,rtnd->rsngd",
        weights.astype(jnp.bfloat16),
        values,
        preferred_element_type=jnp.float32,
    )
    block_out = block_out * value_scales[:, 0, :].astype(jnp.float32)[:, None, :, None, None]
    partial_value = (
        block_max.reshape(rows, heads),
        block_sum.reshape(rows, heads),
        block_out.reshape(rows, heads, head_dim),
    )
    peaks, totals, pieces = (
        lax.all_to_all(partial_value[0], "tensor", split_axis=1, concat_axis=0, tiled=True),
        *sent_together((partial_value[1], partial_value[2]), "tensor", 1, 0, 2),
    )
    peaks = peaks.reshape(tensors, rows, local_heads)
    top = jnp.max(peaks, axis=0)
    factor = jnp.exp(peaks - top[None])
    total = jnp.sum(totals.reshape(tensors, rows, local_heads) * factor, axis=0)
    summed = jnp.sum(
        pieces.reshape(tensors, rows, local_heads, head_dim) * factor[..., None], axis=0
    )
    attended = (
        (summed / total[..., None]).astype(jnp.bfloat16).reshape(rows, local_heads * head_dim)
    )
    terms = jnp.dot(attended, o_weight, preferred_element_type=jnp.float32)
    shares = sent_and_summed(terms, "tensor", 1)
    width = shares.shape[1]
    residual = lax.dynamic_slice_in_dim(hidden, rank * width, width, 1).astype(jnp.float32)
    return (residual + jnp.tanh(attn_gate[0]) * shares).astype(jnp.bfloat16)


def local(
    hidden,
    q_weight,
    q_gain,
    o_weight,
    attn_gate,
    key_codes,
    value_codes,
    key_scales,
    value_scales,
    lengths,
    dest_replica,
    move_slot,
):
    replicas = lax.axis_size("replica")
    here = lax.axis_index("replica")
    held = key_codes.shape[0]
    slots = move_slot[0]
    own_dest = lax.dynamic_index_in_dim(dest_replica, here, 0, keepdims=False)
    replica_ids = jnp.arange(replicas, dtype=jnp.int32)
    slot_ids = jnp.arange(held, dtype=jnp.int32)
    slot_match = slots[:, None] == slot_ids[None, :]
    send_table = jnp.any(
        (own_dest[:, None, None] == replica_ids[None, :, None]) & slot_match[:, None, :], axis=0
    ).astype(jnp.bfloat16)
    arrive = dest_replica == here
    select = jnp.any(slot_match.T[:, None, :] & arrive[None, :, :], axis=2).astype(jnp.bfloat16)
    keep = jnp.logical_not(jnp.any(slot_match, axis=0))
    received = sent_together(
        (
            outgoing(send_table, key_codes),
            outgoing(send_table, value_codes),
            outgoing(send_table, key_scales),
            outgoing(send_table, value_scales),
        ),
        "replica",
        0,
        0,
        1,
    )
    new_keys = incoming(select, keep, received[0], key_codes)
    new_values = incoming(select, keep, received[1], value_codes)
    new_key_scales = incoming(select, keep, received[2], key_scales)
    new_value_scales = incoming(select, keep, received[3], value_scales)
    mixed = attend(
        hidden,
        q_weight,
        q_gain,
        o_weight,
        attn_gate,
        key_codes,
        value_codes,
        key_scales,
        value_scales,
        lengths,
    )
    return (mixed, new_keys, new_values, new_key_scales, new_value_scales)


def solution(mesh):
    return jax.shard_map(
        local,
        mesh=mesh,
        in_specs=(
            P("replica", None),
            P(None, "tensor"),
            P(),
            P("tensor", None),
            P(),
            P("replica", "tensor", None),
            P("replica", "tensor", None),
            P("replica", "tensor", None),
            P("replica", "tensor", None),
            P("replica"),
            P(),
            P("replica", None),
        ),
        out_specs=(
            P("replica", "tensor"),
            P("replica", "tensor", None),
            P("replica", "tensor", None),
            P("replica", "tensor", None),
            P("replica", "tensor", None),
        ),
        check_vma=False,
    )
```

profile of v0, /device:TPU:32, one launch (start us, length us, event | category | flops | bytes accessed | tf_op | source)
XLA Modules:
  0.0 155.7 jit_solution(13727029361715227020)
XLA Ops:
  0.7 3.2 %fusion.35 = f32[32,256]{1,0:T(8,128)S(1)} fusion(bf16[32,8192]{1,0:T(8,128)(2,1)} %param.12, bf16[8192,256]{1,0:T(8,128)(2,1)} %param.13), kind=kOutput, calls=%fused_computation.72 | convolution fusion | flops 134217728 | bytes 4751360 | tf_op jit(solution)/shard_map/dot_general | solution.py:84
  5.0 5.5 %all-to-all-start = ((bf16[16,32,2,128]{3,1,2,0:T(8,128)(2,1)}), bf16[16,32,2,128]{3,1,2,0:T(8,128)(2,1)S(1)}, u32[]{:S(2)}, u32[]{:S(2)}) async-start(bf16[16,32,2,128]{3,1,2,0:T(8,128)(2,1)} %broadcast_in_dim.65), calls=%async_computation | async-start | bytes 524288 | tf_op jit(solution)/shard_map/all_to_all | solution.py:18
  11.0 7.6 %all-to-all-done = bf16[16,32,2,128]{3,1,2,0:T(8,128)(2,1)S(1)} async-done(((bf16[16,32,2,128]{3,1,2,0:T(8,128)(2,1)}), bf16[16,32,2,128]{3,1,2,0:T(8,128)(2,1)S(1)}, u32[]{:S(2)}, u32[]{:S(2)}) %all-to-all-start) | async-done | bytes 262176 | tf_op jit(solution)/shard_map/all_to_all | solution.py:18
  19.1 0.8 fusion.15
  21.1 1.6 %copy.145 = f32[32,32,129]{2,0,1:T(8,128)} copy(f32[32,32,129]{2,1,0:T(8,128)S(1)} %pad_maximum_fusion) | data formatting | bytes 1056768 | tf_op jit(solution)/shard_map/concatenate | solution.py:27
  22.7 3.7 %all-to-all-start.1 = ((f32[32,32,129]{2,0,1:T(8,128)}), f32[32,32,129]{2,0,1:T(8,128)S(1)}, u32[]{:S(2)}, u32[]{:S(2)}) async-start(f32[32,32,129]{2,0,1:T(8,128)} %copy.145), calls=%async_computation.1 | async-start | bytes 2097152 | tf_op jit(solution)/shard_map/all_to_all | solution.py:29
  26.4 6.4 %copy.163 = bf16[8192,256]{1,0:T(8,128)(2,1)} copy(bf16[8192,256]{0,1:T(8,128)(2,1)} %bitcast.112) | data formatting | bytes 8388608 | tf_op jit(solution)/shard_map/dot_general | solution.py:129
  34.4 8.5 %all-to-all-done.1 = f32[32,32,129]{2,0,1:T(8,128)S(1)} async-done(((f32[32,32,129]{2,0,1:T(8,128)}), f32[32,32,129]{2,0,1:T(8,128)S(1)}, u32[]{:S(2)}, u32[]{:S(2)}) %all-to-all-start.1) | async-done | bytes 528416 | tf_op jit(solution)/shard_map/all_to_all | solution.py:29
  42.9 3.5 %all-to-all-start.2 = ((f32[32,16,2]{0,2,1:T(2,128)}), f32[32,16,2]{0,2,1:T(2,128)S(1)}, u32[]{:S(2)}, u32[]{:S(2)}) async-start(f32[32,16,2]{0,2,1:T(2,128)} %all_to_all.44), calls=%async_computation.2 | async-start | bytes 32768 | tf_op jit(solution)/shard_map/all_to_all | solution.py:116
  46.9 5.4 %all-to-all-done.2 = f32[32,16,2]{0,2,1:T(2,128)S(1)} async-done(((f32[32,16,2]{0,2,1:T(2,128)}), f32[32,16,2]{0,2,1:T(2,128)S(1)}, u32[]{:S(2)}, u32[]{:S(2)}) %all-to-all-start.2) | async-done | bytes 4128 | tf_op jit(solution)/shard_map/all_to_all | solution.py:116
  52.8 4.5 %convolution_bitcast_fusion = f32[16,32,512]{2,1,0:T(8,128)} fusion(bf16[32,256,1]{1,0,2:T(8,128)(2,1)S(1)} %reshape.208, bf16[16,512,256]{2,1,0:T(8,128)(2,1)} %bitcast.102), kind=kOutput, calls=%fused_computation.9 | convolution fusion | flops 134217728 | bytes 5259264 | tf_op jit(solution)/shard_map/dot_general | solution.py:129
  57.3 4.4 %all-to-all-start.3 = ((f32[16,32,512]{2,1,0:T(8,128)}), f32[16,32,512]{2,1,0:T(8,128)}, u32[]{:S(2)}, u32[]{:S(2)}) async-start(f32[16,32,512]{2,1,0:T(8,128)} %convolution_bitcast_fusion), calls=%async_computation.3 | async-start | bytes 2097152 | tf_op jit(solution)/shard_map/all_to_all | solution.py:47
  64.3 1.4 copy-done
  66.1 3.9 %reduce.4 = bf16[16,65552]{1,0:T(8,128)(2,1)S(1)} reduce(bf16[16,1,65552]{2,0,1:T(8,128)(2,1)} %bitcast.107, bf16[]{:T(256)} %broadcast.80), dimensions={1}, to_apply=%copy.154.reduce_sub_computation | reduce | bytes 4195330 | tf_op jit(solution)/shard_map/all_to_all | solution.py:29
  70.0 2.5 %reshape.212 = bf16[16,2,32776]{2,1,0:T(2,128)(2,1)} reshape(bf16[16,65552]{1,0:T(8,128)(2,1)S(1)} %reduce.4) | data formatting | bytes 4195328
  72.5 5.7 %all-to-all-done.3 = f32[16,32,512]{2,1,0:T(8,128)} async-done(((f32[16,32,512]{2,1,0:T(8,128)}), f32[16,32,512]{2,1,0:T(8,128)}, u32[]{:S(2)}, u32[]{:S(2)}) %all-to-all-start.3) | async-done | bytes 1048608 | tf_op jit(solution)/shard_map/all_to_all | solution.py:47
  78.2 10.7 %all-to-all-start.4 = ((bf16[16,2,32776]{2,1,0:T(2,128)(2,1)}), bf16[16,2,32776]{2,1,0:T(2,128)(2,1)S(1)}, u32[]{:S(2)}, u32[]{:S(2)}) async-start(bf16[16,2,32776]{2,1,0:T(2,128)(2,1)} %reshape.212), calls=%async_computation.4 | async-start | bytes 4210688 | tf_op jit(solution)/shard_map/all_to_all | solution.py:29
  89.8 1.3 reduce_sum.49
  91.1 1.4 add_convert_fusion
  92.5 46.7 %all-to-all-done.4 = bf16[16,2,32776]{2,1,0:T(2,128)(2,1)S(1)} async-done(((bf16[16,2,32776]{2,1,0:T(2,128)(2,1)}), bf16[16,2,32776]{2,1,0:T(2,128)(2,1)S(1)}, u32[]{:S(2)}, u32[]{:S(2)}) %all-to-all-start.4) | async-done | bytes 2097696 | tf_op jit(solution)/shard_map/all_to_all | solution.py:29
  139.2 9.9 %reshape.213 = bf16[16,1,65552]{2,1,0:T(2,128)(2,1)} reshape(bf16[16,2,32776]{2,1,0:T(2,128)(2,1)S(1)} %all-to-all-done.4) | data formatting | bytes 4195328
  149.1 2.4 %copy.190 = bf16[16,1,65552]{2,0,1:T(8,128)(2,1)S(1)} copy(bf16[16,1,65552]{2,1,0:T(2,128)(2,1)} %reshape.213) | data formatting | bytes 4195328
  153.6 1.1 copy.156
  154.7 1.1 copy.155
  (71 shorter events, 11.0 us)
Async XLA Ops:
  0.6 3.5 %copy-start.6 = (f32[128]{0:T(128)S(1)}, f32[128]{0:T(128)}, u32[]{:S(2)}) copy-start(f32[128]{0:T(128)} %param.14) | copy-start | bytes 1540
  0.6 9.9 %copy-start.5 = (bf16[8,1,8]{2,0,1:T(8,128)(2,1)S(1)}, bf16[8,1,8]{2,0,1:T(8,128)(2,1)}, u32[]{:S(2)}) copy-start(bf16[8,1,8]{2,0,1:T(8,128)(2,1)} %param.19) | copy-start | bytes 388
  0.7 9.9 %copy-start.4 = (bf16[8,1,8]{2,0,1:T(8,128)(2,1)S(1)}, bf16[8,1,8]{2,0,1:T(8,128)(2,1)}, u32[]{:S(2)}) copy-start(bf16[8,1,8]{2,0,1:T(8,128)(2,1)} %param.20) | copy-start | bytes 388
  0.7 9.9 %copy-start.1 = (bf16[8,32,1024]{2,1,0:T(8,128)(2,1)S(1)}, bf16[8,32,1024]{2,1,0:T(8,128)(2,1)}, u32[]{:S(2)}) copy-start(bf16[8,32,1024]{2,1,0:T(8,128)(2,1)} %param.18) | copy-start | bytes 1572868
  3.9 6.8 %copy-start.2 = (bf16[8,32,1024]{2,1,0:T(8,128)(2,1)S(1)}, bf16[8,32,1024]{2,1,0:T(8,128)(2,1)}, u32[]{:S(2)}) copy-start(bf16[8,32,1024]{2,1,0:T(8,128)(2,1)} %param.17) | copy-start | bytes 1572868
  3.9 6.9 %copy-start.7 = (s32[8]{0:T(128)S(1)}, s32[8]{0:T(128)}, u32[]{:S(2)}) copy-start(s32[8]{0:T(128)} %param.21) | copy-start | bytes 100
  5.0 13.5 %all-to-all-start = ((bf16[16,32,2,128]{3,1,2,0:T(8,128)(2,1)}), bf16[16,32,2,128]{3,1,2,0:T(8,128)(2,1)S(1)}, u32[]{:S(2)}, u32[]{:S(2)}) async-start(bf16[16,32,2,128]{3,1,2,0:T(8,128)(2,1)} %broadcast_in_dim.65), calls=%async_computation | async-start | bytes 524288 | tf_op jit(solution)/shard_map/all_to_all | solution.py:18
  22.7 20.2 %all-to-all-start.1 = ((f32[32,32,129]{2,0,1:T(8,128)}), f32[32,32,129]{2,0,1:T(8,128)S(1)}, u32[]{:S(2)}, u32[]{:S(2)}) async-start(f32[32,32,129]{2,0,1:T(8,128)} %copy.145), calls=%async_computation.1 | async-start | bytes 2097152 | tf_op jit(solution)/shard_map/all_to_all | solution.py:29
  26.4 6.4 %copy-start.3 = (s32[16,6]{0,1:T(8,128)S(1)}, s32[16,6]{0,1:T(8,128)}, u32[]{:S(2)}) copy-start(s32[16,6]{0,1:T(8,128)} %param.22) | copy-start | bytes 1156
  26.4 6.7 %copy-start.8 = (s32[1,6]{1,0:T(1,128)S(1)}, s32[1,6]{1,0:T(1,128)}, u32[]{:S(2)}) copy-start(s32[1,6]{1,0:T(1,128)} %param.23) | copy-start | bytes 76
  42.9 9.5 %all-to-all-start.2 = ((f32[32,16,2]{0,2,1:T(2,128)}), f32[32,16,2]{0,2,1:T(2,128)S(1)}, u32[]{:S(2)}, u32[]{:S(2)}) async-start(f32[32,16,2]{0,2,1:T(2,128)} %all_to_all.44), calls=%async_computation.2 | async-start | bytes 32768 | tf_op jit(solution)/shard_map/all_to_all | solution.py:116
  57.3 20.9 %all-to-all-start.3 = ((f32[16,32,512]{2,1,0:T(8,128)}), f32[16,32,512]{2,1,0:T(8,128)}, u32[]{:S(2)}, u32[]{:S(2)}) async-start(f32[16,32,512]{2,1,0:T(8,128)} %convolution_bitcast_fusion), calls=%async_computation.3 | async-start | bytes 2097152 | tf_op jit(solution)/shard_map/all_to_all | solution.py:47
  64.3 1.4 copy-start
  78.2 61.0 %all-to-all-start.4 = ((bf16[16,2,32776]{2,1,0:T(2,128)(2,1)}), bf16[16,2,32776]{2,1,0:T(2,128)(2,1)S(1)}, u32[]{:S(2)}, u32[]{:S(2)}) async-start(bf16[16,2,32776]{2,1,0:T(2,128)(2,1)} %reshape.212), calls=%async_computation.4 | async-start | bytes 4210688 | tf_op jit(solution)/shard_map/all_to_all | solution.py:29
where the time goes:
time: 157 us; the launch traced here: 156 us
  waiting for transfers between devices  73.9 us (47%)
  local copies, waits for them, and re-layouts  31.4 us (20%)
  starting transfers between devices  27.7 us (18%)
  matrix products  12.2 us (8%)
  other arithmetic  8.71 us (6%)
  between operations  1.72 us (1%)
    all_to_all x2, waiting for transfers between devices, sent_together(): lax.all_to_all(both, axis, split_axis=split_dim, concat_axis=concat_dim,...  55.2 us
    unnamed x28, local copies, waits for them, and re-layouts  19.3 us
    all_to_all x2, starting transfers between devices, sent_together(): lax.all_to_all(both, axis, split_axis=split_dim, concat_axis=concat_dim,...  14.4 us
    all_to_all x1, waiting for transfers between devices, from_everyone(): return lax.all_to_all(copies, axis, split_axis=0, concat_axis=0, tiled=True)  7.57 us
    dot_general x1, local copies, waits for them, and re-layouts, attend(): terms = jnp.dot(attended, o_weight, preferred_element_type=jnp.float32)  6.4 us
    all_to_all x1, waiting for transfers between devices, sent_and_summed(): tiles = lax.all_to_all(cut_along(array, dim, count), axis, 0, 0, tiled=True)  5.73 us
    all_to_all x1, starting transfers between devices, from_everyone(): return lax.all_to_all(copies, axis, split_axis=0, concat_axis=0, tiled=True)  5.5 us
    all_to_all x1, waiting for transfers between devices, attend(): lax.all_to_all(partial_value[0], 'tensor', split_axis=1, concat_axis=0, t...  5.44 us
  transfers between devices with their start and end apart: 5, of which 5 were waited for; matrix products, arithmetic and copies ran while one was open for 13% of the time, Pallas kernels for 0%

commit v1 on v0

v1 whole, which is shorter than its diff:
```python
import functools

import jax
import jax.numpy as jnp
from jax import lax
from jax.experimental import pallas as pl
from jax.experimental.pallas import tpu as pltpu
from jax.sharding import PartitionSpec as P

NEGATIVE = -1e30
EPSILON = 1e-06
BF16, F32, I32 = jnp.bfloat16, jnp.float32, jnp.int32

REPLICAS = 16
MOVE = 6
HELD = 8
SPAN = 32
SPEC = 4
ROWS = HELD * SPEC
KVH = 8
HD = 128
TENSORS = 16
SLOT = 2 * KVH * SPAN + 8
COLS = 512


VMEM = pl.BlockSpec(memory_space=pltpu.VMEM)
SMEM = pl.BlockSpec(memory_space=pltpu.SMEM)
ANY = pl.BlockSpec(memory_space=pl.ANY)


def cost(flops, moved):
    return pl.CostEstimate(flops=flops, bytes_accessed=moved, transcendentals=0)


def room(mib):
    return pltpu.CompilerParams(vmem_limit_bytes=mib << 20)


def shape(dims, dtype):
    return jax.ShapeDtypeStruct(dims, dtype)


def iota(dims, axis):
    return lax.broadcasted_iota(I32, dims, axis)


def scale_rows(scr, key_scales, value_scales):
    scr[...] = jnp.zeros_like(scr)
    scr[0:HELD, 0:KVH] = key_scales[...].astype(F32)
    scr[HELD : 2 * HELD, 0:KVH] = value_scales[...].astype(F32)


def pack_kernel(
    at, dest, slots, keys, values, key_scales, value_scales, out, held, stage, scr, in_sem, out_sem
):
    here = at[0]
    loads = []
    for j in range(MOVE):
        s = slots[0, j]
        pair = (
            pltpu.make_async_copy(keys.at[s], held.at[j, 0], in_sem.at[j, 0]),
            pltpu.make_async_copy(values.at[s], held.at[j, 1], in_sem.at[j, 1]),
        )
        for copy in pair:
            copy.start()
        loads.append(pair)
    scale_rows(scr, key_scales, value_scales)
    row = iota((8, HD), 0)
    stores = []
    for j in range(MOVE):
        s = slots[0, j]
        both = jnp.where(
            row == 0,
            scr[pl.ds(s, 1), :],
            jnp.where(row == 1, scr[pl.ds(HELD + s, 1), :], 0.0),
        )
        stage[j, 2 * KVH * SPAN : SLOT, :] = both.astype(BF16)
        for which in range(2):
            loads[j][which].wait()
            for c in range(KVH):
                at_row = (which * KVH + c) * SPAN
                stage[j, at_row : at_row + SPAN, :] = held[j, which, :, c * HD : (c + 1) * HD]
        copy = pltpu.make_async_copy(stage.at[j], out.at[dest[j, here]], out_sem.at[j])
        copy.start()
        stores.append(copy)
    for copy in stores:
        copy.wait()


def pack(at, dest, slots, keys, values, key_scales, value_scales):
    return pl.pallas_call(
        pack_kernel,
        out_shape=shape((REPLICAS, SLOT, HD), BF16),
        in_specs=[SMEM, SMEM, SMEM, ANY, ANY, VMEM, VMEM],
        out_specs=ANY,
        scratch_shapes=[
            pltpu.VMEM((MOVE, 2, SPAN, KVH * HD), BF16),
            pltpu.VMEM((MOVE, SLOT, HD), BF16),
            pltpu.VMEM((2 * HELD, HD), F32),
            pltpu.SemaphoreType.DMA((MOVE, 2)),
            pltpu.SemaphoreType.DMA((MOVE,)),
        ],
        cost_estimate=cost(1 << 20, 4 << 20),
        name="pack",
    )(at, dest, slots, keys, values, key_scales, value_scales)


def unpack_kernel(
    at,
    dest,
    slots,
    received,
    keys,
    values,
    key_scales,
    value_scales,
    new_keys,
    new_values,
    new_key_scales,
    new_value_scales,
    landed,
    stage,
    kept,
    scr,
    in_sem,
    out_sem,
    kept_sem,
):
    here = at[0]
    loads = []
    for j in range(MOVE):
        source = jnp.int32(0)
        for p in range(REPLICAS):
            source = jnp.where(dest[j, p] == here, p, source)
        copy = pltpu.make_async_copy(received.at[source], landed.at[j], in_sem.at[j])
        copy.start()
        loads.append(copy)
    stays = []
    for r in range(HELD):
        moving = slots[0, 0] == r
        for j in range(1, MOVE):
            moving = jnp.logical_or(moving, slots[0, j] == r)
        stays.append(jnp.logical_not(moving))

    def kept_in(r):
        return (
            pltpu.make_async_copy(keys.at[r], kept.at[r, 0], kept_sem.at[r, 0]),
            pltpu.make_async_copy(values.at[r], kept.at[r, 1], kept_sem.at[r, 1]),
        )

    def kept_out(r):
        return (
            pltpu.make_async_copy(kept.at[r, 0], new_keys.at[r], kept_sem.at[r, 0]),
            pltpu.make_async_copy(kept.at[r, 1], new_values.at[r], kept_sem.at[r, 1]),
        )

    for r in range(HELD):

        @pl.when(stays[r])
        def _():
            for copy in kept_in(r):
                copy.start()

    scale_rows(scr, key_scales, value_scales)
    for r in range(HELD):

        @pl.when(stays[r])
        def _():
            for copy in kept_in(r):
                copy.wait()
            for copy in kept_out(r):
                copy.start()

    stores = []
    for j in range(MOVE):
        s = slots[0, j]
        loads[j].wait()
        both = landed[j, 2 * KVH * SPAN : SLOT, :].astype(F32)
        scr[pl.ds(s, 1), :] = both[0:1, :]
        scr[pl.ds(HELD + s, 1), :] = both[1:2, :]
        for which, target in ((0, new_keys), (1, new_values)):
            for c in range(KVH):
                at_row = (which * KVH + c) * SPAN
                stage[j, which, :, c * HD : (c + 1) * HD] = landed[j, at_row : at_row + SPAN, :]
            copy = pltpu.make_async_copy(stage.at[j, which], target.at[s], out_sem.at[j, which])
            copy.start()
            stores.append(copy)
    new_key_scales[...] = scr[0:HELD, 0:KVH].astype(BF16)
    new_value_scales[...] = scr[HELD : 2 * HELD, 0:KVH].astype(BF16)
    for r in range(HELD):

        @pl.when(stays[r])
        def _():
            for copy in kept_out(r):
                copy.wait()

    for copy in stores:
        copy.wait()


def unpack(at, dest, slots, received, keys, values, key_scales, value_scales):
    return pl.pallas_call(
        unpack_kernel,
        out_shape=(
            shape(keys.shape, BF16),
            shape(values.shape, BF16),
            shape((HELD, KVH), BF16),
            shape((HELD, KVH), BF16),
        ),
        in_specs=[SMEM, SMEM, SMEM, ANY, ANY, ANY, VMEM, VMEM],
        out_specs=(ANY, ANY, VMEM, VMEM),
        scratch_shapes=[
            pltpu.VMEM((MOVE, SLOT, HD), BF16),
            pltpu.VMEM((MOVE, 2, SPAN, KVH * HD), BF16),
            pltpu.VMEM((HELD, 2, SPAN, KVH * HD), BF16),
            pltpu.VMEM((2 * HELD, HD), F32),
            pltpu.SemaphoreType.DMA((MOVE,)),
            pltpu.SemaphoreType.DMA((MOVE, 2)),
            pltpu.SemaphoreType.DMA((HELD, 2)),
        ],
        cost_estimate=cost(1 << 20, 4 << 20),
        compiler_params=room(8),
        name="unpack",
    )(at, dest, slots, received, keys, values, key_scales, value_scales)


def query_kernel(hidden, weight, gain, query, total):
    step = pl.program_id(0)

    @pl.when(step == 0)
    def _():
        total[...] = jnp.zeros_like(total)

    total[...] += jnp.dot(hidden[...], weight[...], preferred_element_type=F32)

    @pl.when(step == pl.num_programs(0) - 1)
    def _():
        for h in range(2):
            part = total[:, h * HD : (h + 1) * HD]
            mean = jnp.mean(part * part, axis=-1, keepdims=True)
            part = part * lax.rsqrt(mean + EPSILON)
            query[:, h * HD : (h + 1) * HD] = (part * gain[...] * HD ** (-0.5)).astype(BF16)


def project_query(hidden, q_weight, q_gain):
    depth = hidden.shape[1]
    steps = 8
    block = depth // steps
    return pl.pallas_call(
        query_kernel,
        grid=(steps,),
        out_shape=shape((ROWS, 2 * HD), BF16),
        in_specs=[
            pl.BlockSpec((ROWS, block), lambda i: (0, i)),
            pl.BlockSpec((block, 2 * HD), lambda i: (i, 0)),
            pl.BlockSpec((1, HD), lambda i: (0, 0)),
        ],
        out_specs=pl.BlockSpec((ROWS, 2 * HD), lambda i: (0, 0)),
        scratch_shapes=[pltpu.VMEM((ROWS, 2 * HD), F32)],
        cost_estimate=cost(4 << 20, 4 << 20),
        compiler_params=room(8),
        name="query",
    )(hidden, q_weight, q_gain.reshape(1, HD))


def split3(x):
    high = x.astype(BF16).astype(F32)
    rest = x - high
    middle = rest.astype(BF16).astype(F32)
    return high, middle, rest - middle


def put_stats(out, at_row, stats):
    high, middle, low = split3(stats)
    out[at_row : at_row + 16, :] = jnp.concatenate([high, middle], axis=0).astype(BF16)
    out[at_row + 16 : at_row + 32, :] = jnp.concatenate(
        [low, jnp.zeros_like(low)], axis=0
    ).astype(BF16)


def get_stats(message, at_row):
    first = message[at_row : at_row + 16, :].astype(F32)
    second = message[at_row + 16 : at_row + 32, :].astype(F32)
    return (first[0:8] + first[8:16]) + second[0:8]


def columns_of(rows):
    short = HD - rows.shape[0]
    return jnp.concatenate([rows, jnp.zeros((short, HD), F32)], axis=0).T


def attend_kernel(
    at, lengths, q0, q1, q2, q3, keys, values, key_scales, value_scales,
    o0, o1, o2, o3, q_all, o_all, mask, stats,
):
    rank = at[1]
    y = rank // 4
    x = (rank // 2) % 2
    for k, q in enumerate((q0, q1, q2, q3)):
        q_all[k] = q[...]
    tokens = HELD * SPAN
    row_request = (iota((HD, tokens), 0) // SPEC) % HELD
    col = iota((HD, tokens), 1)
    limit = jnp.zeros((1, tokens), I32)
    col1 = iota((1, tokens), 1)
    for r in range(HELD):
        limit = jnp.where(col1 // SPAN == r, lengths[r], limit)
    in_reach = rank * SPAN + col1 % SPAN < limit
    ok = jnp.logical_and(row_request == col // SPAN, in_reach)
    mask[...] = jnp.where(ok, 1.0, 0.0)
    spread_cols = (iota((HELD, tokens), 1) // SPAN == iota((HELD, tokens), 0)).astype(BF16)
    spread_rows = ((iota((HD, HELD), 0) // SPEC) % HELD == iota((HD, HELD), 1)).astype(BF16)
    col_scale = lax.dot_general(
        key_scales[...], spread_cols, (((0,), (0,)), ((), ())), preferred_element_type=F32
    )
    row_scale = jnp.dot(spread_rows, value_scales[...], preferred_element_type=F32)
    lane = iota((HD, HD), 1)
    stats[...] = jnp.zeros_like(stats)
    for m in range(KVH):
        k = (y - m // 2 + 4) % 4
        dx = (m % 2 + x) % 2
        near = q_all[k, 2 * dx]
        far = q_all[k, 2 * dx + 1]
        grouped = jnp.concatenate(
            [near[:, :HD], near[:, HD:], far[:, :HD], far[:, HD:]], axis=0
        )
        key = keys[:, :, m * HD : (m + 1) * HD].reshape(tokens, HD)
        value = values[:, :, m * HD : (m + 1) * HD].reshape(tokens, HD)
        scores = lax.dot_general(
            grouped, key, (((1,), (1,)), ((), ())), preferred_element_type=F32
        )
        scores = scores * col_scale[m : m + 1, :]
        good = mask[...] > 0.5
        peak = jnp.max(jnp.where(good, scores, NEGATIVE), axis=1, keepdims=True)
        weight = jnp.where(good, jnp.exp(scores - peak), 0.0)
        total = jnp.sum(weight, axis=1, keepdims=True)
        out = jnp.dot(weight.astype(BF16), value, preferred_element_type=F32)
        o_all[k, dx] = (out * row_scale[:, m : m + 1]).astype(BF16)
        first = 8 * k + 2 * dx
        stats[...] = jnp.where(
            lane == first, peak, jnp.where(lane == first + 1, total, stats[...])
        )
    turned = stats[...].T
    for k, o in enumerate((o0, o1, o2, o3)):
        o[0:HD, :] = o_all[k, 0]
        o[HD : 2 * HD, :] = o_all[k, 1]
        put_stats(o, 2 * HD, turned[8 * k : 8 * k + 8])


def attend(at, lengths, queries, keys, values, key_scales, value_scales):
    out = shape((2 * HD + 32, HD), BF16)
    return pl.pallas_call(
        attend_kernel,
        out_shape=(out,) * 4,
        in_specs=[SMEM, SMEM] + [VMEM] * 8,
        out_specs=(VMEM,) * 4,
        scratch_shapes=[
            pltpu.VMEM((4, 4, ROWS, 2 * HD), BF16),
            pltpu.VMEM((4, 2, HD, HD), BF16),
            pltpu.VMEM((HD, HELD * SPAN), F32),
            pltpu.VMEM((HD, HD), F32),
        ],
        cost_estimate=cost(4 << 20, 2 << 20),
        compiler_params=room(8),
        name="attend",
    )(at, lengths, *queries, keys, values, key_scales, value_scales)


def merged(stats):
    top = functools.reduce(jnp.maximum, stats)
    factors = [jnp.exp(s - top) for s in stats]
    total = sum(s * pltpu.roll(f, 1, 0) for s, f in zip(stats, factors))
    peak_row = iota(top.shape, 0) % 2 == 0
    return factors, jnp.where(peak_row, top, total)


def combine_kernel(p0, p1, p2, p3, o0, o1, o2, o3):
    parts = (p0, p1, p2, p3)
    factors, both = merged([get_stats(p, 2 * HD) for p in parts])
    column = columns_of(jnp.concatenate(factors, axis=0))
    outs = ((o0, o1), (o2, o3))
    for dx in range(2):
        summed = jnp.zeros((HD, HD), F32)
        for k, p in enumerate(parts):
            part = p[dx * HD : (dx + 1) * HD, :].astype(F32)
            summed = summed + part * column[:, 8 * k + 2 * dx : 8 * k + 2 * dx + 1]
        for dc in range(2):
            outs[dx][dc][0 : HD // 2, :] = summed[dc * 64 : dc * 64 + 64].astype(BF16)
            put_stats(outs[dx][dc], HD // 2, both)


def combine(parts):
    out = shape((HD // 2 + 32, HD), BF16)
    return pl.pallas_call(
        combine_kernel,
        out_shape=(out,) * 4,
        in_specs=[VMEM] * 4,
        out_specs=(VMEM,) * 4,
        cost_estimate=cost(1 << 20, 1 << 19),
        compiler_params=room(4),
        name="combine",
    )(*parts)


def finish_kernel(p0, p1, p2, p3, attended):
    parts = (p0, p1, p2, p3)
    stats = []
    for d, p in enumerate(parts):
        s = get_stats(p, HD // 2)
        if d // 2:
            s = pltpu.roll(s, 6, 0)
        if d % 2:
            s = pltpu.roll(s, HD // 2, 1)
        stats.append(s)
    factors, both = merged(stats)
    over = pltpu.roll(both, 7, 0)
    column = columns_of(jnp.concatenate([f / over for f in factors], axis=0))
    summed = jnp.zeros((HD // 2, HD), F32)
    for d, p in enumerate(parts):
        summed = summed + p[0 : HD // 2, :].astype(F32) * column[0 : HD // 2, 8 * d : 8 * d + 1]
    for h in range(2):
        attended[:, h * HD : (h + 1) * HD] = summed[h * ROWS : (h + 1) * ROWS].astype(BF16)


def finish(parts):
    return pl.pallas_call(
        finish_kernel,
        out_shape=shape((ROWS, 2 * HD), BF16),
        in_specs=[VMEM] * 4,
        out_specs=VMEM,
        cost_estimate=cost(1 << 20, 1 << 19),
        compiler_params=room(4),
        name="finish",
    )(*parts)


def output_kernel(other, at, attended, weight, out, blocks, sem):
    core = (at[1] + other) % 2
    copies = []
    for i in range(TENSORS // 2):
        start = pl.multiple_of((2 * i + core) * COLS, COLS)
        copy = pltpu.make_async_copy(weight.at[:, pl.ds(start, COLS)], blocks.at[i], sem.at[i])
        copy.start()
        copies.append(copy)
    for i in range(TENSORS // 2):
        copies[i].wait()
        out[i] = jnp.dot(attended[...], blocks[i], preferred_element_type=F32).astype(out.dtype)


def project_output(other, dtype, at, attended, o_weight):
    half = TENSORS // 2
    return pl.pallas_call(
        functools.partial(output_kernel, other),
        out_shape=shape((half, ROWS, COLS), dtype),
        in_specs=[SMEM, VMEM, ANY],
        out_specs=VMEM,
        scratch_shapes=[
            pltpu.VMEM((half, 2 * HD, COLS), BF16),
            pltpu.SemaphoreType.DMA((half,)),
        ],
        cost_estimate=cost(1 << 22, 2 << 20),
        compiler_params=room(8),
        name="output_other" if other else "output_own",
    )(at, attended, o_weight)


def share_kernel(at, own, received, keep, s1, s2, s3):
    y = at[1] // 4
    for k in range(4):
        group = (y - k + 4) % 4
        for c in range(2):
            value = own[2 * group + c] + received[2 * group + c].astype(F32)
            if k == 0:
                keep[c] = value
            else:
                (s1, s2, s3)[k - 1][c] = value.astype(BF16)


def share(at, own, received):
    out = shape((2, ROWS, COLS), BF16)
    return pl.pallas_call(
        share_kernel,
        out_shape=(shape((2, ROWS, COLS), F32), out, out, out),
        in_specs=[SMEM, VMEM, VMEM],
        out_specs=(VMEM,) * 4,
        cost_estimate=cost(1 << 20, 1 << 20),
        compiler_params=room(6),
        name="share",
    )(at, own, received)


def narrow_kernel(at, own, r1, r2, r3, keep, send):
    x = (at[1] // 2) % 2
    for c, out in ((x, keep), (1 - x, send)):
        value = own[c] + r1[c].astype(F32) + r2[c].astype(F32) + r3[c].astype(F32)
        out[...] = value.astype(out.dtype)


def narrow(at, own, received):
    return pl.pallas_call(
        narrow_kernel,
        out_shape=(shape((ROWS, COLS), F32), shape((ROWS, COLS), BF16)),
        in_specs=[SMEM] + [VMEM] * 4,
        out_specs=(VMEM,) * 2,
        cost_estimate=cost(1 << 20, 1 << 19),
        compiler_params=room(4),
        name="narrow",
    )(at, own, *received)


def mix_kernel(at, gate, own, received, hidden, out, rows, sem):
    start = pl.multiple_of(at[1] * COLS, COLS)
    copy = pltpu.make_async_copy(hidden.at[:, pl.ds(start, COLS)], rows, sem)
    copy.start()
    scale = jnp.tanh(jnp.full((8, HD), gate[0], F32))[0:1, 0:1]
    summed = own[...] + received[...].astype(F32)
    copy.wait()
    out[...] = (rows[...].astype(F32) + scale * summed).astype(BF16)


def mix(at, gate, own, received, hidden):
    return pl.pallas_call(
        mix_kernel,
        out_shape=shape((ROWS, COLS), BF16),
        in_specs=[SMEM, SMEM, VMEM, VMEM, ANY],
        out_specs=VMEM,
        scratch_shapes=[pltpu.VMEM((ROWS, COLS), BF16), pltpu.SemaphoreType.DMA],
        cost_estimate=cost(1 << 20, 1 << 18),
        compiler_params=room(4),
        name="mix",
    )(at, gate, own, received, hidden)


def swap(array, bits):
    return lax.ppermute(array, "tensor", [(i, i ^ bits) for i in range(TENSORS)])


def shift(array, rows):
    return lax.ppermute(array, "tensor", [(i, (i + 4 * rows) % TENSORS) for i in range(TENSORS)])


def attention(
    at, hidden, q_weight, q_gain, o_weight, attn_gate, keys, values, key_scales, value_scales, lengths
):
    query = project_query(hidden, q_weight, q_gain)
    local = jnp.stack([query] + [swap(query, d) for d in (1, 2, 3)])
    queries = [local] + [shift(local, k) for k in (1, 2, 3)]
    parts = attend(at, lengths, queries, keys, values, key_scales, value_scales)
    parts = combine([parts[0]] + [shift(parts[k], -k) for k in (1, 2, 3)])
    attended = finish([parts[0]] + [swap(parts[d], d) for d in (1, 2, 3)])
    other = swap(project_output(1, BF16, at, attended, o_weight), 1)
    own = project_output(0, F32, at, attended, o_weight)
    own, *sent = share(at, own, other)
    own, sent = narrow(at, own, [shift(s, -k) for k, s in zip((1, 2, 3), sent)])
    return mix(at, attn_gate, own, swap(sent, 2), hidden)


def local(
    hidden,
    q_weight,
    q_gain,
    o_weight,
    attn_gate,
    key_codes,
    value_codes,
    key_scales,
    value_scales,
    lengths,
    dest_replica,
    move_slot,
):
    at = jnp.stack([lax.axis_index("replica"), lax.axis_index("tensor")]).astype(I32)
    dest = dest_replica.T
    key_scales, value_scales = key_scales[:, 0, :], value_scales[:, 0, :]
    message = pack(at, dest, move_slot, key_codes, value_codes, key_scales, value_scales)
    received = lax.all_to_all(
        message, "replica", split_axis=0, concat_axis=0, tiled=True
    )
    mixed = attention(
        at, hidden, q_weight, q_gain, o_weight, attn_gate,
        key_codes, value_codes, key_scales, value_scales, lengths,
    )
    new_keys, new_values, new_ks, new_vs = unpack(
        at, dest, move_slot, received, key_codes, value_codes, key_scales, value_scales
    )
    return (mixed, new_keys, new_values, new_ks[:, None, :], new_vs[:, None, :])


def solution(mesh):
    return jax.shard_map(
        local,
        mesh=mesh,
        in_specs=(
            P("replica", None),
            P(None, "tensor"),
            P(),
            P("tensor", None),
            P(),
            P("replica", "tensor", None),
            P("replica", "tensor", None),
            P("replica", "tensor", None),
            P("replica", "tensor", None),
            P("replica"),
            P(),
            P("replica", None),
        ),
        out_specs=(
            P("replica", "tensor"),
            P("replica", "tensor", None),
            P("replica", "tensor", None),
            P("replica", "tensor", None),
            P("replica", "tensor", None),
        ),
        check_vma=False,
    )
```

time: 157 us -> 80.6 us (0.51)
  the two profiles are of different devices: /device:TPU:32 before, /device:TPU:100 now
where the time goes in v1:
time: 80.6 us; the launch traced here: 80.4 us
  waiting for transfers between devices  30.4 us (38%)
  starting transfers between devices  27 us (33%)
  Pallas kernels  17.2 us (21%)
  local copies, waits for them, and re-layouts  3.6 us (4%)
  between operations  1.56 us (2%)
    ppermute x9, waiting for transfers between devices, shift(): lax.ppermute(array, 'tensor', [(i, (i + 4 * rows) % TENSORS) for i in ran...  15.8 us
    ppermute x8, waiting for transfers between devices, swap(): lax.ppermute(array, 'tensor', [(i, i ^ bits) for i in range(TENSORS)])  14.6 us
    ppermute x9, starting transfers between devices, shift(): lax.ppermute(array, 'tensor', [(i, (i + 4 * rows) % TENSORS) for i in ran...  11.7 us
    all_to_all x1, starting transfers between devices, local(): lax.all_to_all(message, 'replica', split_axis=0, concat_axis=0, tiled=True)  10.2 us
    ppermute x8, starting transfers between devices, swap(): lax.ppermute(array, 'tensor', [(i, i ^ bits) for i in range(TENSORS)])  5.08 us
    pallas_call x2, Pallas kernels, project_output(): pl.pallas_call(functools.partial(output_kernel, other), out_shape=shape((...  4.07 us
    pallas_call x1, Pallas kernels, unpack(): pl.pallas_call(unpack_kernel, out_shape=(shape(keys.shape, BF16), shape(v...  3.96 us
    unnamed x26, local copies, waits for them, and re-layouts  3.6 us
  transfers between devices with their start and end apart: 18, of which 14 were waited for; matrix products, arithmetic and copies ran while one was open for 0% of the time, Pallas kernels for 13%

profile of v1, /device:TPU:100, one launch (start us, length us, event | category | flops | bytes accessed | tf_op | source)
XLA Modules:
  0.0 80.4 jit_solution(7293381333156352056)
XLA Ops:
  1.2 2.7 %pack.1 = bf16[16,520,128]{2,1,0:T(8,128)(2,1)} custom-call(s32[2]{0:T(128)} %pad_add_fusion.at, s32[6,16]{1,0:T(8,128)} %bitcast.19, s32[1,6]{1,0:T(1,128)} %slots.3, bf16[8,32,1024]{2,1,0:T(8,128)(2,1)} %keys.5, bf16[8,32,1024]{2,1,0:T(8,128)(2,1)} %values.5, bf16[8,8]{1,0:T(8,128)(2,1)} %bitcast.13, bf16[8,8]{1,0:T(8,128)(2,1)} %bitcast.16), custom_call_target="tpu_custom_call" | custom-call | flops 1048576 | bytes 4194304 | tf_op jit(solution)/shard_map/pack/pallas_call | solution.py:92
  4.0 10.2 %all-to-all-start = ((bf16[16,520,128]{2,1,0:T(8,128)(2,1)}), bf16[16,520,128]{2,1,0:T(8,128)(2,1)S(1)}, u32[]{:S(2)}, u32[]{:S(2)}) async-start(bf16[16,520,128]{2,1,0:T(8,128)(2,1)} %pack.1), calls=%async_computation | async-start | bytes 4259840 | tf_op jit(solution)/shard_map/all_to_all | solution.py:577
  14.3 2.3 %copy-done.3 = bf16[8192,256]{1,0:T(8,128)(2,1)S(1)} copy-done((bf16[8192,256]{1,0:T(8,128)(2,1)S(1)}, bf16[8192,256]{1,0:T(8,128)(2,1)}, u32[]{:S(2)}) %copy-start.3) | copy-done | bytes 4194328
  16.6 1.2 %copy-done.4 = bf16[32,8192]{1,0:T(8,128)(2,1)S(1)} copy-done((bf16[32,8192]{1,0:T(8,128)(2,1)S(1)}, bf16[32,8192]{1,0:T(8,128)(2,1)}, u32[]{:S(2)}) %copy-start.4) | copy-done | bytes 524312
  17.8 1.8 %query.1 = bf16[32,256]{1,0:T(8,128)(2,1)S(1)} custom-call(bf16[32,8192]{1,0:T(8,128)(2,1)S(1)} %copy-done.4, bf16[8192,256]{1,0:T(8,128)(2,1)S(1)} %copy-done.3, f32[1,128]{1,0:T(1,128)S(1)} %bitcast.21), custom_call_target="tpu_custom_call" | custom-call | flops 4194304 | bytes 4194304 | tf_op jit(solution)/shard_map/query/pallas_call | solution.py:250
  19.8 1.2 %collective-permute-start.1 = (bf16[32,256]{1,0:T(8,128)(2,1)S(1)}, bf16[32,256]{1,0:T(8,128)(2,1)S(1)}, u32[]{:S(2)}, u32[]{:S(2)}) collective-permute-start(bf16[32,256]{1,0:T(8,128)(2,1)S(1)} %query.1), channel_id=1, source_target_pairs={{0,2},{1,3},{2,0},{3,1},{4,6},{5,7},{6,4},{7,5},{8,10},{9,11},{10,... | collective-permute-start | bytes 49160 | tf_op jit(solution)/shard_map/ppermute | solution.py:536
  21.6 1.6 %collective-permute-done.2 = bf16[32,256]{1,0:T(8,128)(2,1)S(1)} collective-permute-done((bf16[32,256]{1,0:T(8,128)(2,1)S(1)}, bf16[32,256]{1,0:T(8,128)(2,1)S(1)}, u32[]{:S(2)}, u32[]{:S(2)}) %collective-permute-start.2) | collective-permute-done | bytes 16416 | tf_op jit(solution)/shard_map/ppermute | solution.py:536
  23.9 3.1 %collective-permute-start.5 = (bf16[4,32,256]{2,1,0:T(8,128)(2,1)S(1)}, bf16[4,32,256]{2,1,0:T(8,128)(2,1)S(1)}, u32[]{:S(2)}, u32[]{:S(2)}) collective-permute-start(bf16[4,32,256]{2,1,0:T(8,128)(2,1)S(1)} %pad_maximum_fusion.q0), channel_id=1, source_target_pairs={{0,12},{1,13},{2,14},{3,15},{4,0},{5,1},{6,2},{7,3},{8,4},{9,5},{1... | collective-permute-start | bytes 196616 | tf_op jit(solution)/shard_map/ppermute | solution.py:540
  28.6 1.6 %collective-permute-done.5.q3 = bf16[4,32,256]{2,1,0:T(8,128)(2,1)S(1)} collective-permute-done((bf16[4,32,256]{2,1,0:T(8,128)(2,1)S(1)}, bf16[4,32,256]{2,1,0:T(8,128)(2,1)S(1)}, u32[]{:S(2)}, u32[]{:S(2)}) %collective-permute-start.5) | collective-permute-done | bytes 65568 | tf_op jit(solution)/shard_map/ppermute | solution.py:540
  30.2 3.0 %collective-permute-done.4.q2 = bf16[4,32,256]{2,1,0:T(8,128)(2,1)S(1)} collective-permute-done((bf16[4,32,256]{2,1,0:T(8,128)(2,1)S(1)}, bf16[4,32,256]{2,1,0:T(8,128)(2,1)S(1)}, u32[]{:S(2)}, u32[]{:S(2)}) %collective-permute-start.4) | collective-permute-done | bytes 65568 | tf_op jit(solution)/shard_map/ppermute | solution.py:540
  33.9 1.6 %attend.1 = (bf16[288,128]{1,0:T(8,128)(2,1)S(1)}, bf16[288,128]{1,0:T(8,128)(2,1)S(1)}, bf16[288,128]{1,0:T(8,128)(2,1)S(1)}, bf16[288,128]{1,0:T(8,128)(2,1)S(1)}) custom-call(s32[2]{0:T(128)S(1)} %copy-done.6, s32[8]{0:T(128)S(1)} %copy-done.12, bf16[4,32,256]{2,1,0:T(8,128)(2,1)S(1)} %pad_maximum_fusion.q0, ...), custom_call_target="tpu_custom_call" | custom-call | flops 4194304 | bytes 2097152 | tf_op jit(solution)/shard_map/attend/pallas_call | solution.py:353
  36.8 1.2 %collective-permute-start.8 = (bf16[288,128]{1,0:T(8,128)(2,1)S(1)}, bf16[288,128]{1,0:T(8,128)(2,1)S(1)}, u32[]{:S(2)}, u32[]{:S(2)}) collective-permute-start(bf16[288,128]{1,0:T(8,128)(2,1)S(1)} %get-tuple-element.26), channel_id=1, source_target_pairs={{0,4},{1,5},{2,6},{3,7},{4,8},{5,9},{6,10},{7,11},{8,12},{9,13},{1... | collective-permute-start | bytes 221192 | tf_op jit(solution)/shard_map/ppermute | solution.py:540
  38.0 2.2 %collective-permute-done.6.p1 = bf16[288,128]{1,0:T(8,128)(2,1)S(1)} collective-permute-done((bf16[288,128]{1,0:T(8,128)(2,1)S(1)}, bf16[288,128]{1,0:T(8,128)(2,1)S(1)}, u32[]{:S(2)}, u32[]{:S(2)}) %collective-permute-start.6) | collective-permute-done | bytes 73760 | tf_op jit(solution)/shard_map/ppermute | solution.py:540
  40.2 2.4 %collective-permute-done.7.p2 = bf16[288,128]{1,0:T(8,128)(2,1)S(1)} collective-permute-done((bf16[288,128]{1,0:T(8,128)(2,1)S(1)}, bf16[288,128]{1,0:T(8,128)(2,1)S(1)}, u32[]{:S(2)}, u32[]{:S(2)}) %collective-permute-start.7) | collective-permute-done | bytes 73760 | tf_op jit(solution)/shard_map/ppermute | solution.py:540
  43.4 1.1 %collective-permute-start.10 = (bf16[96,128]{1,0:T(8,128)(2,1)S(1)}, bf16[96,128]{1,0:T(8,128)(2,1)S(1)}, u32[]{:S(2)}, u32[]{:S(2)}) collective-permute-start(bf16[96,128]{1,0:T(8,128)(2,1)S(1)} %get-tuple-element.29), channel_id=1, source_target_pairs={{0,2},{1,3},{2,0},{3,1},{4,6},{5,7},{6,4},{7,5},{8,10},{9,11},{10,... | collective-permute-start | bytes 73736 | tf_op jit(solution)/shard_map/ppermute | solution.py:536
  45.3 9.3 %collective-permute-done.10.p2 = bf16[96,128]{1,0:T(8,128)(2,1)S(1)} collective-permute-done((bf16[96,128]{1,0:T(8,128)(2,1)S(1)}, bf16[96,128]{1,0:T(8,128)(2,1)S(1)}, u32[]{:S(2)}, u32[]{:S(2)}) %collective-permute-start.10) | collective-permute-done | bytes 24608 | tf_op jit(solution)/shard_map/ppermute | solution.py:536
  55.5 2.0 %output_other.1 = bf16[8,32,512]{2,1,0:T(8,128)(2,1)S(1)} custom-call(s32[2]{0:T(128)S(1)} %copy-done.6, bf16[32,256]{1,0:T(8,128)(2,1)S(1)} %finish.1.attended, bf16[256,8192]{1,0:T(8,128)(2,1)S(1)} %copy-done), custom_call_target="tpu_custom_call" | custom-call | flops 4194304 | bytes 2097152 | tf_op jit(solution)/shard_map/output_other/pallas_call | solution.py:453
  57.9 2.0 %output_own.1.own = f32[8,32,512]{2,1,0:T(8,128)S(1)} custom-call(s32[2]{0:T(128)S(1)} %copy-done.6, bf16[32,256]{1,0:T(8,128)(2,1)S(1)} %finish.1.attended, bf16[256,8192]{1,0:T(8,128)(2,1)S(1)} %copy-done), custom_call_target="tpu_custom_call" | custom-call | flops 4194304 | bytes 2097152 | tf_op jit(solution)/shard_map/output_own/pallas_call | solution.py:453
  60.5 3.1 %collective-permute-start.13 = (bf16[2,32,512]{2,1,0:T(8,128)(2,1)S(1)}, bf16[2,32,512]{2,1,0:T(8,128)(2,1)S(1)}, u32[]{:S(2)}, u32[]{:S(2)}) collective-permute-start(bf16[2,32,512]{2,1,0:T(8,128)(2,1)S(1)} %get-tuple-element.32), channel_id=1, source_target_pairs={{0,12},{1,13},{2,14},{3,15},{4,0},{5,1},{6,2},{7,3},{8,4},{9,5},{1... | collective-permute-start | bytes 196616 | tf_op jit(solution)/shard_map/ppermute | solution.py:540
  65.1 1.8 %collective-permute-done.13.r1 = bf16[2,32,512]{2,1,0:T(8,128)(2,1)S(1)} collective-permute-done((bf16[2,32,512]{2,1,0:T(8,128)(2,1)S(1)}, bf16[2,32,512]{2,1,0:T(8,128)(2,1)S(1)}, u32[]{:S(2)}, u32[]{:S(2)}) %collective-permute-start.13) | collective-permute-done | bytes 65568 | tf_op jit(solution)/shard_map/ppermute | solution.py:540
  66.9 3.0 %collective-permute-done.14.r2 = bf16[2,32,512]{2,1,0:T(8,128)(2,1)S(1)} collective-permute-done((bf16[2,32,512]{2,1,0:T(8,128)(2,1)S(1)}, bf16[2,32,512]{2,1,0:T(8,128)(2,1)S(1)}, u32[]{:S(2)}, u32[]{:S(2)}) %collective-permute-start.14) | collective-permute-done | bytes 65568 | tf_op jit(solution)/shard_map/ppermute | solution.py:540
  72.7 2.4 %collective-permute-done.16.received = bf16[32,512]{1,0:T(8,128)(2,1)S(1)} collective-permute-done((bf16[32,512]{1,0:T(8,128)(2,1)S(1)}, bf16[32,512]{1,0:T(8,128)(2,1)S(1)}, u32[]{:S(2)}, u32[]{:S(2)}) %collective-permute-start.16) | collective-permute-done | bytes 32800 | tf_op jit(solution)/shard_map/ppermute | solution.py:536
  75.2 1.2 %mix.1 = bf16[32,512]{1,0:T(8,128)(2,1)} custom-call(s32[2]{0:T(128)S(1)} %copy-done.6, f32[1]{0:T(128)S(6)} %copy.17.gate, f32[32,512]{1,0:T(8,128)S(1)} %get-tuple-element.35.own, bf16[32,512]{1,0:T(8,128)(2,1)S(1)} %collective-permute-done.16.received, bf16[32,8192]{1,0:T(8,128)(2,1)S(1)} %copy-done.5), custom_call_target="tpu_custom_call" | custom-call | flops 1048576 | bytes 262144 | tf_op jit(solution)/shard_map/mix/pallas_call | solution.py:523
  76.4 4.0 %unpack.1 = (bf16[8,32,1024]{2,1,0:T(8,128)(2,1)}, bf16[8,32,1024]{2,1,0:T(8,128)(2,1)}, bf16[8,8]{1,0:T(8,128)(2,1)}, bf16[8,8]{1,0:T(8,128)(2,1)}) custom-call(s32[2]{0:T(128)S(1)} %copy-done.6, s32[6,16]{1,0:T(8,128)S(1)} %bitcast.20, s32[1,6]{1,0:T(1,128)S(1)} %copy-done.10, bf16[16,520,128]{2,1,0:T(8,128)(2,1)S(1)} %all-to-all-done.received, ...), custom_call_target="tpu_custom_call" | custom-call | flops 1048576 | bytes 4194304 | tf_op jit(solution)/shard_map/unpack/pallas_call | solution.py:203
  (51 shorter events, 12.7 us)
Async XLA Ops:
  4.0 29.9 %copy-start.1 = (bf16[8,32,1024]{2,1,0:T(8,128)(2,1)S(1)}, bf16[8,32,1024]{2,1,0:T(8,128)(2,1)}, u32[]{:S(2)}) copy-start(bf16[8,32,1024]{2,1,0:T(8,128)(2,1)} %keys.5) | copy-start | bytes 1572868
  4.0 29.9 %copy-start.2 = (bf16[8,32,1024]{2,1,0:T(8,128)(2,1)S(1)}, bf16[8,32,1024]{2,1,0:T(8,128)(2,1)}, u32[]{:S(2)}) copy-start(bf16[8,32,1024]{2,1,0:T(8,128)(2,1)} %values.5) | copy-start | bytes 1572868
  4.0 29.9 %copy-start.6 = (s32[2]{0:T(128)S(1)}, s32[2]{0:T(128)}, u32[]{:S(2)}) copy-start(s32[2]{0:T(128)} %pad_add_fusion.at) | copy-start | bytes 28
  4.0 29.9 %copy-start.7 = (bf16[8,1,8]{2,0,1:T(8,128)(2,1)S(1)}, bf16[8,1,8]{2,0,1:T(8,128)(2,1)}, u32[]{:S(2)}) copy-start(bf16[8,1,8]{2,0,1:T(8,128)(2,1)} %param.19) | copy-start | bytes 388
  4.0 29.9 %copy-start.8 = (bf16[8,1,8]{2,0,1:T(8,128)(2,1)S(1)}, bf16[8,1,8]{2,0,1:T(8,128)(2,1)}, u32[]{:S(2)}) copy-start(bf16[8,1,8]{2,0,1:T(8,128)(2,1)} %param.20) | copy-start | bytes 388
  4.0 72.3 %all-to-all-start = ((bf16[16,520,128]{2,1,0:T(8,128)(2,1)}), bf16[16,520,128]{2,1,0:T(8,128)(2,1)S(1)}, u32[]{:S(2)}, u32[]{:S(2)}) async-start(bf16[16,520,128]{2,1,0:T(8,128)(2,1)} %pack.1), calls=%async_computation | async-start | bytes 4259840 | tf_op jit(solution)/shard_map/all_to_all | solution.py:577
  14.3 41.2 %copy-start = (bf16[256,8192]{1,0:T(8,128)(2,1)S(1)}, bf16[256,8192]{1,0:T(8,128)(2,1)}, u32[]{:S(2)}) copy-start(bf16[256,8192]{1,0:T(8,128)(2,1)} %weight.5) | copy-start | bytes 12582916
  19.6 3.5 %collective-permute-start.2 = (bf16[32,256]{1,0:T(8,128)(2,1)S(1)}, bf16[32,256]{1,0:T(8,128)(2,1)S(1)}, u32[]{:S(2)}, u32[]{:S(2)}) collective-permute-start(bf16[32,256]{1,0:T(8,128)(2,1)S(1)} %query.1), channel_id=1, source_target_pairs={{0,3},{1,2},{2,1},{3,0},{4,7},{5,6},{6,5},{7,4},{8,11},{9,10},{10,... | collective-permute-start | bytes 49160 | tf_op jit(solution)/shard_map/ppermute | solution.py:536
  19.8 4.0 %collective-permute-start.1 = (bf16[32,256]{1,0:T(8,128)(2,1)S(1)}, bf16[32,256]{1,0:T(8,128)(2,1)S(1)}, u32[]{:S(2)}, u32[]{:S(2)}) collective-permute-start(bf16[32,256]{1,0:T(8,128)(2,1)S(1)} %query.1), channel_id=1, source_target_pairs={{0,2},{1,3},{2,0},{3,1},{4,6},{5,7},{6,4},{7,5},{8,10},{9,11},{10,... | collective-permute-start | bytes 49160 | tf_op jit(solution)/shard_map/ppermute | solution.py:536
  21.0 2.8 %collective-permute-start = (bf16[32,256]{1,0:T(8,128)(2,1)S(1)}, bf16[32,256]{1,0:T(8,128)(2,1)S(1)}, u32[]{:S(2)}, u32[]{:S(2)}) collective-permute-start(bf16[32,256]{1,0:T(8,128)(2,1)S(1)} %query.1), channel_id=1, source_target_pairs={{0,1},{1,0},{2,3},{3,2},{4,5},{5,4},{6,7},{7,6},{8,9},{9,8},{10,11... | collective-permute-start | bytes 49160 | tf_op jit(solution)/shard_map/ppermute | solution.py:536
  23.9 6.3 %collective-permute-start.5 = (bf16[4,32,256]{2,1,0:T(8,128)(2,1)S(1)}, bf16[4,32,256]{2,1,0:T(8,128)(2,1)S(1)}, u32[]{:S(2)}, u32[]{:S(2)}) collective-permute-start(bf16[4,32,256]{2,1,0:T(8,128)(2,1)S(1)} %pad_maximum_fusion.q0), channel_id=1, source_target_pairs={{0,12},{1,13},{2,14},{3,15},{4,0},{5,1},{6,2},{7,3},{8,4},{9,5},{1... | collective-permute-start | bytes 196616 | tf_op jit(solution)/shard_map/ppermute | solution.py:540
  27.0 6.2 %collective-permute-start.4 = (bf16[4,32,256]{2,1,0:T(8,128)(2,1)S(1)}, bf16[4,32,256]{2,1,0:T(8,128)(2,1)S(1)}, u32[]{:S(2)}, u32[]{:S(2)}) collective-permute-start(bf16[4,32,256]{2,1,0:T(8,128)(2,1)S(1)} %pad_maximum_fusion.q0), channel_id=1, source_target_pairs={{0,8},{1,9},{2,10},{3,11},{4,12},{5,13},{6,14},{7,15},{8,0},{9,1},... | collective-permute-start | bytes 196616 | tf_op jit(solution)/shard_map/ppermute | solution.py:540
  27.6 6.3 %collective-permute-start.3 = (bf16[4,32,256]{2,1,0:T(8,128)(2,1)S(1)}, bf16[4,32,256]{2,1,0:T(8,128)(2,1)S(1)}, u32[]{:S(2)}, u32[]{:S(2)}) collective-permute-start(bf16[4,32,256]{2,1,0:T(8,128)(2,1)S(1)} %pad_maximum_fusion.q0), channel_id=1, source_target_pairs={{0,4},{1,5},{2,6},{3,7},{4,8},{5,9},{6,10},{7,11},{8,12},{9,13},{1... | collective-permute-start | bytes 196616 | tf_op jit(solution)/shard_map/ppermute | solution.py:540
  35.5 4.7 %collective-permute-start.6 = (bf16[288,128]{1,0:T(8,128)(2,1)S(1)}, bf16[288,128]{1,0:T(8,128)(2,1)S(1)}, u32[]{:S(2)}, u32[]{:S(2)}) collective-permute-start(bf16[288,128]{1,0:T(8,128)(2,1)S(1)} %get-tuple-element.24), channel_id=1, source_target_pairs={{0,12},{1,13},{2,14},{3,15},{4,0},{5,1},{6,2},{7,3},{8,4},{9,5},{1... | collective-permute-start | bytes 221192 | tf_op jit(solution)/shard_map/ppermute | solution.py:540
  36.1 6.4 %collective-permute-start.7 = (bf16[288,128]{1,0:T(8,128)(2,1)S(1)}, bf16[288,128]{1,0:T(8,128)(2,1)S(1)}, u32[]{:S(2)}, u32[]{:S(2)}) collective-permute-start(bf16[288,128]{1,0:T(8,128)(2,1)S(1)} %get-tuple-element.25), channel_id=1, source_target_pairs={{0,8},{1,9},{2,10},{3,11},{4,12},{5,13},{6,14},{7,15},{8,0},{9,1},... | collective-permute-start | bytes 221192 | tf_op jit(solution)/shard_map/ppermute | solution.py:540
  36.8 6.2 %collective-permute-start.8 = (bf16[288,128]{1,0:T(8,128)(2,1)S(1)}, bf16[288,128]{1,0:T(8,128)(2,1)S(1)}, u32[]{:S(2)}, u32[]{:S(2)}) collective-permute-start(bf16[288,128]{1,0:T(8,128)(2,1)S(1)} %get-tuple-element.26), channel_id=1, source_target_pairs={{0,4},{1,5},{2,6},{3,7},{4,8},{5,9},{6,10},{7,11},{8,12},{9,13},{1... | collective-permute-start | bytes 221192 | tf_op jit(solution)/shard_map/ppermute | solution.py:540
  43.3 2.0 %collective-permute-start.9 = (bf16[96,128]{1,0:T(8,128)(2,1)S(1)}, bf16[96,128]{1,0:T(8,128)(2,1)S(1)}, u32[]{:S(2)}, u32[]{:S(2)}) collective-permute-start(bf16[96,128]{1,0:T(8,128)(2,1)S(1)} %get-tuple-element.28), channel_id=1, source_target_pairs={{0,1},{1,0},{2,3},{3,2},{4,5},{5,4},{6,7},{7,6},{8,9},{9,8},{10,11... | collective-permute-start | bytes 73736 | tf_op jit(solution)/shard_map/ppermute | solution.py:536
  43.4 11.2 %collective-permute-start.10 = (bf16[96,128]{1,0:T(8,128)(2,1)S(1)}, bf16[96,128]{1,0:T(8,128)(2,1)S(1)}, u32[]{:S(2)}, u32[]{:S(2)}) collective-permute-start(bf16[96,128]{1,0:T(8,128)(2,1)S(1)} %get-tuple-element.29), channel_id=1, source_target_pairs={{0,2},{1,3},{2,0},{3,1},{4,6},{5,7},{6,4},{7,5},{8,10},{9,11},{10,... | collective-permute-start | bytes 73736 | tf_op jit(solution)/shard_map/ppermute | solution.py:536
  44.5 10.7 %collective-permute-start.11 = (bf16[96,128]{1,0:T(8,128)(2,1)S(1)}, bf16[96,128]{1,0:T(8,128)(2,1)S(1)}, u32[]{:S(2)}, u32[]{:S(2)}) collective-permute-start(bf16[96,128]{1,0:T(8,128)(2,1)S(1)} %get-tuple-element.30), channel_id=1, source_target_pairs={{0,3},{1,2},{2,1},{3,0},{4,7},{5,6},{6,5},{7,4},{8,11},{9,10},{10,... | collective-permute-start | bytes 73736 | tf_op jit(solution)/shard_map/ppermute | solution.py:536
  57.6 2.3 %collective-permute-start.12 = (bf16[8,32,512]{2,1,0:T(8,128)(2,1)S(1)}, bf16[8,32,512]{2,1,0:T(8,128)(2,1)S(1)}, u32[]{:S(2)}, u32[]{:S(2)}) collective-permute-start(bf16[8,32,512]{2,1,0:T(8,128)(2,1)S(1)} %output_other.1), channel_id=1, source_target_pairs={{0,1},{1,0},{2,3},{3,2},{4,5},{5,4},{6,7},{7,6},{8,9},{9,8},{10,11... | collective-permute-start | bytes 786440 | tf_op jit(solution)/shard_map/ppermute | solution.py:536
  60.5 6.4 %collective-permute-start.13 = (bf16[2,32,512]{2,1,0:T(8,128)(2,1)S(1)}, bf16[2,32,512]{2,1,0:T(8,128)(2,1)S(1)}, u32[]{:S(2)}, u32[]{:S(2)}) collective-permute-start(bf16[2,32,512]{2,1,0:T(8,128)(2,1)S(1)} %get-tuple-element.32), channel_id=1, source_target_pairs={{0,12},{1,13},{2,14},{3,15},{4,0},{5,1},{6,2},{7,3},{8,4},{9,5},{1... | collective-permute-start | bytes 196616 | tf_op jit(solution)/shard_map/ppermute | solution.py:540
  63.6 6.2 %collective-permute-start.14 = (bf16[2,32,512]{2,1,0:T(8,128)(2,1)S(1)}, bf16[2,32,512]{2,1,0:T(8,128)(2,1)S(1)}, u32[]{:S(2)}, u32[]{:S(2)}) collective-permute-start(bf16[2,32,512]{2,1,0:T(8,128)(2,1)S(1)} %get-tuple-element.33), channel_id=1, source_target_pairs={{0,8},{1,9},{2,10},{3,11},{4,12},{5,13},{6,14},{7,15},{8,0},{9,1},... | collective-permute-start | bytes 196616 | tf_op jit(solution)/shard_map/ppermute | solution.py:540
  64.3 6.3 %collective-permute-start.15 = (bf16[2,32,512]{2,1,0:T(8,128)(2,1)S(1)}, bf16[2,32,512]{2,1,0:T(8,128)(2,1)S(1)}, u32[]{:S(2)}, u32[]{:S(2)}) collective-permute-start(bf16[2,32,512]{2,1,0:T(8,128)(2,1)S(1)} %get-tuple-element.34), channel_id=1, source_target_pairs={{0,4},{1,5},{2,6},{3,7},{4,8},{5,9},{6,10},{7,11},{8,12},{9,13},{1... | collective-permute-start | bytes 196616 | tf_op jit(solution)/shard_map/ppermute | solution.py:540
  71.2 4.0 %collective-permute-start.16 = (bf16[32,512]{1,0:T(8,128)(2,1)S(1)}, bf16[32,512]{1,0:T(8,128)(2,1)S(1)}, u32[]{:S(2)}, u32[]{:S(2)}) collective-permute-start(bf16[32,512]{1,0:T(8,128)(2,1)S(1)} %get-tuple-element.36), channel_id=1, source_target_pairs={{0,2},{1,3},{2,0},{3,1},{4,6},{5,7},{6,4},{7,5},{8,10},{9,11},{10,... | collective-permute-start | bytes 98312 | tf_op jit(solution)/shard_map/ppermute | solution.py:536
  (7 other events, 104.3 us)

commit v2 on v1

--- a/solution.py
+++ b/solution.py
@@ -22,10 +22,12 @@
 TENSORS = 16
 SLOT = 2 * KVH * SPAN + 8
 COLS = 512
+STEPS = 8
 
 
 VMEM = pl.BlockSpec(memory_space=pltpu.VMEM)
 SMEM = pl.BlockSpec(memory_space=pltpu.SMEM)
+HBM = pl.BlockSpec(memory_space=pltpu.HBM)
 ANY = pl.BlockSpec(memory_space=pl.ANY)
 
 
@@ -51,10 +53,12 @@
     scr[HELD : 2 * HELD, 0:KVH] = value_scales[...].astype(F32)
 
 
-def pack_kernel(
-    at, dest, slots, keys, values, key_scales, value_scales, out, held, stage, scr, in_sem, out_sem
+def front_kernel(
+    dest, slots, keys, values, key_scales, value_scales, hidden, weight, gain,
+    message, query, residual,
+    held, stage, scr, rows, blocks, in_sem, out_sem, rows_sem, block_sem,
 ):
-    here = at[0]
+    here, rank = lax.axis_index("replica"), lax.axis_index("tensor")
     loads = []
     for j in range(MOVE):
         s = slots[0, j]
@@ -65,6 +69,16 @@
         for copy in pair:
             copy.start()
         loads.append(pair)
+    rows_in = pltpu.make_async_copy(hidden, rows, rows_sem)
+    rows_in.start()
+    depth = blocks.shape[1]
+    weights_in = []
+    for i in range(STEPS):
+        copy = pltpu.make_async_copy(
+            weight.at[i * depth : (i + 1) * depth, :], blocks.at[i], block_sem.at[i]
+        )
+        copy.start()
+        weights_in.append(copy)
     scale_rows(scr, key_scales, value_scales)
     row = iota((8, HD), 0)
     stores = []
@@ -81,61 +95,63 @@
             for c in range(KVH):
                 at_row = (which * KVH + c) * SPAN
                 stage[j, at_row : at_row + SPAN, :] = held[j, which, :, c * HD : (c + 1) * HD]
-        copy = pltpu.make_async_copy(stage.at[j], out.at[dest[j, here]], out_sem.at[j])
+        copy = pltpu.make_async_copy(stage.at[j], message.at[dest[j, here]], out_sem.at[j])
         copy.start()
         stores.append(copy)
+    rows_in.wait()
+    total = jnp.zeros((ROWS, 2 * HD), F32)
+    for i in range(STEPS):
+        weights_in[i].wait()
+        total = total + jnp.dot(
+            rows[:, i * depth : (i + 1) * depth], blocks[i], preferred_element_type=F32
+        )
+    for h in range(2):
+        part = total[:, h * HD : (h + 1) * HD]
+        mean = jnp.mean(part * part, axis=-1, keepdims=True)
+        part = part * lax.rsqrt(mean + EPSILON)
+        query[:, h * HD : (h + 1) * HD] = (part * gain[...] * HD ** (-0.5)).astype(BF16)
+    residual[...] = rows[:, pl.ds(pl.multiple_of(rank * COLS, COLS), COLS)]
     for copy in stores:
         copy.wait()
 
 
-def pack(at, dest, slots, keys, values, key_scales, value_scales):
-    return pl.pallas_call(
-        pack_kernel,
-        out_shape=shape((REPLICAS, SLOT, HD), BF16),
-        in_specs=[SMEM, SMEM, SMEM, ANY, ANY, VMEM, VMEM],
-        out_specs=ANY,
+def front(dest, slots, keys, values, key_scales, value_scales, hidden, q_weight, q_gain):
+    depth = hidden.shape[1] // STEPS
+    return pl.pallas_call(
+        front_kernel,
+        out_shape=(
+            shape((REPLICAS, SLOT, HD), BF16),
+            shape((ROWS, 2 * HD), BF16),
+            shape((ROWS, COLS), BF16),
+        ),
+        in_specs=[SMEM, SMEM, HBM, HBM, VMEM, VMEM, HBM, HBM, VMEM],
+        out_specs=(HBM, VMEM, VMEM),
         scratch_shapes=[
             pltpu.VMEM((MOVE, 2, SPAN, KVH * HD), BF16),
             pltpu.VMEM((MOVE, SLOT, HD), BF16),
             pltpu.VMEM((2 * HELD, HD), F32),
+            pltpu.VMEM(hidden.shape, BF16),
+            pltpu.VMEM((STEPS, depth, 2 * HD), BF16),
             pltpu.SemaphoreType.DMA((MOVE, 2)),
             pltpu.SemaphoreType.DMA((MOVE,)),
+            pltpu.SemaphoreType.DMA,
+            pltpu.SemaphoreType.DMA((STEPS,)),
         ],
-        cost_estimate=cost(1 << 20, 4 << 20),
-        name="pack",
-    )(at, dest, slots, keys, values, key_scales, value_scales)
+        cost_estimate=cost(1 << 22, 8 << 20),
+        compiler_params=room(57),
+        name="front",
+    )(
+        dest, slots, keys, values, key_scales, value_scales, hidden, q_weight,
+        q_gain.reshape(1, HD),
+    )
 
 
 def unpack_kernel(
-    at,
-    dest,
-    slots,
-    received,
-    keys,
-    values,
-    key_scales,
-    value_scales,
-    new_keys,
-    new_values,
-    new_key_scales,
-    new_value_scales,
-    landed,
-    stage,
-    kept,
-    scr,
-    in_sem,
-    out_sem,
-    kept_sem,
+    dest, slots, received, keys, values, key_scales, value_scales,
+    new_keys, new_values, new_key_scales, new_value_scales,
+    stage, kept, scr, out_sem, kept_sem,
 ):
-    here = at[0]
-    loads = []
-    for j in range(MOVE):
-        source = jnp.int32(0)
-        for p in range(REPLICAS):
-            source = jnp.where(dest[j, p] == here, p, source)
-        copy = pltpu.make_async_copy(received.at[source], landed.at[j], in_sem.at[j])
-        copy.start()
-        loads.append(copy)
+    here = lax.axis_index("replica")
     stays = []
     for r in range(HELD):
         moving = slots[0, 0] == r
@@ -163,6 +179,26 @@
                 copy.start()
 
     scale_rows(scr, key_scales, value_scales)
+    stores = []
+    for j in range(MOVE):
+        s = slots[0, j]
+        source = jnp.int32(0)
+        for p in range(REPLICAS):
+            source = jnp.where(dest[j, p] == here, p, source)
+        both = received[source, 2 * KVH * SPAN : SLOT, :].astype(F32)
+        scr[pl.ds(s, 1), :] = both[0:1, :]
+        scr[pl.ds(HELD + s, 1), :] = both[1:2, :]
+        for which, target in ((0, new_keys), (1, new_values)):
+            for c in range(KVH):
+                at_row = (which * KVH + c) * SPAN
+                stage[j, which, :, c * HD : (c + 1) * HD] = received[
+                    source, at_row : at_row + SPAN, :
+                ]
+            copy = pltpu.make_async_copy(stage.at[j, which], target.at[s], out_sem.at[j, which])
+            copy.start()
+            stores.append(copy)
+    new_key_scales[...] = scr[0:HELD, 0:KVH].astype(BF16)
+    new_value_scales[...] = scr[HELD : 2 * HELD, 0:KVH].astype(BF16)
     for r in range(HELD):
 
         @pl.when(stays[r])
@@ -172,22 +208,6 @@
             for copy in kept_out(r):
                 copy.start()
 
-    stores = []
-    for j in range(MOVE):
-        s = slots[0, j]
-        loads[j].wait()
-        both = landed[j, 2 * KVH * SPAN : SLOT, :].astype(F32)
-        scr[pl.ds(s, 1), :] = both[0:1, :]
-        scr[pl.ds(HELD + s, 1), :] = both[1:2, :]
-        for which, target in ((0, new_keys), (1, new_values)):
-            for c in range(KVH):
-                at_row = (which * KVH + c) * SPAN
-                stage[j, which, :, c * HD : (c + 1) * HD] = landed[j, at_row : at_row + SPAN, :]
-            copy = pltpu.make_async_copy(stage.at[j, which], target.at[s], out_sem.at[j, which])
-            copy.start()
-            stores.append(copy)
-    new_key_scales[...] = scr[0:HELD, 0:KVH].astype(BF16)
-    new_value_scales[...] = scr[HELD : 2 * HELD, 0:KVH].astype(BF16)
     for r in range(HELD):
 
         @pl.when(stays[r])
@@ -199,7 +219,7 @@
         copy.wait()
 
 
-def unpack(at, dest, slots, received, keys, values, key_scales, value_scales):
+def unpack(dest, slots, received, keys, values, key_scales, value_scales):
     return pl.pallas_call(
         unpack_kernel,
         out_shape=(
@@ -208,60 +228,19 @@
             shape((HELD, KVH), BF16),
             shape((HELD, KVH), BF16),
         ),
-        in_specs=[SMEM, SMEM, SMEM, ANY, ANY, ANY, VMEM, VMEM],
-        out_specs=(ANY, ANY, VMEM, VMEM),
+        in_specs=[SMEM, SMEM, VMEM, HBM, HBM, VMEM, VMEM],
+        out_specs=(HBM, HBM, VMEM, VMEM),
         scratch_shapes=[
-            pltpu.VMEM((MOVE, SLOT, HD), BF16),
             pltpu.VMEM((MOVE, 2, SPAN, KVH * HD), BF16),
             pltpu.VMEM((HELD, 2, SPAN, KVH * HD), BF16),
             pltpu.VMEM((2 * HELD, HD), F32),
-            pltpu.SemaphoreType.DMA((MOVE,)),
             pltpu.SemaphoreType.DMA((MOVE, 2)),
             pltpu.SemaphoreType.DMA((HELD, 2)),
         ],
         cost_estimate=cost(1 << 20, 4 << 20),
         compiler_params=room(8),
         name="unpack",
-    )(at, dest, slots, received, keys, values, key_scales, value_scales)
-
-
-def query_kernel(hidden, weight, gain, query, total):
-    step = pl.program_id(0)
-
-    @pl.when(step == 0)
-    def _():
-        total[...] = jnp.zeros_like(total)
-
-    total[...] += jnp.dot(hidden[...], weight[...], preferred_element_type=F32)
-
-    @pl.when(step == pl.num_programs(0) - 1)
-    def _():
-        for h in range(2):
-            part = total[:, h * HD : (h + 1) * HD]
-            mean = jnp.mean(part * part, axis=-1, keepdims=True)
-            part = part * lax.rsqrt(mean + EPSILON)
-            query[:, h * HD : (h + 1) * HD] = (part * gain[...] * HD ** (-0.5)).astype(BF16)
-
-
-def project_query(hidden, q_weight, q_gain):
-    depth = hidden.shape[1]
-    steps = 8
-    block = depth // steps
-    return pl.pallas_call(
-        query_kernel,
-        grid=(steps,),
-        out_shape=shape((ROWS, 2 * HD), BF16),
-        in_specs=[
-            pl.BlockSpec((ROWS, block), lambda i: (0, i)),
-            pl.BlockSpec((block, 2 * HD), lambda i: (i, 0)),
-            pl.BlockSpec((1, HD), lambda i: (0, 0)),
-        ],
-        out_specs=pl.BlockSpec((ROWS, 2 * HD), lambda i: (0, 0)),
-        scratch_shapes=[pltpu.VMEM((ROWS, 2 * HD), F32)],
-        cost_estimate=cost(4 << 20, 4 << 20),
-        compiler_params=room(8),
-        name="query",
-    )(hidden, q_weight, q_gain.reshape(1, HD))
+    )(dest, slots, received, keys, values, key_scales, value_scales)
 
 
 def split3(x):
@@ -291,10 +270,10 @@
 
 
 def attend_kernel(
-    at, lengths, q0, q1, q2, q3, keys, values, key_scales, value_scales,
+    lengths, q0, q1, q2, q3, keys, values, key_scales, value_scales,
     o0, o1, o2, o3, q_all, o_all, mask, stats,
 ):
-    rank = at[1]
+    rank = lax.axis_index("tensor")
     y = rank // 4
     x = (rank // 2) % 2
     for k, q in enumerate((q0, q1, q2, q3)):
@@ -348,12 +327,12 @@
         put_stats(o, 2 * HD, turned[8 * k : 8 * k + 8])
 
 
-def attend(at, lengths, queries, keys, values, key_scales, value_scales):
+def attend(lengths, queries, keys, values, key_scales, value_scales):
     out = shape((2 * HD + 32, HD), BF16)
     return pl.pallas_call(
         attend_kernel,
         out_shape=(out,) * 4,
-        in_specs=[SMEM, SMEM] + [VMEM] * 8,
+        in_specs=[SMEM] + [VMEM] * 8,
         out_specs=(VMEM,) * 4,
         scratch_shapes=[
             pltpu.VMEM((4, 4, ROWS, 2 * HD), BF16),
@@ -364,7 +343,7 @@
         cost_estimate=cost(4 << 20, 2 << 20),
         compiler_params=room(8),
         name="attend",
-    )(at, lengths, *queries, keys, values, key_scales, value_scales)
+    )(lengths, *queries, keys, values, key_scales, value_scales)
 
 
 def merged(stats):
@@ -403,8 +382,7 @@
     )(*parts)
 
 
-def finish_kernel(p0, p1, p2, p3, attended):
-    parts = (p0, p1, p2, p3)
+def finished(parts):
     stats = []
     for d, p in enumerate(parts):
         s = get_stats(p, HD // 2)
@@ -419,54 +397,75 @@
     summed = jnp.zeros((HD // 2, HD), F32)
     for d, p in enumerate(parts):
         summed = summed + p[0 : HD // 2, :].astype(F32) * column[0 : HD // 2, 8 * d : 8 * d + 1]
-    for h in range(2):
-        attended[:, h * HD : (h + 1) * HD] = summed[h * ROWS : (h + 1) * ROWS].astype(BF16)
-
-
-def finish(parts):
-    return pl.pallas_call(
-        finish_kernel,
-        out_shape=shape((ROWS, 2 * HD), BF16),
-        in_specs=[VMEM] * 4,
-        out_specs=VMEM,
-        cost_estimate=cost(1 << 20, 1 << 19),
-        compiler_params=room(4),
-        name="finish",
-    )(*parts)
-
-
-def output_kernel(other, at, attended, weight, out, blocks, sem):
-    core = (at[1] + other) % 2
+    return summed.astype(BF16)
+
+
+def half_in(core, weight, blocks, sem):
     copies = []
     for i in range(TENSORS // 2):
         start = pl.multiple_of((2 * i + core) * COLS, COLS)
         copy = pltpu.make_async_copy(weight.at[:, pl.ds(start, COLS)], blocks.at[i], sem.at[i])
         copy.start()
         copies.append(copy)
-    for i in range(TENSORS // 2):
-        copies[i].wait()
-        out[i] = jnp.dot(attended[...], blocks[i], preferred_element_type=F32).astype(out.dtype)
-
-
-def project_output(other, dtype, at, attended, o_weight):
-    half = TENSORS // 2
-    return pl.pallas_call(
-        functools.partial(output_kernel, other),
-        out_shape=shape((half, ROWS, COLS), dtype),
-        in_specs=[SMEM, VMEM, ANY],
+    return copies
+
+
+def half_out(copies, attended, blocks, out):
+    for i, copy in enumerate(copies):
+        copy.wait()
+        out[i] = jnp.dot(attended, blocks[i], preferred_element_type=F32).astype(out.dtype)
+
+
+def output_other_kernel(p0, p1, p2, p3, weight, attended, out, blocks, sem):
+    copies = half_in(1 - lax.axis_index("tensor") % 2, weight, blocks, sem)
+    both = finished((p0, p1, p2, p3))
+    for h in range(2):
+        attended[:, h * HD : (h + 1) * HD] = both[h * ROWS : (h + 1) * ROWS]
+    half_out(copies, attended[...], blocks, out)
+
+
+def output_own_kernel(attended, weight, out, blocks, sem):
+    copies = half_in(lax.axis_index("tensor") % 2, weight, blocks, sem)
+    half_out(copies, attended[...], blocks, out)
+
+
+HALF_SCRATCH = [
+    pltpu.VMEM((TENSORS // 2, 2 * HD, COLS), BF16),
+    pltpu.SemaphoreType.DMA((TENSORS // 2,)),
+]
+
+
+def output_other(parts, o_weight):
+    return pl.pallas_call(
+        output_other_kernel,
+        out_shape=(
+            shape((ROWS, 2 * HD), BF16),
+            shape((TENSORS // 2, ROWS, COLS), BF16),
+        ),
+        in_specs=[VMEM] * 4 + [ANY],
+        out_specs=(VMEM, VMEM),
+        scratch_shapes=HALF_SCRATCH,
+        cost_estimate=cost(1 << 22, 2 << 20),
+        compiler_params=room(51),
+        name="output_other",
+    )(*parts, o_weight)
+
+
+def output_own(attended, o_weight):
+    return pl.pallas_call(
+        output_own_kernel,
+        out_shape=shape((TENSORS // 2, ROWS, COLS), F32),
+        in_specs=[VMEM, ANY],
         out_specs=VMEM,
-        scratch_shapes=[
-            pltpu.VMEM((half, 2 * HD, COLS), BF16),
-            pltpu.SemaphoreType.DMA((half,)),
-        ],
+        scratch_shapes=HALF_SCRATCH,
         cost_estimate=cost(1 << 22, 2 << 20),
-        compiler_params=room(8),
-        name="output_other" if other else "output_own",
-    )(at, attended, o_weight)
-
-
-def share_kernel(at, own, received, keep, s1, s2, s3):
-    y = at[1] // 4
+        compiler_params=room(51),
+        name="output_own",
+    )(attended, o_weight)
+
+
+def share_kernel(own, received, keep, s1, s2, s3):
+    y = lax.axis_index("tensor") // 4
     for k in range(4):
         group = (y - k + 4) % 4
         for c in range(2):
@@ -477,59 +476,54 @@
                 (s1, s2, s3)[k - 1][c] = value.astype(BF16)
 
 
-def share(at, own, received):
+def share(own, received):
     out = shape((2, ROWS, COLS), BF16)
     return pl.pallas_call(
         share_kernel,
         out_shape=(shape((2, ROWS, COLS), F32), out, out, out),
-        in_specs=[SMEM, VMEM, VMEM],
+        in_specs=[VMEM, VMEM],
         out_specs=(VMEM,) * 4,
         cost_estimate=cost(1 << 20, 1 << 20),
         compiler_params=room(6),
         name="share",
-    )(at, own, received)
-
-
-def narrow_kernel(at, own, r1, r2, r3, keep, send):
-    x = (at[1] // 2) % 2
+    )(own, received)
+
+
+def narrow_kernel(own, r1, r2, r3, keep, send):
+    x = (lax.axis_index("tensor") // 2) % 2
     for c, out in ((x, keep), (1 - x, send)):
         value = own[c] + r1[c].astype(F32) + r2[c].astype(F32) + r3[c].astype(F32)
         out[...] = value.astype(out.dtype)
 
 
-def narrow(at, own, received):
+def narrow(own, received):
     return pl.pallas_call(
         narrow_kernel,
         out_shape=(shape((ROWS, COLS), F32), shape((ROWS, COLS), BF16)),
-        in_specs=[SMEM] + [VMEM] * 4,
+        in_specs=[VMEM] * 4,
         out_specs=(VMEM,) * 2,
         cost_estimate=cost(1 << 20, 1 << 19),
         compiler_params=room(4),
         name="narrow",
-    )(at, own, *received)
-
-
-def mix_kernel(at, gate, own, received, hidden, out, rows, sem):
-    start = pl.multiple_of(at[1] * COLS, COLS)
-    copy = pltpu.make_async_copy(hidden.at[:, pl.ds(start, COLS)], rows, sem)
-    copy.start()
+    )(own, *received)
+
+
+def mix_kernel(gate, own, received, residual, out):
     scale = jnp.tanh(jnp.full((8, HD), gate[0], F32))[0:1, 0:1]
     summed = own[...] + received[...].astype(F32)
-    copy.wait()
-    out[...] = (rows[...].astype(F32) + scale * summed).astype(BF16)
-
-
-def mix(at, gate, own, received, hidden):
+    out[...] = (residual[...].astype(F32) + scale * summed).astype(BF16)
+
+
+def mix(gate, own, received, residual):
     return pl.pallas_call(
         mix_kernel,
         out_shape=shape((ROWS, COLS), BF16),
-        in_specs=[SMEM, SMEM, VMEM, VMEM, ANY],
+        in_specs=[SMEM, VMEM, VMEM, VMEM],
         out_specs=VMEM,
-        scratch_shapes=[pltpu.VMEM((ROWS, COLS), BF16), pltpu.SemaphoreType.DMA],
         cost_estimate=cost(1 << 20, 1 << 18),
         compiler_params=room(4),
         name="mix",
-    )(at, gate, own, received, hidden)
+    )(gate, own, received, residual)
 
 
 def swap(array, bits):
@@ -541,19 +535,18 @@
 
 
 def attention(
-    at, hidden, q_weight, q_gain, o_weight, attn_gate, keys, values, key_scales, value_scales, lengths
+    query, residual, o_weight, attn_gate, keys, values, key_scales, value_scales, lengths
 ):
-    query = project_query(hidden, q_weight, q_gain)
     local = jnp.stack([query] + [swap(query, d) for d in (1, 2, 3)])
     queries = [local] + [shift(local, k) for k in (1, 2, 3)]
-    parts = attend(at, lengths, queries, keys, values, key_scales, value_scales)
+    parts = attend(lengths, queries, keys, values, key_scales, value_scales)
     parts = combine([parts[0]] + [shift(parts[k], -k) for k in (1, 2, 3)])
-    attended = finish([parts[0]] + [swap(parts[d], d) for d in (1, 2, 3)])
-    other = swap(project_output(1, BF16, at, attended, o_weight), 1)
-    own = project_output(0, F32, at, attended, o_weight)
-    own, *sent = share(at, own, other)
-    own, sent = narrow(at, own, [shift(s, -k) for k, s in zip((1, 2, 3), sent)])
-    return mix(at, attn_gate, own, swap(sent, 2), hidden)
+    parts = [parts[0]] + [swap(parts[d], d) for d in (1, 2, 3)]
+    attended, other = output_other(parts, o_weight)
+    other = swap(other, 1)
+    own, *sent = share(output_own(attended, o_weight), other)
+    own, sent = narrow(own, [shift(s, -k) for k, s in zip((1, 2, 3), sent)])
+    return mix(attn_gate, own, swap(sent, 2), residual)
 
 
 def local(
@@ -570,19 +563,21 @@
     dest_replica,
     move_slot,
 ):
-    at = jnp.stack([lax.axis_index("replica"), lax.axis_index("tensor")]).astype(I32)
     dest = dest_replica.T
     key_scales, value_scales = key_scales[:, 0, :], value_scales[:, 0, :]
-    message = pack(at, dest, move_slot, key_codes, value_codes, key_scales, value_scales)
+    message, query, residual = front(
+        dest, move_slot, key_codes, value_codes, key_scales, value_scales,
+        hidden, q_weight, q_gain,
+    )
     received = lax.all_to_all(
         message, "replica", split_axis=0, concat_axis=0, tiled=True
     )
     mixed = attention(
-        at, hidden, q_weight, q_gain, o_weight, attn_gate,
+        query, residual, o_weight, attn_gate,
         key_codes, value_codes, key_scales, value_scales, lengths,
     )
     new_keys, new_values, new_ks, new_vs = unpack(
-        at, dest, move_slot, received, key_codes, value_codes, key_scales, value_scales
+        dest, move_slot, received, key_codes, value_codes, key_scales, value_scales
     )
     return (mixed, new_keys, new_values, new_ks[:, None, :], new_vs[:, None, :])
 

time: 80.6 us -> 79.5 us (0.986)
  the two profiles are of different devices: /device:TPU:100 before, /device:TPU:96 now
where the time goes in v2:
time: 79.5 us; the launch traced here: 79.3 us
  waiting for transfers between devices  31.3 us (39%)
  starting transfers between devices  30.6 us (38%)
  Pallas kernels  15.9 us (20%)
  between operations  1.45 us (2%)
    ppermute x8, waiting for transfers between devices, swap(): lax.ppermute(array, 'tensor', [(i, i ^ bits) for i in range(TENSORS)])  17.8 us
    ppermute x9, starting transfers between devices, shift(): lax.ppermute(array, 'tensor', [(i, (i + 4 * rows) % TENSORS) for i in ran...  14.2 us
    ppermute x9, waiting for transfers between devices, shift(): lax.ppermute(array, 'tensor', [(i, (i + 4 * rows) % TENSORS) for i in ran...  13.5 us
    all_to_all x1, starting transfers between devices, local(): lax.all_to_all(message, 'replica', split_axis=0, concat_axis=0, tiled=True)  10.1 us
    ppermute x8, starting transfers between devices, swap(): lax.ppermute(array, 'tensor', [(i, i ^ bits) for i in range(TENSORS)])  6.25 us
    pallas_call x1, Pallas kernels, front(): pl.pallas_call(front_kernel, out_shape=(shape((REPLICAS, SLOT, HD), BF16)...  5.88 us
    pallas_call x1, Pallas kernels, unpack(): pl.pallas_call(unpack_kernel, out_shape=(shape(keys.shape, BF16), shape(v...  2.84 us
    pallas_call x1, Pallas kernels, output_other(): pl.pallas_call(output_other_kernel, out_shape=(shape((ROWS, 2 * HD), BF16...  2.3 us
  transfers between devices with their start and end apart: 18, of which 12 were waited for; matrix products, arithmetic and copies ran while one was open for 0% of the time, Pallas kernels for 9%

profile of v2, /device:TPU:96, one launch (start us, length us, event | category | flops | bytes accessed | tf_op | source)
XLA Modules:
  0.0 79.3 jit_solution(9061442623775867312)
XLA Ops:
  0.7 5.9 %front.1 = (bf16[16,520,128]{2,1,0:T(8,128)(2,1)}, bf16[32,256]{1,0:T(8,128)(2,1)}, bf16[32,512]{1,0:T(8,128)(2,1)}) custom-call(s32[6,16]{1,0:T(8,128)} %bitcast.16, s32[1,6]{1,0:T(1,128)} %slots.3, bf16[8,32,1024]{2,1,0:T(8,128)(2,1)} %keys.5, bf16[8,32,1024]{2,1,0:T(8,128)(2,1)} %values.5, bf16[8,8]{1,0:T(8,128)(2,1)} %bitcast.10, bf16[8,8]{1,0:T(8,128)(2,1)} %bitcast.13, ...), custom_call_target="tpu_custom_call" | custom-call | flops 4194304 | bytes 8388608 | tf_op jit(solution)/shard_map/front/pallas_call | solution.py:120
  6.6 10.1 %all-to-all-start = ((bf16[16,520,128]{2,1,0:T(8,128)(2,1)}), bf16[16,520,128]{2,1,0:T(8,128)(2,1)S(1)}, u32[]{:S(2)}, u32[]{:S(2)}) async-start(bf16[16,520,128]{2,1,0:T(8,128)(2,1)} %get-tuple-element.46), calls=%async_computation | async-start | bytes 4259840 | tf_op jit(solution)/shard_map/all_to_all | solution.py:572
  17.5 1.2 %collective-permute-start.2 = (bf16[32,256]{1,0:T(8,128)(2,1)S(1)}, bf16[32,256]{1,0:T(8,128)(2,1)S(1)}, u32[]{:S(2)}, u32[]{:S(2)}) collective-permute-start(bf16[32,256]{1,0:T(8,128)(2,1)S(1)} %copy-done.8), channel_id=1, source_target_pairs={{0,3},{1,2},{2,1},{3,0},{4,7},{5,6},{6,5},{7,4},{8,11},{9,10},{10,... | collective-permute-start | bytes 49160 | tf_op jit(solution)/shard_map/ppermute | solution.py:530
  18.7 6.1 %collective-permute-done.1 = bf16[32,256]{1,0:T(8,128)(2,1)S(1)} collective-permute-done((bf16[32,256]{1,0:T(8,128)(2,1)S(1)}, bf16[32,256]{1,0:T(8,128)(2,1)S(1)}, u32[]{:S(2)}, u32[]{:S(2)}) %collective-permute-start.1) | collective-permute-done | bytes 16416 | tf_op jit(solution)/shard_map/ppermute | solution.py:530
  24.8 1.7 %collective-permute-start.3 = (bf16[4,32,256]{2,1,0:T(8,128)(2,1)S(1)}, bf16[4,32,256]{2,1,0:T(8,128)(2,1)S(1)}, u32[]{:S(2)}, u32[]{:S(2)}) collective-permute-start(bf16[4,32,256]{2,1,0:T(8,128)(2,1)S(1)} %pad_maximum_fusion.q0), channel_id=1, source_target_pairs={{0,4},{1,5},{2,6},{3,7},{4,8},{5,9},{6,10},{7,11},{8,12},{9,13},{1... | collective-permute-start | bytes 196616 | tf_op jit(solution)/shard_map/ppermute | solution.py:534
  26.5 2.9 %collective-permute-start.4 = (bf16[4,32,256]{2,1,0:T(8,128)(2,1)S(1)}, bf16[4,32,256]{2,1,0:T(8,128)(2,1)S(1)}, u32[]{:S(2)}, u32[]{:S(2)}) collective-permute-start(bf16[4,32,256]{2,1,0:T(8,128)(2,1)S(1)} %pad_maximum_fusion.q0), channel_id=1, source_target_pairs={{0,8},{1,9},{2,10},{3,11},{4,12},{5,13},{6,14},{7,15},{8,0},{9,1},... | collective-permute-start | bytes 196616 | tf_op jit(solution)/shard_map/ppermute | solution.py:534
  29.4 1.3 %collective-permute-start.5 = (bf16[4,32,256]{2,1,0:T(8,128)(2,1)S(1)}, bf16[4,32,256]{2,1,0:T(8,128)(2,1)S(1)}, u32[]{:S(2)}, u32[]{:S(2)}) collective-permute-start(bf16[4,32,256]{2,1,0:T(8,128)(2,1)S(1)} %pad_maximum_fusion.q0), channel_id=1, source_target_pairs={{0,12},{1,13},{2,14},{3,15},{4,0},{5,1},{6,2},{7,3},{8,4},{9,5},{1... | collective-permute-start | bytes 196616 | tf_op jit(solution)/shard_map/ppermute | solution.py:534
  30.7 2.3 %collective-permute-done.4.q2 = bf16[4,32,256]{2,1,0:T(8,128)(2,1)S(1)} collective-permute-done((bf16[4,32,256]{2,1,0:T(8,128)(2,1)S(1)}, bf16[4,32,256]{2,1,0:T(8,128)(2,1)S(1)}, u32[]{:S(2)}, u32[]{:S(2)}) %collective-permute-start.4) | collective-permute-done | bytes 65568 | tf_op jit(solution)/shard_map/ppermute | solution.py:534
  33.7 1.6 %attend.1 = (bf16[288,128]{1,0:T(8,128)(2,1)S(1)}, bf16[288,128]{1,0:T(8,128)(2,1)S(1)}, bf16[288,128]{1,0:T(8,128)(2,1)S(1)}, bf16[288,128]{1,0:T(8,128)(2,1)S(1)}) custom-call(s32[8]{0:T(128)S(1)} %copy-done.7, bf16[4,32,256]{2,1,0:T(8,128)(2,1)S(1)} %pad_maximum_fusion.q0, bf16[4,32,256]{2,1,0:T(8,128)(2,1)S(1)} %collective-permute-done.3.q1, ...), custom_call_target="tpu_custom_call" | custom-call | flops 4194304 | bytes 2097152 | tf_op jit(solution)/shard_map/attend/pallas_call | solution.py:332
  35.3 2.6 %collective-permute-start.6 = (bf16[288,128]{1,0:T(8,128)(2,1)S(1)}, bf16[288,128]{1,0:T(8,128)(2,1)S(1)}, u32[]{:S(2)}, u32[]{:S(2)}) collective-permute-start(bf16[288,128]{1,0:T(8,128)(2,1)S(1)} %get-tuple-element.30), channel_id=1, source_target_pairs={{0,12},{1,13},{2,14},{3,15},{4,0},{5,1},{6,2},{7,3},{8,4},{9,5},{1... | collective-permute-start | bytes 221192 | tf_op jit(solution)/shard_map/ppermute | solution.py:534
  38.1 0.8 %collective-permute-start.8 = (bf16[288,128]{1,0:T(8,128)(2,1)S(1)}, bf16[288,128]{1,0:T(8,128)(2,1)S(1)}, u32[]{:S(2)}, u32[]{:S(2)}) collective-permute-start(bf16[288,128]{1,0:T(8,128)(2,1)S(1)} %get-tuple-element.32), channel_id=1, source_target_pairs={{0,4},{1,5},{2,6},{3,7},{4,8},{5,9},{6,10},{7,11},{8,12},{9,13},{1... | collective-permute-start | bytes 221192 | tf_op jit(solution)/shard_map/ppermute | solution.py:534
  38.9 1.7 %collective-permute-done.6.p1 = bf16[288,128]{1,0:T(8,128)(2,1)S(1)} collective-permute-done((bf16[288,128]{1,0:T(8,128)(2,1)S(1)}, bf16[288,128]{1,0:T(8,128)(2,1)S(1)}, u32[]{:S(2)}, u32[]{:S(2)}) %collective-permute-start.6) | collective-permute-done | bytes 73760 | tf_op jit(solution)/shard_map/ppermute | solution.py:534
  40.6 3.3 %collective-permute-done.7.p2 = bf16[288,128]{1,0:T(8,128)(2,1)S(1)} collective-permute-done((bf16[288,128]{1,0:T(8,128)(2,1)S(1)}, bf16[288,128]{1,0:T(8,128)(2,1)S(1)}, u32[]{:S(2)}, u32[]{:S(2)}) %collective-permute-start.7) | collective-permute-done | bytes 73760 | tf_op jit(solution)/shard_map/ppermute | solution.py:534
  44.8 1.5 %collective-permute-start.10 = (bf16[96,128]{1,0:T(8,128)(2,1)S(1)}, bf16[96,128]{1,0:T(8,128)(2,1)S(1)}, u32[]{:S(2)}, u32[]{:S(2)}) collective-permute-start(bf16[96,128]{1,0:T(8,128)(2,1)S(1)} %get-tuple-element.35), channel_id=1, source_target_pairs={{0,2},{1,3},{2,0},{3,1},{4,6},{5,7},{6,4},{7,5},{8,10},{9,11},{10,... | collective-permute-start | bytes 73736 | tf_op jit(solution)/shard_map/ppermute | solution.py:530
  47.0 9.5 %collective-permute-done.10.p2 = bf16[96,128]{1,0:T(8,128)(2,1)S(1)} collective-permute-done((bf16[96,128]{1,0:T(8,128)(2,1)S(1)}, bf16[96,128]{1,0:T(8,128)(2,1)S(1)}, u32[]{:S(2)}, u32[]{:S(2)}) %collective-permute-start.10) | collective-permute-done | bytes 24608 | tf_op jit(solution)/shard_map/ppermute | solution.py:530
  56.8 2.3 %output_other.1 = (bf16[32,256]{1,0:T(8,128)(2,1)S(1)}, bf16[8,32,512]{2,1,0:T(8,128)(2,1)S(1)}) custom-call(bf16[96,128]{1,0:T(8,128)(2,1)S(1)} %get-tuple-element.33.p0, bf16[96,128]{1,0:T(8,128)(2,1)S(1)} %collective-permute-done.9.p1, bf16[96,128]{1,0:T(8,128)(2,1)S(1)} %collective-permute-done.10.p2, bf16[96,128]{1,0:T(8,128)(2,1)S(1)} %collective-permute-done.11.p3, ...), custom_call_target="tpu_custom_call" | custom-call | flops 4194304 | bytes 2097152 | tf_op jit(solution)/shard_map/output_other/pallas_call | solution.py:439
  59.7 2.3 %output_own.1.own = f32[8,32,512]{2,1,0:T(8,128)S(1)} custom-call(bf16[32,256]{1,0:T(8,128)(2,1)S(1)} %get-tuple-element.37.attended, bf16[256,8192]{1,0:T(8,128)(2,1)} %weight.5), custom_call_target="tpu_custom_call" | custom-call | flops 4194304 | bytes 2097152 | tf_op jit(solution)/shard_map/output_own/pallas_call | solution.py:455
  62.0 3.1 %collective-permute-start.13 = (bf16[2,32,512]{2,1,0:T(8,128)(2,1)S(1)}, bf16[2,32,512]{2,1,0:T(8,128)(2,1)S(1)}, u32[]{:S(2)}, u32[]{:S(2)}) collective-permute-start(bf16[2,32,512]{2,1,0:T(8,128)(2,1)S(1)} %get-tuple-element.40), channel_id=1, source_target_pairs={{0,12},{1,13},{2,14},{3,15},{4,0},{5,1},{6,2},{7,3},{8,4},{9,5},{1... | collective-permute-start | bytes 196616 | tf_op jit(solution)/shard_map/ppermute | solution.py:534
  65.6 1.1 %collective-permute-start.15 = (bf16[2,32,512]{2,1,0:T(8,128)(2,1)S(1)}, bf16[2,32,512]{2,1,0:T(8,128)(2,1)S(1)}, u32[]{:S(2)}, u32[]{:S(2)}) collective-permute-start(bf16[2,32,512]{2,1,0:T(8,128)(2,1)S(1)} %get-tuple-element.42), channel_id=1, source_target_pairs={{0,4},{1,5},{2,6},{3,7},{4,8},{5,9},{6,10},{7,11},{8,12},{9,13},{1... | collective-permute-start | bytes 196616 | tf_op jit(solution)/shard_map/ppermute | solution.py:534
  66.7 1.4 %collective-permute-done.13.r1 = bf16[2,32,512]{2,1,0:T(8,128)(2,1)S(1)} collective-permute-done((bf16[2,32,512]{2,1,0:T(8,128)(2,1)S(1)}, bf16[2,32,512]{2,1,0:T(8,128)(2,1)S(1)}, u32[]{:S(2)}, u32[]{:S(2)}) %collective-permute-start.13) | collective-permute-done | bytes 65568 | tf_op jit(solution)/shard_map/ppermute | solution.py:534
  68.2 2.9 %collective-permute-done.14.r2 = bf16[2,32,512]{2,1,0:T(8,128)(2,1)S(1)} collective-permute-done((bf16[2,32,512]{2,1,0:T(8,128)(2,1)S(1)}, bf16[2,32,512]{2,1,0:T(8,128)(2,1)S(1)}, u32[]{:S(2)}, u32[]{:S(2)}) %collective-permute-start.14) | collective-permute-done | bytes 65568 | tf_op jit(solution)/shard_map/ppermute | solution.py:534
  71.8 1.5 %collective-permute-start.16 = (bf16[32,512]{1,0:T(8,128)(2,1)S(1)}, bf16[32,512]{1,0:T(8,128)(2,1)S(1)}, u32[]{:S(2)}, u32[]{:S(2)}) collective-permute-start(bf16[32,512]{1,0:T(8,128)(2,1)S(1)} %get-tuple-element.44), channel_id=1, source_target_pairs={{0,2},{1,3},{2,0},{3,1},{4,6},{5,7},{6,4},{7,5},{8,10},{9,11},{10,... | collective-permute-start | bytes 98312 | tf_op jit(solution)/shard_map/ppermute | solution.py:530
  74.0 1.8 %collective-permute-done.16.received = bf16[32,512]{1,0:T(8,128)(2,1)S(1)} collective-permute-done((bf16[32,512]{1,0:T(8,128)(2,1)S(1)}, bf16[32,512]{1,0:T(8,128)(2,1)S(1)}, u32[]{:S(2)}, u32[]{:S(2)}) %collective-permute-start.16) | collective-permute-done | bytes 32800 | tf_op jit(solution)/shard_map/ppermute | solution.py:530
  76.4 2.8 %unpack.1 = (bf16[8,32,1024]{2,1,0:T(8,128)(2,1)}, bf16[8,32,1024]{2,1,0:T(8,128)(2,1)}, bf16[8,8]{1,0:T(8,128)(2,1)}, bf16[8,8]{1,0:T(8,128)(2,1)}) custom-call(s32[6,16]{1,0:T(8,128)S(1)} %bitcast.17, s32[1,6]{1,0:T(1,128)S(1)} %copy-done.6, bf16[16,520,128]{2,1,0:T(8,128)(2,1)S(1)} %all-to-all-done.received, bf16[8,32,1024]{2,1,0:T(8,128)(2,1)S(1)} %copy-done, ...), custom_call_target="tpu_custom_call" | custom-call | flops 1048576 | bytes 4194304 | tf_op jit(solution)/shard_map/unpack/pallas_call | solution.py:223
  (40 shorter events, 5.9 us)
Async XLA Ops:
  0.6 33.0 %copy-start = (bf16[8,32,1024]{2,1,0:T(8,128)(2,1)S(1)}, bf16[8,32,1024]{2,1,0:T(8,128)(2,1)}, u32[]{:S(2)}) copy-start(bf16[8,32,1024]{2,1,0:T(8,128)(2,1)} %keys.5) | copy-start | bytes 1572868
  0.6 33.0 %copy-start.1 = (bf16[8,32,1024]{2,1,0:T(8,128)(2,1)S(1)}, bf16[8,32,1024]{2,1,0:T(8,128)(2,1)}, u32[]{:S(2)}) copy-start(bf16[8,32,1024]{2,1,0:T(8,128)(2,1)} %values.5) | copy-start | bytes 1572868
  0.7 33.0 %copy-start.3 = (bf16[8,1,8]{2,0,1:T(8,128)(2,1)S(1)}, bf16[8,1,8]{2,0,1:T(8,128)(2,1)}, u32[]{:S(2)}) copy-start(bf16[8,1,8]{2,0,1:T(8,128)(2,1)} %param.19) | copy-start | bytes 388
  0.7 33.0 %copy-start.4 = (bf16[8,1,8]{2,0,1:T(8,128)(2,1)S(1)}, bf16[8,1,8]{2,0,1:T(8,128)(2,1)}, u32[]{:S(2)}) copy-start(bf16[8,1,8]{2,0,1:T(8,128)(2,1)} %param.20) | copy-start | bytes 388
  0.7 33.0 %copy-start.7 = (s32[8]{0:T(128)S(1)}, s32[8]{0:T(128)}, u32[]{:S(2)}) copy-start(s32[8]{0:T(128)} %lengths.1) | copy-start | bytes 100
  6.6 69.9 %all-to-all-start = ((bf16[16,520,128]{2,1,0:T(8,128)(2,1)}), bf16[16,520,128]{2,1,0:T(8,128)(2,1)S(1)}, u32[]{:S(2)}, u32[]{:S(2)}) async-start(bf16[16,520,128]{2,1,0:T(8,128)(2,1)} %get-tuple-element.46), calls=%async_computation | async-start | bytes 4259840 | tf_op jit(solution)/shard_map/all_to_all | solution.py:572
  16.7 2.0 %collective-permute-start = (bf16[32,256]{1,0:T(8,128)(2,1)S(1)}, bf16[32,256]{1,0:T(8,128)(2,1)S(1)}, u32[]{:S(2)}, u32[]{:S(2)}) collective-permute-start(bf16[32,256]{1,0:T(8,128)(2,1)S(1)} %copy-done.8), channel_id=1, source_target_pairs={{0,1},{1,0},{2,3},{3,2},{4,5},{5,4},{6,7},{7,6},{8,9},{9,8},{10,11... | collective-permute-start | bytes 49160 | tf_op jit(solution)/shard_map/ppermute | solution.py:530
  16.8 8.0 %collective-permute-start.1 = (bf16[32,256]{1,0:T(8,128)(2,1)S(1)}, bf16[32,256]{1,0:T(8,128)(2,1)S(1)}, u32[]{:S(2)}, u32[]{:S(2)}) collective-permute-start(bf16[32,256]{1,0:T(8,128)(2,1)S(1)} %copy-done.8), channel_id=1, source_target_pairs={{0,2},{1,3},{2,0},{3,1},{4,6},{5,7},{6,4},{7,5},{8,10},{9,11},{10,... | collective-permute-start | bytes 49160 | tf_op jit(solution)/shard_map/ppermute | solution.py:530
  17.5 7.3 %collective-permute-start.2 = (bf16[32,256]{1,0:T(8,128)(2,1)S(1)}, bf16[32,256]{1,0:T(8,128)(2,1)S(1)}, u32[]{:S(2)}, u32[]{:S(2)}) collective-permute-start(bf16[32,256]{1,0:T(8,128)(2,1)S(1)} %copy-done.8), channel_id=1, source_target_pairs={{0,3},{1,2},{2,1},{3,0},{4,7},{5,6},{6,5},{7,4},{8,11},{9,10},{10,... | collective-permute-start | bytes 49160 | tf_op jit(solution)/shard_map/ppermute | solution.py:530
  24.8 5.9 %collective-permute-start.3 = (bf16[4,32,256]{2,1,0:T(8,128)(2,1)S(1)}, bf16[4,32,256]{2,1,0:T(8,128)(2,1)S(1)}, u32[]{:S(2)}, u32[]{:S(2)}) collective-permute-start(bf16[4,32,256]{2,1,0:T(8,128)(2,1)S(1)} %pad_maximum_fusion.q0), channel_id=1, source_target_pairs={{0,4},{1,5},{2,6},{3,7},{4,8},{5,9},{6,10},{7,11},{8,12},{9,13},{1... | collective-permute-start | bytes 196616 | tf_op jit(solution)/shard_map/ppermute | solution.py:534
  26.5 6.6 %collective-permute-start.4 = (bf16[4,32,256]{2,1,0:T(8,128)(2,1)S(1)}, bf16[4,32,256]{2,1,0:T(8,128)(2,1)S(1)}, u32[]{:S(2)}, u32[]{:S(2)}) collective-permute-start(bf16[4,32,256]{2,1,0:T(8,128)(2,1)S(1)} %pad_maximum_fusion.q0), channel_id=1, source_target_pairs={{0,8},{1,9},{2,10},{3,11},{4,12},{5,13},{6,14},{7,15},{8,0},{9,1},... | collective-permute-start | bytes 196616 | tf_op jit(solution)/shard_map/ppermute | solution.py:534
  29.4 4.3 %collective-permute-start.5 = (bf16[4,32,256]{2,1,0:T(8,128)(2,1)S(1)}, bf16[4,32,256]{2,1,0:T(8,128)(2,1)S(1)}, u32[]{:S(2)}, u32[]{:S(2)}) collective-permute-start(bf16[4,32,256]{2,1,0:T(8,128)(2,1)S(1)} %pad_maximum_fusion.q0), channel_id=1, source_target_pairs={{0,12},{1,13},{2,14},{3,15},{4,0},{5,1},{6,2},{7,3},{8,4},{9,5},{1... | collective-permute-start | bytes 196616 | tf_op jit(solution)/shard_map/ppermute | solution.py:534
  35.3 5.3 %collective-permute-start.6 = (bf16[288,128]{1,0:T(8,128)(2,1)S(1)}, bf16[288,128]{1,0:T(8,128)(2,1)S(1)}, u32[]{:S(2)}, u32[]{:S(2)}) collective-permute-start(bf16[288,128]{1,0:T(8,128)(2,1)S(1)} %get-tuple-element.30), channel_id=1, source_target_pairs={{0,12},{1,13},{2,14},{3,15},{4,0},{5,1},{6,2},{7,3},{8,4},{9,5},{1... | collective-permute-start | bytes 221192 | tf_op jit(solution)/shard_map/ppermute | solution.py:534
  37.9 6.0 %collective-permute-start.7 = (bf16[288,128]{1,0:T(8,128)(2,1)S(1)}, bf16[288,128]{1,0:T(8,128)(2,1)S(1)}, u32[]{:S(2)}, u32[]{:S(2)}) collective-permute-start(bf16[288,128]{1,0:T(8,128)(2,1)S(1)} %get-tuple-element.31), channel_id=1, source_target_pairs={{0,8},{1,9},{2,10},{3,11},{4,12},{5,13},{6,14},{7,15},{8,0},{9,1},... | collective-permute-start | bytes 221192 | tf_op jit(solution)/shard_map/ppermute | solution.py:534
  38.1 6.4 %collective-permute-start.8 = (bf16[288,128]{1,0:T(8,128)(2,1)S(1)}, bf16[288,128]{1,0:T(8,128)(2,1)S(1)}, u32[]{:S(2)}, u32[]{:S(2)}) collective-permute-start(bf16[288,128]{1,0:T(8,128)(2,1)S(1)} %get-tuple-element.32), channel_id=1, source_target_pairs={{0,4},{1,5},{2,6},{3,7},{4,8},{5,9},{6,10},{7,11},{8,12},{9,13},{1... | collective-permute-start | bytes 221192 | tf_op jit(solution)/shard_map/ppermute | solution.py:534
  44.8 11.8 %collective-permute-start.10 = (bf16[96,128]{1,0:T(8,128)(2,1)S(1)}, bf16[96,128]{1,0:T(8,128)(2,1)S(1)}, u32[]{:S(2)}, u32[]{:S(2)}) collective-permute-start(bf16[96,128]{1,0:T(8,128)(2,1)S(1)} %get-tuple-element.35), channel_id=1, source_target_pairs={{0,2},{1,3},{2,0},{3,1},{4,6},{5,7},{6,4},{7,5},{8,10},{9,11},{10,... | collective-permute-start | bytes 73736 | tf_op jit(solution)/shard_map/ppermute | solution.py:530
  46.3 10.5 %collective-permute-start.11 = (bf16[96,128]{1,0:T(8,128)(2,1)S(1)}, bf16[96,128]{1,0:T(8,128)(2,1)S(1)}, u32[]{:S(2)}, u32[]{:S(2)}) collective-permute-start(bf16[96,128]{1,0:T(8,128)(2,1)S(1)} %get-tuple-element.36), channel_id=1, source_target_pairs={{0,3},{1,2},{2,1},{3,0},{4,7},{5,6},{6,5},{7,4},{8,11},{9,10},{10,... | collective-permute-start | bytes 73736 | tf_op jit(solution)/shard_map/ppermute | solution.py:530
  46.3 10.5 %collective-permute-start.9 = (bf16[96,128]{1,0:T(8,128)(2,1)S(1)}, bf16[96,128]{1,0:T(8,128)(2,1)S(1)}, u32[]{:S(2)}, u32[]{:S(2)}) collective-permute-start(bf16[96,128]{1,0:T(8,128)(2,1)S(1)} %get-tuple-element.34), channel_id=1, source_target_pairs={{0,1},{1,0},{2,3},{3,2},{4,5},{5,4},{6,7},{7,6},{8,9},{9,8},{10,11... | collective-permute-start | bytes 73736 | tf_op jit(solution)/shard_map/ppermute | solution.py:530
  56.8 19.7 %copy-start.6 = (s32[1,6]{1,0:T(1,128)S(1)}, s32[1,6]{1,0:T(1,128)}, u32[]{:S(2)}) copy-start(s32[1,6]{1,0:T(1,128)} %slots.3) | copy-start | bytes 76
  59.1 2.8 %collective-permute-start.12 = (bf16[8,32,512]{2,1,0:T(8,128)(2,1)S(1)}, bf16[8,32,512]{2,1,0:T(8,128)(2,1)S(1)}, u32[]{:S(2)}, u32[]{:S(2)}) collective-permute-start(bf16[8,32,512]{2,1,0:T(8,128)(2,1)S(1)} %get-tuple-element.38), channel_id=1, source_target_pairs={{0,1},{1,0},{2,3},{3,2},{4,5},{5,4},{6,7},{7,6},{8,9},{9,8},{10,11... | collective-permute-start | bytes 786440 | tf_op jit(solution)/shard_map/ppermute | solution.py:530
  62.0 6.1 %collective-permute-start.13 = (bf16[2,32,512]{2,1,0:T(8,128)(2,1)S(1)}, bf16[2,32,512]{2,1,0:T(8,128)(2,1)S(1)}, u32[]{:S(2)}, u32[]{:S(2)}) collective-permute-start(bf16[2,32,512]{2,1,0:T(8,128)(2,1)S(1)} %get-tuple-element.40), channel_id=1, source_target_pairs={{0,12},{1,13},{2,14},{3,15},{4,0},{5,1},{6,2},{7,3},{8,4},{9,5},{1... | collective-permute-start | bytes 196616 | tf_op jit(solution)/shard_map/ppermute | solution.py:534
  65.1 6.0 %collective-permute-start.14 = (bf16[2,32,512]{2,1,0:T(8,128)(2,1)S(1)}, bf16[2,32,512]{2,1,0:T(8,128)(2,1)S(1)}, u32[]{:S(2)}, u32[]{:S(2)}) collective-permute-start(bf16[2,32,512]{2,1,0:T(8,128)(2,1)S(1)} %get-tuple-element.41), channel_id=1, source_target_pairs={{0,8},{1,9},{2,10},{3,11},{4,12},{5,13},{6,14},{7,15},{8,0},{9,1},... | collective-permute-start | bytes 196616 | tf_op jit(solution)/shard_map/ppermute | solution.py:534
  65.6 6.1 %collective-permute-start.15 = (bf16[2,32,512]{2,1,0:T(8,128)(2,1)S(1)}, bf16[2,32,512]{2,1,0:T(8,128)(2,1)S(1)}, u32[]{:S(2)}, u32[]{:S(2)}) collective-permute-start(bf16[2,32,512]{2,1,0:T(8,128)(2,1)S(1)} %get-tuple-element.42), channel_id=1, source_target_pairs={{0,4},{1,5},{2,6},{3,7},{4,8},{5,9},{6,10},{7,11},{8,12},{9,13},{1... | collective-permute-start | bytes 196616 | tf_op jit(solution)/shard_map/ppermute | solution.py:534
  71.8 4.0 %collective-permute-start.16 = (bf16[32,512]{1,0:T(8,128)(2,1)S(1)}, bf16[32,512]{1,0:T(8,128)(2,1)S(1)}, u32[]{:S(2)}, u32[]{:S(2)}) collective-permute-start(bf16[32,512]{1,0:T(8,128)(2,1)S(1)} %get-tuple-element.44), channel_id=1, source_target_pairs={{0,2},{1,3},{2,0},{3,1},{4,6},{5,7},{6,4},{7,5},{8,10},{9,11},{10,... | collective-permute-start | bytes 98312 | tf_op jit(solution)/shard_map/ppermute | solution.py:530
  (3 other events, 48.8 us)

commit v3 on v2

v3 whole, which is shorter than its diff:
```python
import functools

import jax
import jax.numpy as jnp
from jax import lax
from jax.experimental import pallas as pl
from jax.experimental.pallas import tpu as pltpu
from jax.sharding import PartitionSpec as P

NEGATIVE = -1e30
EPSILON = 1e-06
BF16, F32, I32 = jnp.bfloat16, jnp.float32, jnp.int32

REPLICAS = 16
MOVE = 6
HELD = 8
SPAN = 32
SPEC = 4
ROWS = HELD * SPEC
KVH = 8
HD = 128
TENSORS = 16
SLOT = 2 * KVH * SPAN + 8
COLS = 512
STEPS = 8
FRONT_ROOM, QUERY_ROOM, OUTPUT_ROOM = 57, 53.6, 51


VMEM = pl.BlockSpec(memory_space=pltpu.VMEM)
SMEM = pl.BlockSpec(memory_space=pltpu.SMEM)
HBM = pl.BlockSpec(memory_space=pltpu.HBM)
ANY = pl.BlockSpec(memory_space=pl.ANY)


def cost(flops, moved):
    return pl.CostEstimate(flops=flops, bytes_accessed=moved, transcendentals=0)


def room(mib):
    return pltpu.CompilerParams(vmem_limit_bytes=int(mib * (1 << 20)))


def shape(dims, dtype):
    return jax.ShapeDtypeStruct(dims, dtype)


def iota(dims, axis):
    return lax.broadcasted_iota(I32, dims, axis)


def scale_rows(scr, key_scales, value_scales):
    scr[...] = jnp.zeros_like(scr)
    scr[0:HELD, 0:KVH] = key_scales[...].astype(F32)
    scr[HELD : 2 * HELD, 0:KVH] = value_scales[...].astype(F32)


def front_kernel(
    dest, slots, keys, values, key_scales, value_scales,
    message, other, plan,
    held, stage, scr, in_sem, out_sem,
):
    here = lax.axis_index("replica")
    x = (lax.axis_index("tensor") // 2) % 2
    loads = []
    for r in range(HELD):
        pair = (
            pltpu.make_async_copy(keys.at[r], held.at[r, 0], in_sem.at[r, 0]),
            pltpu.make_async_copy(values.at[r], held.at[r, 1], in_sem.at[r, 1]),
        )
        for copy in pair:
            copy.start()
        loads.append(pair)
    scale_rows(scr, key_scales, value_scales)
    for r in range(HELD):
        plan[r] = -1
    for j in range(MOVE):
        source = jnp.int32(0)
        for p in range(REPLICAS):
            source = jnp.where(dest[j, p] == here, p, source)
        plan[slots[0, j]] = source
    row = iota((8, HD), 0)
    for pair in loads:
        for copy in pair:
            copy.wait()
    stores = []
    for j in range(MOVE):
        s = slots[0, j]
        both = jnp.where(
            row == 0,
            scr[pl.ds(s, 1), :],
            jnp.where(row == 1, scr[pl.ds(HELD + s, 1), :], 0.0),
        )
        stage[j, 2 * KVH * SPAN : SLOT, :] = both.astype(BF16)
        for which in range(2):
            for c in range(KVH):
                at_row = (which * KVH + c) * SPAN
                stage[j, at_row : at_row + SPAN, :] = held[s, which, :, c * HD : (c + 1) * HD]
        copy = pltpu.make_async_copy(stage.at[j], message.at[dest[j, here]], out_sem.at[j])
        copy.start()
        stores.append(copy)
    for i in range(KVH // 2):
        start = pl.multiple_of((2 * i + 1 - x) * HD, HD)
        for which in range(2):
            for r in range(HELD):
                at_row = (which * HELD + r) * SPAN
                other[at_row : at_row + SPAN, i * HD : (i + 1) * HD] = held[
                    r, which, :, pl.ds(start, HD)
                ]
    other[2 * HELD * SPAN :, 0:HD] = scr[...].astype(BF16)
    other[2 * HELD * SPAN :, HD:] = jnp.zeros((2 * HELD, 3 * HD), BF16)
    for copy in stores:
        copy.wait()


def front(dest, slots, keys, values, key_scales, value_scales):
    return pl.pallas_call(
        front_kernel,
        out_shape=(
            shape((REPLICAS, SLOT, HD), BF16),
            shape((2 * HELD * SPAN + 2 * HELD, KVH // 2 * HD), BF16),
            shape((HELD,), I32),
        ),
        in_specs=[SMEM, SMEM, HBM, HBM, VMEM, VMEM],
        out_specs=(HBM, VMEM, SMEM),
        scratch_shapes=[
            pltpu.VMEM((HELD, 2, SPAN, KVH * HD), BF16),
            pltpu.VMEM((MOVE, SLOT, HD), BF16),
            pltpu.VMEM((2 * HELD, HD), F32),
            pltpu.SemaphoreType.DMA((HELD, 2)),
            pltpu.SemaphoreType.DMA((MOVE,)),
        ],
        cost_estimate=cost(1 << 20, 4 << 20),
        compiler_params=room(FRONT_ROOM),
        name="front",
    )(dest, slots, keys, values, key_scales, value_scales)


def unpack_kernel(
    plan, received, keys, values, key_scales, value_scales,
    new_keys, new_values, new_key_scales, new_value_scales,
    stage, scr, in_sem, out_sem,
):
    def copies(r, inward):
        pairs = ((keys, new_keys), (values, new_values))
        if inward:
            return [
                pltpu.make_async_copy(old.at[r], stage.at[r, i], in_sem.at[r, i])
                for i, (old, _) in enumerate(pairs)
            ]
        return [
            pltpu.make_async_copy(stage.at[r, i], new.at[r], out_sem.at[r, i])
            for i, (_, new) in enumerate(pairs)
        ]

    for r in range(HELD):

        @pl.when(plan[r] < 0)
        def _():
            for copy in copies(r, True):
                copy.start()

    scale_rows(scr, key_scales, value_scales)
    for r in range(HELD):
        source = plan[r]

        @pl.when(source >= 0)
        def _():
            both = received[source, 2 * KVH * SPAN : SLOT, :].astype(F32)
            scr[r : r + 1, :] = both[0:1, :]
            scr[HELD + r : HELD + r + 1, :] = both[1:2, :]
            for which in range(2):
                for c in range(KVH):
                    at_row = (which * KVH + c) * SPAN
                    stage[r, which, :, c * HD : (c + 1) * HD] = received[
                        source, at_row : at_row + SPAN, :
                    ]
            for copy in copies(r, False):
                copy.start()

    for r in range(HELD):

        @pl.when(plan[r] < 0)
        def _():
            for copy in copies(r, True):
                copy.wait()
            for copy in copies(r, False):
                copy.start()

    new_key_scales[...] = scr[0:HELD, 0:KVH].astype(BF16)
    new_value_scales[...] = scr[HELD : 2 * HELD, 0:KVH].astype(BF16)
    for r in range(HELD):
        for copy in copies(r, False):
            copy.wait()


def unpack(plan, received, keys, values, key_scales, value_scales):
    return pl.pallas_call(
        unpack_kernel,
        out_shape=(
            shape(keys.shape, BF16),
            shape(values.shape, BF16),
            shape((HELD, KVH), BF16),
            shape((HELD, KVH), BF16),
        ),
        in_specs=[SMEM, VMEM, HBM, HBM, VMEM, VMEM],
        out_specs=(HBM, HBM, VMEM, VMEM),
        scratch_shapes=[
            pltpu.VMEM((HELD, 2, SPAN, KVH * HD), BF16),
            pltpu.VMEM((2 * HELD, HD), F32),
            pltpu.SemaphoreType.DMA((HELD, 2)),
            pltpu.SemaphoreType.DMA((HELD, 2)),
        ],
        cost_estimate=cost(1 << 20, 4 << 20),
        compiler_params=room(8),
        name="unpack",
    )(plan, received, keys, values, key_scales, value_scales)


def query_kernel(hidden, weight, gain, query, residual, rows, blocks, rows_sem, block_sem):
    rank = lax.axis_index("tensor")
    depth = blocks.shape[1]
    rows_in = pltpu.make_async_copy(hidden, rows, rows_sem)
    rows_in.start()
    weights_in = []
    for i in range(STEPS):
        copy = pltpu.make_async_copy(
            weight.at[i * depth : (i + 1) * depth, :], blocks.at[i], block_sem.at[i]
        )
        copy.start()
        weights_in.append(copy)
    rows_in.wait()
    residual[...] = rows[:, pl.ds(pl.multiple_of(rank * COLS, COLS), COLS)]
    total = jnp.zeros((ROWS, 2 * HD), F32)
    for i in range(STEPS):
        weights_in[i].wait()
        total = total + jnp.dot(
            rows[:, i * depth : (i + 1) * depth], blocks[i], preferred_element_type=F32
        )
    for h in range(2):
        part = total[:, h * HD : (h + 1) * HD]
        mean = jnp.mean(part * part, axis=-1, keepdims=True)
        part = part * lax.rsqrt(mean + EPSILON)
        query[:, h * HD : (h + 1) * HD] = (part * gain[...] * HD ** (-0.5)).astype(BF16)


def project_query(hidden, q_weight, q_gain):
    depth = hidden.shape[1] // STEPS
    return pl.pallas_call(
        query_kernel,
        out_shape=(shape((ROWS, 2 * HD), BF16), shape((ROWS, COLS), BF16)),
        in_specs=[HBM, HBM, VMEM],
        out_specs=(VMEM, VMEM),
        scratch_shapes=[
            pltpu.VMEM(hidden.shape, BF16),
            pltpu.VMEM((STEPS, depth, 2 * HD), BF16),
            pltpu.SemaphoreType.DMA,
            pltpu.SemaphoreType.DMA((STEPS,)),
        ],
        cost_estimate=cost(1 << 22, 5 << 20),
        compiler_params=room(QUERY_ROOM),
        name="query",
    )(hidden, q_weight, q_gain.reshape(1, HD))


def split3(x):
    high = x.astype(BF16).astype(F32)
    rest = x - high
    middle = rest.astype(BF16).astype(F32)
    return high, middle, rest - middle


def put_stats(out, at_row, stats):
    high, middle, low = split3(stats)
    out[at_row : at_row + 16, :] = jnp.concatenate([high, middle], axis=0).astype(BF16)
    out[at_row + 16 : at_row + 32, :] = jnp.concatenate(
        [low, jnp.zeros_like(low)], axis=0
    ).astype(BF16)


def get_stats(message, at_row):
    first = message[at_row : at_row + 16, :].astype(F32)
    second = message[at_row + 16 : at_row + 32, :].astype(F32)
    return (first[0:8] + first[8:16]) + second[0:8]


def columns_of(rows):
    short = HD - rows.shape[0]
    return jnp.concatenate([rows, jnp.zeros((short, HD), F32)], axis=0).T


def attend_kernel(
    lengths, q0, q1, q2, q3, keys, values, key_scales, value_scales, other,
    o0, o1, o2, o3, q_all, o_all, mask, stats,
):
    rank = lax.axis_index("tensor")
    y = rank // 4
    x = (rank // 2) % 2
    for k, q in enumerate((q0, q1, q2, q3)):
        q_all[k] = q[...]
    tokens = HELD * SPAN
    row_request = (iota((HD, tokens), 0) // SPEC) % HELD
    col = iota((HD, tokens), 1)
    limit = jnp.zeros((1, tokens), I32)
    col1 = iota((1, tokens), 1)
    for r in range(HELD):
        limit = jnp.where(col1 // SPAN == r, lengths[r], limit)
    own_request = row_request == col // SPAN
    beside = rank + 2 - 4 * x
    for b, block in enumerate((rank, beside)):
        in_reach = block * SPAN + col1 % SPAN < limit
        mask[b] = jnp.where(jnp.logical_and(own_request, in_reach), 1.0, 0.0)
    spread_cols = (iota((HELD, tokens), 1) // SPAN == iota((HELD, tokens), 0)).astype(BF16)
    spread_rows = ((iota((HD, HELD), 0) // SPEC) % HELD == iota((HD, HELD), 1)).astype(BF16)
    end = 2 * tokens
    scales = (
        (key_scales[...], value_scales[...]),
        (other[end : end + HELD, 0:KVH], other[end + HELD : end + 2 * HELD, 0:KVH]),
    )
    col_scale = [
        lax.dot_general(
            k, spread_cols, (((0,), (0,)), ((), ())), preferred_element_type=F32
        )
        for k, _ in scales
    ]
    row_scale = [jnp.dot(spread_rows, v, preferred_element_type=F32) for _, v in scales]
    lane = iota((HD, HD), 1)
    stats[...] = jnp.zeros_like(stats)
    for i in range(KVH // 2):
        k = (y - i + 4) % 4
        near, far = q_all[k, 0], q_all[k, 1]
        grouped = jnp.concatenate(
            [near[:, :HD], near[:, HD:], far[:, :HD], far[:, HD:]], axis=0
        )
        start = pl.multiple_of((2 * i + x) * HD, HD)
        lanes = slice(i * HD, (i + 1) * HD)
        key = (keys[:, :, pl.ds(start, HD)].reshape(tokens, HD), other[0:tokens, lanes])
        value = (
            values[:, :, pl.ds(start, HD)].reshape(tokens, HD),
            other[tokens : 2 * tokens, lanes],
        )
        scores, peaks = [], []
        for b in range(2):
            across = jnp.where(
                x == 0, col_scale[b][2 * i : 2 * i + 1], col_scale[b][2 * i + 1 : 2 * i + 2]
            )
            score = across * lax.dot_general(
                grouped, key[b], (((1,), (1,)), ((), ())), preferred_element_type=F32
            )
            scores.append(score)
            masked = jnp.where(mask[b] > 0.5, score, NEGATIVE)
            peaks.append(jnp.max(masked, axis=1, keepdims=True))
        peak = jnp.maximum(*peaks)
        total, out = 0.0, 0.0
        for b in range(2):
            weight = jnp.where(mask[b] > 0.5, jnp.exp(scores[b] - peak), 0.0)
            total = total + jnp.sum(weight, axis=1, keepdims=True)
            down = jnp.where(
                x == 0, row_scale[b][:, 2 * i : 2 * i + 1], row_scale[b][:, 2 * i + 1 : 2 * i + 2]
            )
            out = out + down * jnp.dot(
                weight.astype(BF16), value[b], preferred_element_type=F32
            )
        o_all[k] = out.astype(BF16)
        stats[...] = jnp.where(
            lane == 8 * k, peak, jnp.where(lane == 8 * k + 1, total, stats[...])
        )
    turned = stats[...].T
    for k, o in enumerate((o0, o1, o2, o3)):
        o[0:HD, :] = o_all[k]
        put_stats(o, HD, turned[8 * k : 8 * k + 8])


def attend(lengths, queries, keys, values, key_scales, value_scales, other):
    out = shape((HD + 32, HD), BF16)
    return pl.pallas_call(
        attend_kernel,
        out_shape=(out,) * 4,
        in_specs=[SMEM] + [VMEM] * 9,
        out_specs=(VMEM,) * 4,
        scratch_shapes=[
            pltpu.VMEM((4, 2, ROWS, 2 * HD), BF16),
            pltpu.VMEM((4, HD, HD), BF16),
            pltpu.VMEM((2, HD, HELD * SPAN), F32),
            pltpu.VMEM((HD, HD), F32),
        ],
        cost_estimate=cost(4 << 20, 2 << 20),
        compiler_params=room(8),
        name="attend",
    )(lengths, *queries, keys, values, key_scales, value_scales, other)


def merged(stats):
    top = functools.reduce(jnp.maximum, stats)
    factors = [jnp.exp(s - top) for s in stats]
    total = sum(s * pltpu.roll(f, 1, 0) for s, f in zip(stats, factors))
    peak_row = iota(top.shape, 0) % 2 == 0
    return factors, jnp.where(peak_row, top, total)


def combine_kernel(p0, p1, p2, p3, o0, o1):
    parts = (p0, p1, p2, p3)
    factors, both = merged([get_stats(p, HD) for p in parts])
    column = columns_of(jnp.concatenate(factors, axis=0))
    summed = jnp.zeros((HD, HD), F32)
    for k, p in enumerate(parts):
        summed = summed + p[0:HD, :].astype(F32) * column[:, 8 * k : 8 * k + 1]
    for dc, o in enumerate((o0, o1)):
        o[0 : HD // 2, :] = summed[dc * 64 : dc * 64 + 64].astype(BF16)
        put_stats(o, HD // 2, both)


def combine(parts):
    out = shape((HD // 2 + 32, HD), BF16)
    return pl.pallas_call(
        combine_kernel,
        out_shape=(out,) * 2,
        in_specs=[VMEM] * 4,
        out_specs=(VMEM,) * 2,
        cost_estimate=cost(1 << 20, 1 << 19),
        compiler_params=room(4),
        name="combine",
    )(*parts)


def finished(parts):
    stats = []
    for d, p in enumerate(parts):
        s = get_stats(p, HD // 2)
        stats.append(pltpu.roll(s, HD // 2, 1) if d else s)
    factors, both = merged(stats)
    over = pltpu.roll(both, 7, 0)
    column = columns_of(jnp.concatenate([f / over for f in factors], axis=0))
    summed = jnp.zeros((HD // 2, HD), F32)
    for d, p in enumerate(parts):
        summed = summed + p[0 : HD // 2, :].astype(F32) * column[0 : HD // 2, 8 * d : 8 * d + 1]
    return summed.astype(BF16)


def half_in(core, weight, blocks, sem):
    copies = []
    for i in range(TENSORS // 2):
        start = pl.multiple_of((2 * i + core) * COLS, COLS)
        copy = pltpu.make_async_copy(weight.at[:, pl.ds(start, COLS)], blocks.at[i], sem.at[i])
        copy.start()
        copies.append(copy)
    return copies


def half_out(copies, attended, blocks, out):
    for i, copy in enumerate(copies):
        copy.wait()
        out[i] = jnp.dot(attended, blocks[i], preferred_element_type=F32).astype(out.dtype)


def output_other_kernel(p0, p1, weight, attended, out, blocks, sem):
    copies = half_in(1 - lax.axis_index("tensor") % 2, weight, blocks, sem)
    both = finished((p0, p1))
    for h in range(2):
        attended[:, h * HD : (h + 1) * HD] = both[h * ROWS : (h + 1) * ROWS]
    half_out(copies, attended[...], blocks, out)


def output_own_kernel(attended, weight, out, blocks, sem):
    copies = half_in(lax.axis_index("tensor") % 2, weight, blocks, sem)
    half_out(copies, attended[...], blocks, out)


HALF_SCRATCH = [
    pltpu.VMEM((TENSORS // 2, 2 * HD, COLS), BF16),
    pltpu.SemaphoreType.DMA((TENSORS // 2,)),
]


def output_other(parts, o_weight):
    return pl.pallas_call(
        output_other_kernel,
        out_shape=(
            shape((ROWS, 2 * HD), BF16),
            shape((TENSORS // 2, ROWS, COLS), BF16),
        ),
        in_specs=[VMEM] * 2 + [ANY],
        out_specs=(VMEM, VMEM),
        scratch_shapes=HALF_SCRATCH,
        cost_estimate=cost(1 << 22, 2 << 20),
        compiler_params=room(OUTPUT_ROOM),
        name="output_other",
    )(*parts, o_weight)


def output_own(attended, o_weight):
    return pl.pallas_call(
        output_own_kernel,
        out_shape=shape((TENSORS // 2, ROWS, COLS), F32),
        in_specs=[VMEM, ANY],
        out_specs=VMEM,
        scratch_shapes=HALF_SCRATCH,
        cost_estimate=cost(1 << 22, 2 << 20),
        compiler_params=room(OUTPUT_ROOM),
        name="output_own",
    )(attended, o_weight)


def share_kernel(own, received, keep, s1, s2, s3):
    y = lax.axis_index("tensor") // 4
    for k in range(4):
        group = (y - k + 4) % 4
        for c in range(2):
            value = own[2 * group + c] + received[2 * group + c].astype(F32)
            if k == 0:
                keep[c] = value
            else:
                (s1, s2, s3)[k - 1][c] = value.astype(BF16)


def share(own, received):
    out = shape((2, ROWS, COLS), BF16)
    return pl.pallas_call(
        share_kernel,
        out_shape=(shape((2, ROWS, COLS), F32), out, out, out),
        in_specs=[VMEM, VMEM],
        out_specs=(VMEM,) * 4,
        cost_estimate=cost(1 << 20, 1 << 20),
        compiler_params=room(6),
        name="share",
    )(own, received)


def narrow_kernel(own, r1, r2, r3, keep, send):
    x = (lax.axis_index("tensor") // 2) % 2
    for c, out in ((x, keep), (1 - x, send)):
        value = own[c] + r1[c].astype(F32) + r2[c].astype(F32) + r3[c].astype(F32)
        out[...] = value.astype(out.dtype)


def narrow(own, received):
    return pl.pallas_call(
        narrow_kernel,
        out_shape=(shape((ROWS, COLS), F32), shape((ROWS, COLS), BF16)),
        in_specs=[VMEM] * 4,
        out_specs=(VMEM,) * 2,
        cost_estimate=cost(1 << 20, 1 << 19),
        compiler_params=room(4),
        name="narrow",
    )(own, *received)


def mix_kernel(gate, own, received, residual, out):
    scale = jnp.tanh(jnp.full((8, HD), gate[0], F32))[0:1, 0:1]
    summed = own[...] + received[...].astype(F32)
    out[...] = (residual[...].astype(F32) + scale * summed).astype(BF16)


def mix(gate, own, received, residual):
    return pl.pallas_call(
        mix_kernel,
        out_shape=shape((ROWS, COLS), BF16),
        in_specs=[SMEM, VMEM, VMEM, VMEM],
        out_specs=VMEM,
        cost_estimate=cost(1 << 20, 1 << 18),
        compiler_params=room(4),
        name="mix",
    )(gate, own, received, residual)


def swap(array, bits):
    return lax.ppermute(array, "tensor", [(i, i ^ bits) for i in range(TENSORS)])


def shift(array, rows):
    return lax.ppermute(array, "tensor", [(i, (i + 4 * rows) % TENSORS) for i in range(TENSORS)])


def attention(
    hidden, q_weight, q_gain, o_weight, attn_gate,
    keys, values, key_scales, value_scales, other, lengths,
):
    query, residual = project_query(hidden, q_weight, q_gain)
    local = jnp.stack([query, swap(query, 1)])
    queries = [local] + [shift(local, k) for k in (1, 2, 3)]
    parts = attend(lengths, queries, keys, values, key_scales, value_scales, other)
    parts = combine([parts[0]] + [shift(parts[k], -k) for k in (1, 2, 3)])
    attended, sent = output_other([parts[0], swap(parts[1], 1)], o_weight)
    sent = swap(sent, 1)
    own, *sent = share(output_own(attended, o_weight), sent)
    own, sent = narrow(own, [shift(s, -k) for k, s in zip((1, 2, 3), sent)])
    return mix(attn_gate, own, swap(sent, 2), residual)


def local(
    hidden,
    q_weight,
    q_gain,
    o_weight,
    attn_gate,
    key_codes,
    value_codes,
    key_scales,
    value_scales,
    lengths,
    dest_replica,
    move_slot,
):
    dest = dest_replica.T
    key_scales, value_scales = key_scales[:, 0, :], value_scales[:, 0, :]
    message, other, plan = front(dest, move_slot, key_codes, value_codes, key_scales, value_scales)
    other = swap(other, 2)
    received = lax.all_to_all(
        message, "replica", split_axis=0, concat_axis=0, tiled=True
    )
    mixed = attention(
        hidden, q_weight, q_gain, o_weight, attn_gate,
        key_codes, value_codes, key_scales, value_scales, other, lengths,
    )
    new_keys, new_values, new_ks, new_vs = unpack(
        plan, received, key_codes, value_codes, key_scales, value_scales
    )
    return (mixed, new_keys, new_values, new_ks[:, None, :], new_vs[:, None, :])


def solution(mesh):
    return jax.shard_map(
        local,
        mesh=mesh,
        in_specs=(
            P("replica", None),
            P(None, "tensor"),
            P(),
            P("tensor", None),
            P(),
            P("replica", "tensor", None),
            P("replica", "tensor", None),
            P("replica", "tensor", None),
            P("replica", "tensor", None),
            P("replica"),
            P(),
            P("replica", None),
        ),
        out_specs=(
            P("replica", "tensor"),
            P("replica", "tensor", None),
            P("replica", "tensor", None),
            P("replica", "tensor", None),
            P("replica", "tensor", None),
        ),
        check_vma=False,
    )
```

time: 79.5 us -> 73.8 us (0.928)
  the two profiles are of different devices: /device:TPU:96 before, /device:TPU:68 now
where the time goes in v3:
time: 73.8 us; the launch traced here: 73.4 us
  waiting for transfers between devices  27.1 us (37%)
  starting transfers between devices  26.9 us (36%)
  Pallas kernels  18 us (24%)
  between operations  1.44 us (2%)
    ppermute x5, waiting for transfers between devices, swap(): lax.ppermute(array, 'tensor', [(i, i ^ bits) for i in range(TENSORS)])  15.5 us
    ppermute x9, starting transfers between devices, shift(): lax.ppermute(array, 'tensor', [(i, (i + 4 * rows) % TENSORS) for i in ran...  13.6 us
    ppermute x9, waiting for transfers between devices, shift(): lax.ppermute(array, 'tensor', [(i, (i + 4 * rows) % TENSORS) for i in ran...  11.6 us
    all_to_all x1, starting transfers between devices, local(): lax.all_to_all(message, 'replica', split_axis=0, concat_axis=0, tiled=True)  10.7 us
    pallas_call x1, Pallas kernels, front(): pl.pallas_call(front_kernel, out_shape=(shape((REPLICAS, SLOT, HD), BF16)...  4.06 us
    pallas_call x1, Pallas kernels, project_query(): pl.pallas_call(query_kernel, out_shape=(shape((ROWS, 2 * HD), BF16), shap...  3.7 us
    pallas_call x1, Pallas kernels, unpack(): pl.pallas_call(unpack_kernel, out_shape=(shape(keys.shape, BF16), shape(v...  2.8 us
    ppermute x5, starting transfers between devices, swap(): lax.ppermute(array, 'tensor', [(i, i ^ bits) for i in range(TENSORS)])  2.55 us
  transfers between devices with their start and end apart: 15, of which 12 were waited for; matrix products, arithmetic and copies ran while one was open for 0% of the time, Pallas kernels for 15%

profile of v3, /device:TPU:68, one launch (start us, length us, event | category | flops | bytes accessed | tf_op | source)
XLA Modules:
  0.0 73.4 jit_solution(11226943061930302955)
XLA Ops:
  0.6 4.1 %front.1 = (bf16[16,520,128]{2,1,0:T(8,128)(2,1)}, bf16[528,512]{1,0:T(8,128)(2,1)}, s32[8]{0:T(128)}) custom-call(s32[6,16]{1,0:T(8,128)} %bitcast.17, s32[1,6]{1,0:T(1,128)} %slots.1, bf16[8,32,1024]{2,1,0:T(8,128)(2,1)} %keys.5, bf16[8,32,1024]{2,1,0:T(8,128)(2,1)} %values.5, bf16[8,8]{1,0:T(8,128)(2,1)} %bitcast.8, bf16[8,8]{1,0:T(8,128)(2,1)} %bitcast.11), custom_call_target="tpu_custom_call" | custom-call | flops 1048576 | bytes 4194304 | tf_op jit(solution)/shard_map/front/pallas_call | solution.py:116
  4.8 10.7 %all-to-all-start = ((bf16[16,520,128]{2,1,0:T(8,128)(2,1)}), bf16[16,520,128]{2,1,0:T(8,128)(2,1)S(1)}, u32[]{:S(2)}, u32[]{:S(2)}) async-start(bf16[16,520,128]{2,1,0:T(8,128)(2,1)} %get-tuple-element.46), calls=%async_computation | async-start | bytes 4259840 | tf_op jit(solution)/shard_map/all_to_all | solution.py:607
  15.5 1.2 %collective-permute-start.4 = (bf16[528,512]{1,0:T(8,128)(2,1)}, bf16[528,512]{1,0:T(8,128)(2,1)S(1)}, u32[]{:S(2)}, u32[]{:S(2)}) collective-permute-start(bf16[528,512]{1,0:T(8,128)(2,1)} %get-tuple-element.29), channel_id=1, source_target_pairs={{0,2},{1,3},{2,0},{3,1},{4,6},{5,7},{6,4},{7,5},{8,10},{9,11},{10,... | collective-permute-start | bytes 1622024 | tf_op jit(solution)/shard_map/ppermute | solution.py:566
  16.7 3.7 %query.1 = (bf16[32,256]{1,0:T(8,128)(2,1)S(1)}, bf16[32,512]{1,0:T(8,128)(2,1)S(1)}) custom-call(bf16[32,8192]{1,0:T(8,128)(2,1)} %hidden.1, bf16[8192,256]{1,0:T(8,128)(2,1)} %weight.3, f32[1,128]{1,0:T(1,128)S(1)} %bitcast.15), custom_call_target="tpu_custom_call" | custom-call | flops 4194304 | bytes 5242880 | tf_op jit(solution)/shard_map/query/pallas_call | solution.py:248
  20.5 1.2 %collective-permute-done = bf16[32,256]{1,0:T(8,128)(2,1)S(1)} collective-permute-done((bf16[32,256]{1,0:T(8,128)(2,1)S(1)}, bf16[32,256]{1,0:T(8,128)(2,1)S(1)}, u32[]{:S(2)}, u32[]{:S(2)}) %collective-permute-start) | collective-permute-done | bytes 16416 | tf_op jit(solution)/shard_map/ppermute | solution.py:566
  21.7 1.6 %collective-permute-start.1 = (bf16[2,32,256]{2,1,0:T(8,128)(2,1)S(1)}, bf16[2,32,256]{2,1,0:T(8,128)(2,1)S(1)}, u32[]{:S(2)}, u32[]{:S(2)}) collective-permute-start(bf16[2,32,256]{2,1,0:T(8,128)(2,1)S(1)} %pad_maximum_fusion.q0), channel_id=1, source_target_pairs={{0,4},{1,5},{2,6},{3,7},{4,8},{5,9},{6,10},{7,11},{8,12},{9,13},{1... | collective-permute-start | bytes 98312 | tf_op jit(solution)/shard_map/ppermute | solution.py:570
  23.2 2.9 %collective-permute-start.2 = (bf16[2,32,256]{2,1,0:T(8,128)(2,1)S(1)}, bf16[2,32,256]{2,1,0:T(8,128)(2,1)S(1)}, u32[]{:S(2)}, u32[]{:S(2)}) collective-permute-start(bf16[2,32,256]{2,1,0:T(8,128)(2,1)S(1)} %pad_maximum_fusion.q0), channel_id=1, source_target_pairs={{0,8},{1,9},{2,10},{3,11},{4,12},{5,13},{6,14},{7,15},{8,0},{9,1},... | collective-permute-start | bytes 98312 | tf_op jit(solution)/shard_map/ppermute | solution.py:570
  26.1 1.3 %collective-permute-start.3 = (bf16[2,32,256]{2,1,0:T(8,128)(2,1)S(1)}, bf16[2,32,256]{2,1,0:T(8,128)(2,1)S(1)}, u32[]{:S(2)}, u32[]{:S(2)}) collective-permute-start(bf16[2,32,256]{2,1,0:T(8,128)(2,1)S(1)} %pad_maximum_fusion.q0), channel_id=1, source_target_pairs={{0,12},{1,13},{2,14},{3,15},{4,0},{5,1},{6,2},{7,3},{8,4},{9,5},{1... | collective-permute-start | bytes 98312 | tf_op jit(solution)/shard_map/ppermute | solution.py:570
  27.5 1.2 %collective-permute-done.2.q2 = bf16[2,32,256]{2,1,0:T(8,128)(2,1)S(1)} collective-permute-done((bf16[2,32,256]{2,1,0:T(8,128)(2,1)S(1)}, bf16[2,32,256]{2,1,0:T(8,128)(2,1)S(1)}, u32[]{:S(2)}, u32[]{:S(2)}) %collective-permute-start.2) | collective-permute-done | bytes 32800 | tf_op jit(solution)/shard_map/ppermute | solution.py:570
  28.7 1.4 %collective-permute-done.3.q3 = bf16[2,32,256]{2,1,0:T(8,128)(2,1)S(1)} collective-permute-done((bf16[2,32,256]{2,1,0:T(8,128)(2,1)S(1)}, bf16[2,32,256]{2,1,0:T(8,128)(2,1)S(1)}, u32[]{:S(2)}, u32[]{:S(2)}) %collective-permute-start.3) | collective-permute-done | bytes 32800 | tf_op jit(solution)/shard_map/ppermute | solution.py:570
  30.1 10.8 %collective-permute-done.4.other = bf16[528,512]{1,0:T(8,128)(2,1)S(1)} collective-permute-done((bf16[528,512]{1,0:T(8,128)(2,1)}, bf16[528,512]{1,0:T(8,128)(2,1)S(1)}, u32[]{:S(2)}, u32[]{:S(2)}) %collective-permute-start.4) | collective-permute-done | bytes 540704 | tf_op jit(solution)/shard_map/ppermute | solution.py:566
  40.8 1.9 %attend.1 = (bf16[160,128]{1,0:T(8,128)(2,1)S(1)}, bf16[160,128]{1,0:T(8,128)(2,1)S(1)}, bf16[160,128]{1,0:T(8,128)(2,1)S(1)}, bf16[160,128]{1,0:T(8,128)(2,1)S(1)}) custom-call(s32[8]{0:T(128)S(1)} %copy-done.4, bf16[2,32,256]{2,1,0:T(8,128)(2,1)S(1)} %pad_maximum_fusion.q0, bf16[2,32,256]{2,1,0:T(8,128)(2,1)S(1)} %collective-permute-done.1.q1, ...), custom_call_target="tpu_custom_call" | custom-call | flops 4194304 | bytes 2097152 | tf_op jit(solution)/shard_map/attend/pallas_call | solution.py:375
  42.8 3.1 %collective-permute-start.5 = (bf16[160,128]{1,0:T(8,128)(2,1)S(1)}, bf16[160,128]{1,0:T(8,128)(2,1)S(1)}, u32[]{:S(2)}, u32[]{:S(2)}) collective-permute-start(bf16[160,128]{1,0:T(8,128)(2,1)S(1)} %get-tuple-element.31), channel_id=1, source_target_pairs={{0,12},{1,13},{2,14},{3,15},{4,0},{5,1},{6,2},{7,3},{8,4},{9,5},{1... | collective-permute-start | bytes 122888 | tf_op jit(solution)/shard_map/ppermute | solution.py:570
  47.5 3.8 %collective-permute-done.6.p2 = bf16[160,128]{1,0:T(8,128)(2,1)S(1)} collective-permute-done((bf16[160,128]{1,0:T(8,128)(2,1)S(1)}, bf16[160,128]{1,0:T(8,128)(2,1)S(1)}, u32[]{:S(2)}, u32[]{:S(2)}) %collective-permute-start.6) | collective-permute-done | bytes 40992 | tf_op jit(solution)/shard_map/ppermute | solution.py:570
  52.2 1.2 %collective-permute-done.8.p1 = bf16[96,128]{1,0:T(8,128)(2,1)S(1)} collective-permute-done((bf16[96,128]{1,0:T(8,128)(2,1)S(1)}, bf16[96,128]{1,0:T(8,128)(2,1)S(1)}, u32[]{:S(2)}, u32[]{:S(2)}) %collective-permute-start.8) | collective-permute-done | bytes 24608 | tf_op jit(solution)/shard_map/ppermute | solution.py:566
  53.3 2.3 %output_other.1 = (bf16[32,256]{1,0:T(8,128)(2,1)S(1)}, bf16[8,32,512]{2,1,0:T(8,128)(2,1)S(1)}) custom-call(bf16[96,128]{1,0:T(8,128)(2,1)S(1)} %get-tuple-element.34.p0, bf16[96,128]{1,0:T(8,128)(2,1)S(1)} %collective-permute-done.8.p1, bf16[256,8192]{1,0:T(8,128)(2,1)} %weight.5), custom_call_target="tpu_custom_call" | custom-call | flops 4194304 | bytes 2097152 | tf_op jit(solution)/shard_map/output_other/pallas_call | solution.py:475
  55.9 2.3 %output_own.1.own = f32[8,32,512]{2,1,0:T(8,128)S(1)} custom-call(bf16[32,256]{1,0:T(8,128)(2,1)S(1)} %get-tuple-element.36.attended, bf16[256,8192]{1,0:T(8,128)(2,1)} %weight.5), custom_call_target="tpu_custom_call" | custom-call | flops 4194304 | bytes 2097152 | tf_op jit(solution)/shard_map/output_own/pallas_call | solution.py:491
  58.9 1.2 %collective-permute-start.11 = (bf16[2,32,512]{2,1,0:T(8,128)(2,1)S(1)}, bf16[2,32,512]{2,1,0:T(8,128)(2,1)S(1)}, u32[]{:S(2)}, u32[]{:S(2)}) collective-permute-start(bf16[2,32,512]{2,1,0:T(8,128)(2,1)S(1)} %get-tuple-element.40), channel_id=1, source_target_pairs={{0,8},{1,9},{2,10},{3,11},{4,12},{5,13},{6,14},{7,15},{8,0},{9,1},... | collective-permute-start | bytes 196616 | tf_op jit(solution)/shard_map/ppermute | solution.py:570
  60.0 1.3 %collective-permute-start.12 = (bf16[2,32,512]{2,1,0:T(8,128)(2,1)S(1)}, bf16[2,32,512]{2,1,0:T(8,128)(2,1)S(1)}, u32[]{:S(2)}, u32[]{:S(2)}) collective-permute-start(bf16[2,32,512]{2,1,0:T(8,128)(2,1)S(1)} %get-tuple-element.41), channel_id=1, source_target_pairs={{0,4},{1,5},{2,6},{3,7},{4,8},{5,9},{6,10},{7,11},{8,12},{9,13},{1... | collective-permute-start | bytes 196616 | tf_op jit(solution)/shard_map/ppermute | solution.py:570
  61.3 2.0 %collective-permute-done.10.r1 = bf16[2,32,512]{2,1,0:T(8,128)(2,1)S(1)} collective-permute-done((bf16[2,32,512]{2,1,0:T(8,128)(2,1)S(1)}, bf16[2,32,512]{2,1,0:T(8,128)(2,1)S(1)}, u32[]{:S(2)}, u32[]{:S(2)}) %collective-permute-start.10) | collective-permute-done | bytes 65568 | tf_op jit(solution)/shard_map/ppermute | solution.py:570
  63.3 1.5 %collective-permute-done.11.r2 = bf16[2,32,512]{2,1,0:T(8,128)(2,1)S(1)} collective-permute-done((bf16[2,32,512]{2,1,0:T(8,128)(2,1)S(1)}, bf16[2,32,512]{2,1,0:T(8,128)(2,1)S(1)}, u32[]{:S(2)}, u32[]{:S(2)}) %collective-permute-start.11) | collective-permute-done | bytes 65568 | tf_op jit(solution)/shard_map/ppermute | solution.py:570
  64.7 1.2 %collective-permute-done.12.r3 = bf16[2,32,512]{2,1,0:T(8,128)(2,1)S(1)} collective-permute-done((bf16[2,32,512]{2,1,0:T(8,128)(2,1)S(1)}, bf16[2,32,512]{2,1,0:T(8,128)(2,1)S(1)}, u32[]{:S(2)}, u32[]{:S(2)}) %collective-permute-start.12) | collective-permute-done | bytes 65568 | tf_op jit(solution)/shard_map/ppermute | solution.py:570
  67.6 2.4 %collective-permute-done.13.received = bf16[32,512]{1,0:T(8,128)(2,1)S(1)} collective-permute-done((bf16[32,512]{1,0:T(8,128)(2,1)S(1)}, bf16[32,512]{1,0:T(8,128)(2,1)S(1)}, u32[]{:S(2)}, u32[]{:S(2)}) %collective-permute-start.13) | collective-permute-done | bytes 32800 | tf_op jit(solution)/shard_map/ppermute | solution.py:566
  70.6 2.8 %unpack.1 = (bf16[8,32,1024]{2,1,0:T(8,128)(2,1)}, bf16[8,32,1024]{2,1,0:T(8,128)(2,1)}, bf16[8,8]{1,0:T(8,128)(2,1)}, bf16[8,8]{1,0:T(8,128)(2,1)}) custom-call(s32[8]{0:T(128)S(1)} %copy-done.6, bf16[16,520,128]{2,1,0:T(8,128)(2,1)S(1)} %all-to-all-done.received, bf16[8,32,1024]{2,1,0:T(8,128)(2,1)S(1)} %copy-done, bf16[8,32,1024]{2,1,0:T(8,128)(2,1)S(1)} %copy-done.1, ...), custom_call_target="tpu_custom_call" | custom-call | flops 1048576 | bytes 4194304 | tf_op jit(solution)/shard_map/unpack/pallas_call | solution.py:197
  (31 shorter events, 5.1 us)
Async XLA Ops:
  0.6 16.0 %copy-start.5 = (f32[128]{0:T(128)S(1)}, f32[128]{0:T(128)}, u32[]{:S(2)}) copy-start(f32[128]{0:T(128)} %param.14) | copy-start | bytes 1540
  4.7 36.1 %copy-start = (bf16[8,32,1024]{2,1,0:T(8,128)(2,1)S(1)}, bf16[8,32,1024]{2,1,0:T(8,128)(2,1)}, u32[]{:S(2)}) copy-start(bf16[8,32,1024]{2,1,0:T(8,128)(2,1)} %keys.5) | copy-start | bytes 1572868
  4.7 36.1 %copy-start.1 = (bf16[8,32,1024]{2,1,0:T(8,128)(2,1)S(1)}, bf16[8,32,1024]{2,1,0:T(8,128)(2,1)}, u32[]{:S(2)}) copy-start(bf16[8,32,1024]{2,1,0:T(8,128)(2,1)} %values.5) | copy-start | bytes 1572868
  4.7 36.1 %copy-start.2 = (bf16[8,1,8]{2,0,1:T(8,128)(2,1)S(1)}, bf16[8,1,8]{2,0,1:T(8,128)(2,1)}, u32[]{:S(2)}) copy-start(bf16[8,1,8]{2,0,1:T(8,128)(2,1)} %param.19) | copy-start | bytes 388
  4.7 36.1 %copy-start.3 = (bf16[8,1,8]{2,0,1:T(8,128)(2,1)S(1)}, bf16[8,1,8]{2,0,1:T(8,128)(2,1)}, u32[]{:S(2)}) copy-start(bf16[8,1,8]{2,0,1:T(8,128)(2,1)} %param.20) | copy-start | bytes 388
  4.8 36.1 %copy-start.4 = (s32[8]{0:T(128)S(1)}, s32[8]{0:T(128)}, u32[]{:S(2)}) copy-start(s32[8]{0:T(128)} %lengths.1) | copy-start | bytes 100
  4.8 65.9 %all-to-all-start = ((bf16[16,520,128]{2,1,0:T(8,128)(2,1)}), bf16[16,520,128]{2,1,0:T(8,128)(2,1)S(1)}, u32[]{:S(2)}, u32[]{:S(2)}) async-start(bf16[16,520,128]{2,1,0:T(8,128)(2,1)} %get-tuple-element.46), calls=%async_computation | async-start | bytes 4259840 | tf_op jit(solution)/shard_map/all_to_all | solution.py:607
  15.5 25.3 %collective-permute-start.4 = (bf16[528,512]{1,0:T(8,128)(2,1)}, bf16[528,512]{1,0:T(8,128)(2,1)S(1)}, u32[]{:S(2)}, u32[]{:S(2)}) collective-permute-start(bf16[528,512]{1,0:T(8,128)(2,1)} %get-tuple-element.29), channel_id=1, source_target_pairs={{0,2},{1,3},{2,0},{3,1},{4,6},{5,7},{6,4},{7,5},{8,10},{9,11},{10,... | collective-permute-start | bytes 1622024 | tf_op jit(solution)/shard_map/ppermute | solution.py:566
  20.4 1.3 %collective-permute-start = (bf16[32,256]{1,0:T(8,128)(2,1)S(1)}, bf16[32,256]{1,0:T(8,128)(2,1)S(1)}, u32[]{:S(2)}, u32[]{:S(2)}) collective-permute-start(bf16[32,256]{1,0:T(8,128)(2,1)S(1)} %get-tuple-element.28), channel_id=1, source_target_pairs={{0,1},{1,0},{2,3},{3,2},{4,5},{5,4},{6,7},{7,6},{8,9},{9,8},{10,11... | collective-permute-start | bytes 49160 | tf_op jit(solution)/shard_map/ppermute | solution.py:566
  21.7 5.8 %collective-permute-start.1 = (bf16[2,32,256]{2,1,0:T(8,128)(2,1)S(1)}, bf16[2,32,256]{2,1,0:T(8,128)(2,1)S(1)}, u32[]{:S(2)}, u32[]{:S(2)}) collective-permute-start(bf16[2,32,256]{2,1,0:T(8,128)(2,1)S(1)} %pad_maximum_fusion.q0), channel_id=1, source_target_pairs={{0,4},{1,5},{2,6},{3,7},{4,8},{5,9},{6,10},{7,11},{8,12},{9,13},{1... | collective-permute-start | bytes 98312 | tf_op jit(solution)/shard_map/ppermute | solution.py:570
  23.2 5.4 %collective-permute-start.2 = (bf16[2,32,256]{2,1,0:T(8,128)(2,1)S(1)}, bf16[2,32,256]{2,1,0:T(8,128)(2,1)S(1)}, u32[]{:S(2)}, u32[]{:S(2)}) collective-permute-start(bf16[2,32,256]{2,1,0:T(8,128)(2,1)S(1)} %pad_maximum_fusion.q0), channel_id=1, source_target_pairs={{0,8},{1,9},{2,10},{3,11},{4,12},{5,13},{6,14},{7,15},{8,0},{9,1},... | collective-permute-start | bytes 98312 | tf_op jit(solution)/shard_map/ppermute | solution.py:570
  26.1 3.9 %collective-permute-start.3 = (bf16[2,32,256]{2,1,0:T(8,128)(2,1)S(1)}, bf16[2,32,256]{2,1,0:T(8,128)(2,1)S(1)}, u32[]{:S(2)}, u32[]{:S(2)}) collective-permute-start(bf16[2,32,256]{2,1,0:T(8,128)(2,1)S(1)} %pad_maximum_fusion.q0), channel_id=1, source_target_pairs={{0,12},{1,13},{2,14},{3,15},{4,0},{5,1},{6,2},{7,3},{8,4},{9,5},{1... | collective-permute-start | bytes 98312 | tf_op jit(solution)/shard_map/ppermute | solution.py:570
  42.8 4.8 %collective-permute-start.5 = (bf16[160,128]{1,0:T(8,128)(2,1)S(1)}, bf16[160,128]{1,0:T(8,128)(2,1)S(1)}, u32[]{:S(2)}, u32[]{:S(2)}) collective-permute-start(bf16[160,128]{1,0:T(8,128)(2,1)S(1)} %get-tuple-element.31), channel_id=1, source_target_pairs={{0,12},{1,13},{2,14},{3,15},{4,0},{5,1},{6,2},{7,3},{8,4},{9,5},{1... | collective-permute-start | bytes 122888 | tf_op jit(solution)/shard_map/ppermute | solution.py:570
  45.8 5.5 %collective-permute-start.6 = (bf16[160,128]{1,0:T(8,128)(2,1)S(1)}, bf16[160,128]{1,0:T(8,128)(2,1)S(1)}, u32[]{:S(2)}, u32[]{:S(2)}) collective-permute-start(bf16[160,128]{1,0:T(8,128)(2,1)S(1)} %get-tuple-element.32), channel_id=1, source_target_pairs={{0,8},{1,9},{2,10},{3,11},{4,12},{5,13},{6,14},{7,15},{8,0},{9,1},... | collective-permute-start | bytes 122888 | tf_op jit(solution)/shard_map/ppermute | solution.py:570
  46.5 5.3 %collective-permute-start.7 = (bf16[160,128]{1,0:T(8,128)(2,1)S(1)}, bf16[160,128]{1,0:T(8,128)(2,1)S(1)}, u32[]{:S(2)}, u32[]{:S(2)}) collective-permute-start(bf16[160,128]{1,0:T(8,128)(2,1)S(1)} %get-tuple-element.33), channel_id=1, source_target_pairs={{0,4},{1,5},{2,6},{3,7},{4,8},{5,9},{6,10},{7,11},{8,12},{9,13},{1... | collective-permute-start | bytes 122888 | tf_op jit(solution)/shard_map/ppermute | solution.py:570
  52.1 1.3 %collective-permute-start.8 = (bf16[96,128]{1,0:T(8,128)(2,1)S(1)}, bf16[96,128]{1,0:T(8,128)(2,1)S(1)}, u32[]{:S(2)}, u32[]{:S(2)}) collective-permute-start(bf16[96,128]{1,0:T(8,128)(2,1)S(1)} %get-tuple-element.35), channel_id=1, source_target_pairs={{0,1},{1,0},{2,3},{3,2},{4,5},{5,4},{6,7},{7,6},{8,9},{9,8},{10,11... | collective-permute-start | bytes 73736 | tf_op jit(solution)/shard_map/ppermute | solution.py:566
  53.3 17.3 %copy-start.6 = (s32[8]{0:T(128)S(1)}, s32[8]{0:T(128)}, u32[]{:S(2)}) copy-start(s32[8]{0:T(128)} %get-tuple-element.45.plan) | copy-start | bytes 100
  55.6 2.5 %collective-permute-start.9 = (bf16[8,32,512]{2,1,0:T(8,128)(2,1)S(1)}, bf16[8,32,512]{2,1,0:T(8,128)(2,1)S(1)}, u32[]{:S(2)}, u32[]{:S(2)}) collective-permute-start(bf16[8,32,512]{2,1,0:T(8,128)(2,1)S(1)} %get-tuple-element.37), channel_id=1, source_target_pairs={{0,1},{1,0},{2,3},{3,2},{4,5},{5,4},{6,7},{7,6},{8,9},{9,8},{10,11... | collective-permute-start | bytes 786440 | tf_op jit(solution)/shard_map/ppermute | solution.py:566
  58.2 5.0 %collective-permute-start.10 = (bf16[2,32,512]{2,1,0:T(8,128)(2,1)S(1)}, bf16[2,32,512]{2,1,0:T(8,128)(2,1)S(1)}, u32[]{:S(2)}, u32[]{:S(2)}) collective-permute-start(bf16[2,32,512]{2,1,0:T(8,128)(2,1)S(1)} %get-tuple-element.39), channel_id=1, source_target_pairs={{0,12},{1,13},{2,14},{3,15},{4,0},{5,1},{6,2},{7,3},{8,4},{9,5},{1... | collective-permute-start | bytes 196616 | tf_op jit(solution)/shard_map/ppermute | solution.py:570
  58.9 5.9 %collective-permute-start.11 = (bf16[2,32,512]{2,1,0:T(8,128)(2,1)S(1)}, bf16[2,32,512]{2,1,0:T(8,128)(2,1)S(1)}, u32[]{:S(2)}, u32[]{:S(2)}) collective-permute-start(bf16[2,32,512]{2,1,0:T(8,128)(2,1)S(1)} %get-tuple-element.40), channel_id=1, source_target_pairs={{0,8},{1,9},{2,10},{3,11},{4,12},{5,13},{6,14},{7,15},{8,0},{9,1},... | collective-permute-start | bytes 196616 | tf_op jit(solution)/shard_map/ppermute | solution.py:570
  60.0 5.9 %collective-permute-start.12 = (bf16[2,32,512]{2,1,0:T(8,128)(2,1)S(1)}, bf16[2,32,512]{2,1,0:T(8,128)(2,1)S(1)}, u32[]{:S(2)}, u32[]{:S(2)}) collective-permute-start(bf16[2,32,512]{2,1,0:T(8,128)(2,1)S(1)} %get-tuple-element.41), channel_id=1, source_target_pairs={{0,4},{1,5},{2,6},{3,7},{4,8},{5,9},{6,10},{7,11},{8,12},{9,13},{1... | collective-permute-start | bytes 196616 | tf_op jit(solution)/shard_map/ppermute | solution.py:570
  66.0 4.0 %collective-permute-start.13 = (bf16[32,512]{1,0:T(8,128)(2,1)S(1)}, bf16[32,512]{1,0:T(8,128)(2,1)S(1)}, u32[]{:S(2)}, u32[]{:S(2)}) collective-permute-start(bf16[32,512]{1,0:T(8,128)(2,1)S(1)} %get-tuple-element.43), channel_id=1, source_target_pairs={{0,2},{1,3},{2,0},{3,1},{4,6},{5,7},{6,4},{7,5},{8,10},{9,11},{10,... | collective-permute-start | bytes 98312 | tf_op jit(solution)/shard_map/ppermute | solution.py:566

commit v4 on v3

--- a/solution.py
+++ b/solution.py
@@ -55,22 +55,38 @@
 
 
 def front_kernel(
-    dest, slots, keys, values, key_scales, value_scales,
-    message, other, plan,
-    held, stage, scr, in_sem, out_sem,
+    dest_in, slots_in, keys, values, key_scales_in, value_scales_in,
+    message, other_out, plan_out,
+    dest, slots, plan, scales, held, stage, other, scr,
+    small_sem, in_sem, out_sem, end_sem,
 ):
     here = lax.axis_index("replica")
     x = (lax.axis_index("tensor") // 2) % 2
-    loads = []
-    for r in range(HELD):
-        pair = (
+    small = [
+        pltpu.make_async_copy(source, target, small_sem.at[i])
+        for i, (source, target) in enumerate(
+            (
+                (slots_in, slots),
+                (dest_in, dest),
+                (key_scales_in, scales.at[0]),
+                (value_scales_in, scales.at[1]),
+            )
+        )
+    ]
+    for copy in small:
+        copy.start()
+
+    def loads(r):
+        return (
             pltpu.make_async_copy(keys.at[r], held.at[r, 0], in_sem.at[r, 0]),
             pltpu.make_async_copy(values.at[r], held.at[r, 1], in_sem.at[r, 1]),
         )
-        for copy in pair:
+
+    for r in range(HELD):
+        for copy in loads(r):
             copy.start()
-        loads.append(pair)
-    scale_rows(scr, key_scales, value_scales)
+    for copy in small:
+        copy.wait()
     for r in range(HELD):
         plan[r] = -1
     for j in range(MOVE):
@@ -78,9 +94,12 @@
         for p in range(REPLICAS):
             source = jnp.where(dest[j, p] == here, p, source)
         plan[slots[0, j]] = source
+    plan_copy = pltpu.make_async_copy(plan, plan_out, end_sem.at[0])
+    plan_copy.start()
+    scale_rows(scr, scales.at[0], scales.at[1])
     row = iota((8, HD), 0)
-    for pair in loads:
-        for copy in pair:
+    for r in range(HELD):
+        for copy in loads(r):
             copy.wait()
     stores = []
     for j in range(MOVE):
@@ -108,26 +127,38 @@
                 ]
     other[2 * HELD * SPAN :, 0:HD] = scr[...].astype(BF16)
     other[2 * HELD * SPAN :, HD:] = jnp.zeros((2 * HELD, 3 * HD), BF16)
+    other_copy = pltpu.make_async_copy(other, other_out, end_sem.at[1])
+    other_copy.start()
     for copy in stores:
         copy.wait()
+    plan_copy.wait()
+    other_copy.wait()
 
 
 def front(dest, slots, keys, values, key_scales, value_scales):
+    other = (2 * HELD * SPAN + 2 * HELD, KVH // 2 * HD)
     return pl.pallas_call(
         front_kernel,
         out_shape=(
             shape((REPLICAS, SLOT, HD), BF16),
-            shape((2 * HELD * SPAN + 2 * HELD, KVH // 2 * HD), BF16),
+            shape(other, BF16),
             shape((HELD,), I32),
         ),
-        in_specs=[SMEM, SMEM, HBM, HBM, VMEM, VMEM],
-        out_specs=(HBM, VMEM, SMEM),
+        in_specs=[HBM] * 6,
+        out_specs=(HBM, HBM, HBM),
         scratch_shapes=[
+            pltpu.SMEM(dest.shape, I32),
+            pltpu.SMEM(slots.shape, I32),
+            pltpu.SMEM((HELD,), I32),
+            pltpu.VMEM((2, HELD, KVH), BF16),
             pltpu.VMEM((HELD, 2, SPAN, KVH * HD), BF16),
             pltpu.VMEM((MOVE, SLOT, HD), BF16),
+            pltpu.VMEM(other, BF16),
             pltpu.VMEM((2 * HELD, HD), F32),
+            pltpu.SemaphoreType.DMA((4,)),
             pltpu.SemaphoreType.DMA((HELD, 2)),
             pltpu.SemaphoreType.DMA((MOVE,)),
+            pltpu.SemaphoreType.DMA((2,)),
         ],
         cost_estimate=cost(1 << 20, 4 << 20),
         compiler_params=room(FRONT_ROOM),
@@ -138,7 +169,7 @@
 def unpack_kernel(
     plan, received, keys, values, key_scales, value_scales,
     new_keys, new_values, new_key_scales, new_value_scales,
-    stage, scr, in_sem, out_sem,
+    stage, scr, thin, in_sem, out_sem, thin_sem,
 ):
     def copies(r, inward):
         pairs = ((keys, new_keys), (values, new_values))
@@ -177,6 +208,14 @@
             for copy in copies(r, False):
                 copy.start()
 
+    thin[0] = scr[0:HELD, 0:KVH].astype(BF16)
+    thin[1] = scr[HELD : 2 * HELD, 0:KVH].astype(BF16)
+    scales_out = [
+        pltpu.make_async_copy(thin.at[i], new, thin_sem.at[i])
+        for i, new in enumerate((new_key_scales, new_value_scales))
+    ]
+    for copy in scales_out:
+        copy.start()
     for r in range(HELD):
 
         @pl.when(plan[r] < 0)
@@ -186,11 +225,11 @@
             for copy in copies(r, False):
                 copy.start()
 
-    new_key_scales[...] = scr[0:HELD, 0:KVH].astype(BF16)
-    new_value_scales[...] = scr[HELD : 2 * HELD, 0:KVH].astype(BF16)
     for r in range(HELD):
         for copy in copies(r, False):
             copy.wait()
+    for copy in scales_out:
+        copy.wait()
 
 
 def unpack(plan, received, keys, values, key_scales, value_scales):
@@ -203,12 +242,14 @@
             shape((HELD, KVH), BF16),
         ),
         in_specs=[SMEM, VMEM, HBM, HBM, VMEM, VMEM],
-        out_specs=(HBM, HBM, VMEM, VMEM),
+        out_specs=(HBM, HBM, HBM, HBM),
         scratch_shapes=[
             pltpu.VMEM((HELD, 2, SPAN, KVH * HD), BF16),
             pltpu.VMEM((2 * HELD, HD), F32),
+            pltpu.VMEM((2, HELD, KVH), BF16),
             pltpu.SemaphoreType.DMA((HELD, 2)),
             pltpu.SemaphoreType.DMA((HELD, 2)),
+            pltpu.SemaphoreType.DMA((2,)),
         ],
         cost_estimate=cost(1 << 20, 4 << 20),
         compiler_params=room(8),
@@ -602,7 +643,9 @@
 ):
     dest = dest_replica.T
     key_scales, value_scales = key_scales[:, 0, :], value_scales[:, 0, :]
-    message, other, plan = front(dest, move_slot, key_codes, value_codes, key_scales, value_scales)
+    message, other, plan = front(
+        dest, move_slot, key_codes, value_codes, key_scales, value_scales
+    )
     other = swap(other, 2)
     received = lax.all_to_all(
         message, "replica", split_axis=0, concat_axis=0, tiled=True

time: 73.8 us -> 71.7 us (0.972)
  Pallas kernels: 18 us -> 16 us
    pallas_call x1, Pallas kernels: 4.06 us -> 2.58 us  [front(): pl.pallas_call(front_kernel, out_shape=(shape((REPLICAS, SLOT, HD), BF16)...]
  transfers between devices with their start and end apart: 15 -> 15, of which waited for: 12 -> 12; matrix products, arithmetic and copies ran while one was open for 0% -> 0% of each run, Pallas kernels for 15% -> 16%
where the time goes in v4:
time: 71.7 us; the launch traced here: 71.4 us
  waiting for transfers between devices  27.1 us (38%)
  starting transfers between devices  26.9 us (38%)
  Pallas kernels  16 us (22%)
  between operations  1.44 us (2%)
    ppermute x5, waiting for transfers between devices, swap(): lax.ppermute(array, 'tensor', [(i, i ^ bits) for i in range(TENSORS)])  15.5 us
    ppermute x9, starting transfers between devices, shift(): lax.ppermute(array, 'tensor', [(i, (i + 4 * rows) % TENSORS) for i in ran...  13.6 us
    ppermute x9, waiting for transfers between devices, shift(): lax.ppermute(array, 'tensor', [(i, (i + 4 * rows) % TENSORS) for i in ran...  11.6 us
    all_to_all x1, starting transfers between devices, local(): lax.all_to_all(message, 'replica', split_axis=0, concat_axis=0, tiled=True)  10.7 us
    pallas_call x1, Pallas kernels, project_query(): pl.pallas_call(query_kernel, out_shape=(shape((ROWS, 2 * HD), BF16), shap...  3.7 us
    pallas_call x1, Pallas kernels, front(): pl.pallas_call(front_kernel, out_shape=(shape((REPLICAS, SLOT, HD), BF16)...  2.58 us
    ppermute x5, starting transfers between devices, swap(): lax.ppermute(array, 'tensor', [(i, i ^ bits) for i in range(TENSORS)])  2.56 us
    pallas_call x1, Pallas kernels, output_other(): pl.pallas_call(output_other_kernel, out_shape=(shape((ROWS, 2 * HD), BF16...  2.28 us
  transfers between devices with their start and end apart: 15, of which 12 were waited for; matrix products, arithmetic and copies ran while one was open for 0% of the time, Pallas kernels for 16%

profile of v4, /device:TPU:68, one launch (start us, length us, event | category | flops | bytes accessed | tf_op | source)
XLA Modules:
  0.0 71.4 jit_solution(12690668811283208062)
XLA Ops:
  0.6 2.6 %front.1 = (bf16[16,520,128]{2,1,0:T(8,128)(2,1)}, bf16[528,512]{1,0:T(8,128)(2,1)}, s32[8]{0:T(128)}) custom-call(s32[6,16]{1,0:T(8,128)} %bitcast.17, s32[1,6]{1,0:T(1,128)} %slots_in.1, bf16[8,32,1024]{2,1,0:T(8,128)(2,1)} %keys.5, bf16[8,32,1024]{2,1,0:T(8,128)(2,1)} %values.5, bf16[8,8]{1,0:T(8,128)(2,1)} %bitcast.8, bf16[8,8]{1,0:T(8,128)(2,1)} %bitcast.11), custom_call_target="tpu_custom_call" | custom-call | flops 1048576 | bytes 4194304 | tf_op jit(solution)/shard_map/front/pallas_call | solution.py:140
  3.3 10.7 %all-to-all-start = ((bf16[16,520,128]{2,1,0:T(8,128)(2,1)}), bf16[16,520,128]{2,1,0:T(8,128)(2,1)S(1)}, u32[]{:S(2)}, u32[]{:S(2)}) async-start(bf16[16,520,128]{2,1,0:T(8,128)(2,1)} %get-tuple-element.46), calls=%async_computation | async-start | bytes 4259840 | tf_op jit(solution)/shard_map/all_to_all | solution.py:650
  14.0 1.2 %collective-permute-start.4 = (bf16[528,512]{1,0:T(8,128)(2,1)}, bf16[528,512]{1,0:T(8,128)(2,1)S(1)}, u32[]{:S(2)}, u32[]{:S(2)}) collective-permute-start(bf16[528,512]{1,0:T(8,128)(2,1)} %get-tuple-element.29), channel_id=1, source_target_pairs={{0,2},{1,3},{2,0},{3,1},{4,6},{5,7},{6,4},{7,5},{8,10},{9,11},{10,... | collective-permute-start | bytes 1622024 | tf_op jit(solution)/shard_map/ppermute | solution.py:607
  15.2 3.7 %query.1 = (bf16[32,256]{1,0:T(8,128)(2,1)S(1)}, bf16[32,512]{1,0:T(8,128)(2,1)S(1)}) custom-call(bf16[32,8192]{1,0:T(8,128)(2,1)} %hidden.1, bf16[8192,256]{1,0:T(8,128)(2,1)} %weight.3, f32[1,128]{1,0:T(1,128)S(1)} %bitcast.15), custom_call_target="tpu_custom_call" | custom-call | flops 4194304 | bytes 5242880 | tf_op jit(solution)/shard_map/query/pallas_call | solution.py:289
  19.0 1.2 %collective-permute-done = bf16[32,256]{1,0:T(8,128)(2,1)S(1)} collective-permute-done((bf16[32,256]{1,0:T(8,128)(2,1)S(1)}, bf16[32,256]{1,0:T(8,128)(2,1)S(1)}, u32[]{:S(2)}, u32[]{:S(2)}) %collective-permute-start) | collective-permute-done | bytes 16416 | tf_op jit(solution)/shard_map/ppermute | solution.py:607
  20.2 1.6 %collective-permute-start.1 = (bf16[2,32,256]{2,1,0:T(8,128)(2,1)S(1)}, bf16[2,32,256]{2,1,0:T(8,128)(2,1)S(1)}, u32[]{:S(2)}, u32[]{:S(2)}) collective-permute-start(bf16[2,32,256]{2,1,0:T(8,128)(2,1)S(1)} %pad_maximum_fusion.q0), channel_id=1, source_target_pairs={{0,4},{1,5},{2,6},{3,7},{4,8},{5,9},{6,10},{7,11},{8,12},{9,13},{1... | collective-permute-start | bytes 98312 | tf_op jit(solution)/shard_map/ppermute | solution.py:611
  21.8 2.9 %collective-permute-start.2 = (bf16[2,32,256]{2,1,0:T(8,128)(2,1)S(1)}, bf16[2,32,256]{2,1,0:T(8,128)(2,1)S(1)}, u32[]{:S(2)}, u32[]{:S(2)}) collective-permute-start(bf16[2,32,256]{2,1,0:T(8,128)(2,1)S(1)} %pad_maximum_fusion.q0), channel_id=1, source_target_pairs={{0,8},{1,9},{2,10},{3,11},{4,12},{5,13},{6,14},{7,15},{8,0},{9,1},... | collective-permute-start | bytes 98312 | tf_op jit(solution)/shard_map/ppermute | solution.py:611
  24.7 1.3 %collective-permute-start.3 = (bf16[2,32,256]{2,1,0:T(8,128)(2,1)S(1)}, bf16[2,32,256]{2,1,0:T(8,128)(2,1)S(1)}, u32[]{:S(2)}, u32[]{:S(2)}) collective-permute-start(bf16[2,32,256]{2,1,0:T(8,128)(2,1)S(1)} %pad_maximum_fusion.q0), channel_id=1, source_target_pairs={{0,12},{1,13},{2,14},{3,15},{4,0},{5,1},{6,2},{7,3},{8,4},{9,5},{1... | collective-permute-start | bytes 98312 | tf_op jit(solution)/shard_map/ppermute | solution.py:611
  26.0 1.2 %collective-permute-done.2.q2 = bf16[2,32,256]{2,1,0:T(8,128)(2,1)S(1)} collective-permute-done((bf16[2,32,256]{2,1,0:T(8,128)(2,1)S(1)}, bf16[2,32,256]{2,1,0:T(8,128)(2,1)S(1)}, u32[]{:S(2)}, u32[]{:S(2)}) %collective-permute-start.2) | collective-permute-done | bytes 32800 | tf_op jit(solution)/shard_map/ppermute | solution.py:611
  27.2 1.4 %collective-permute-done.3.q3 = bf16[2,32,256]{2,1,0:T(8,128)(2,1)S(1)} collective-permute-done((bf16[2,32,256]{2,1,0:T(8,128)(2,1)S(1)}, bf16[2,32,256]{2,1,0:T(8,128)(2,1)S(1)}, u32[]{:S(2)}, u32[]{:S(2)}) %collective-permute-start.3) | collective-permute-done | bytes 32800 | tf_op jit(solution)/shard_map/ppermute | solution.py:611
  28.6 10.8 %collective-permute-done.4.other = bf16[528,512]{1,0:T(8,128)(2,1)S(1)} collective-permute-done((bf16[528,512]{1,0:T(8,128)(2,1)}, bf16[528,512]{1,0:T(8,128)(2,1)S(1)}, u32[]{:S(2)}, u32[]{:S(2)}) %collective-permute-start.4) | collective-permute-done | bytes 540704 | tf_op jit(solution)/shard_map/ppermute | solution.py:607
  39.4 1.9 %attend.1 = (bf16[160,128]{1,0:T(8,128)(2,1)S(1)}, bf16[160,128]{1,0:T(8,128)(2,1)S(1)}, bf16[160,128]{1,0:T(8,128)(2,1)S(1)}, bf16[160,128]{1,0:T(8,128)(2,1)S(1)}) custom-call(s32[8]{0:T(128)S(1)} %copy-done.4, bf16[2,32,256]{2,1,0:T(8,128)(2,1)S(1)} %pad_maximum_fusion.q0, bf16[2,32,256]{2,1,0:T(8,128)(2,1)S(1)} %collective-permute-done.1.q1, ...), custom_call_target="tpu_custom_call" | custom-call | flops 4194304 | bytes 2097152 | tf_op jit(solution)/shard_map/attend/pallas_call | solution.py:416
  41.3 3.1 %collective-permute-start.5 = (bf16[160,128]{1,0:T(8,128)(2,1)S(1)}, bf16[160,128]{1,0:T(8,128)(2,1)S(1)}, u32[]{:S(2)}, u32[]{:S(2)}) collective-permute-start(bf16[160,128]{1,0:T(8,128)(2,1)S(1)} %get-tuple-element.31), channel_id=1, source_target_pairs={{0,12},{1,13},{2,14},{3,15},{4,0},{5,1},{6,2},{7,3},{8,4},{9,5},{1... | collective-permute-start | bytes 122888 | tf_op jit(solution)/shard_map/ppermute | solution.py:611
  46.0 3.8 %collective-permute-done.6.p2 = bf16[160,128]{1,0:T(8,128)(2,1)S(1)} collective-permute-done((bf16[160,128]{1,0:T(8,128)(2,1)S(1)}, bf16[160,128]{1,0:T(8,128)(2,1)S(1)}, u32[]{:S(2)}, u32[]{:S(2)}) %collective-permute-start.6) | collective-permute-done | bytes 40992 | tf_op jit(solution)/shard_map/ppermute | solution.py:611
  50.7 1.2 %collective-permute-done.8.p1 = bf16[96,128]{1,0:T(8,128)(2,1)S(1)} collective-permute-done((bf16[96,128]{1,0:T(8,128)(2,1)S(1)}, bf16[96,128]{1,0:T(8,128)(2,1)S(1)}, u32[]{:S(2)}, u32[]{:S(2)}) %collective-permute-start.8) | collective-permute-done | bytes 24608 | tf_op jit(solution)/shard_map/ppermute | solution.py:607
  51.9 2.3 %output_other.1 = (bf16[32,256]{1,0:T(8,128)(2,1)S(1)}, bf16[8,32,512]{2,1,0:T(8,128)(2,1)S(1)}) custom-call(bf16[96,128]{1,0:T(8,128)(2,1)S(1)} %get-tuple-element.34.p0, bf16[96,128]{1,0:T(8,128)(2,1)S(1)} %collective-permute-done.8.p1, bf16[256,8192]{1,0:T(8,128)(2,1)} %weight.5), custom_call_target="tpu_custom_call" | custom-call | flops 4194304 | bytes 2097152 | tf_op jit(solution)/shard_map/output_other/pallas_call | solution.py:516
  54.4 2.3 %output_own.1.own = f32[8,32,512]{2,1,0:T(8,128)S(1)} custom-call(bf16[32,256]{1,0:T(8,128)(2,1)S(1)} %get-tuple-element.36.attended, bf16[256,8192]{1,0:T(8,128)(2,1)} %weight.5), custom_call_target="tpu_custom_call" | custom-call | flops 4194304 | bytes 2097152 | tf_op jit(solution)/shard_map/output_own/pallas_call | solution.py:532
  57.4 1.2 %collective-permute-start.11 = (bf16[2,32,512]{2,1,0:T(8,128)(2,1)S(1)}, bf16[2,32,512]{2,1,0:T(8,128)(2,1)S(1)}, u32[]{:S(2)}, u32[]{:S(2)}) collective-permute-start(bf16[2,32,512]{2,1,0:T(8,128)(2,1)S(1)} %get-tuple-element.40), channel_id=1, source_target_pairs={{0,8},{1,9},{2,10},{3,11},{4,12},{5,13},{6,14},{7,15},{8,0},{9,1},... | collective-permute-start | bytes 196616 | tf_op jit(solution)/shard_map/ppermute | solution.py:611
  58.6 1.3 %collective-permute-start.12 = (bf16[2,32,512]{2,1,0:T(8,128)(2,1)S(1)}, bf16[2,32,512]{2,1,0:T(8,128)(2,1)S(1)}, u32[]{:S(2)}, u32[]{:S(2)}) collective-permute-start(bf16[2,32,512]{2,1,0:T(8,128)(2,1)S(1)} %get-tuple-element.41), channel_id=1, source_target_pairs={{0,4},{1,5},{2,6},{3,7},{4,8},{5,9},{6,10},{7,11},{8,12},{9,13},{1... | collective-permute-start | bytes 196616 | tf_op jit(solution)/shard_map/ppermute | solution.py:611
  59.8 2.0 %collective-permute-done.10.r1 = bf16[2,32,512]{2,1,0:T(8,128)(2,1)S(1)} collective-permute-done((bf16[2,32,512]{2,1,0:T(8,128)(2,1)S(1)}, bf16[2,32,512]{2,1,0:T(8,128)(2,1)S(1)}, u32[]{:S(2)}, u32[]{:S(2)}) %collective-permute-start.10) | collective-permute-done | bytes 65568 | tf_op jit(solution)/shard_map/ppermute | solution.py:611
  61.8 1.5 %collective-permute-done.11.r2 = bf16[2,32,512]{2,1,0:T(8,128)(2,1)S(1)} collective-permute-done((bf16[2,32,512]{2,1,0:T(8,128)(2,1)S(1)}, bf16[2,32,512]{2,1,0:T(8,128)(2,1)S(1)}, u32[]{:S(2)}, u32[]{:S(2)}) %collective-permute-start.11) | collective-permute-done | bytes 65568 | tf_op jit(solution)/shard_map/ppermute | solution.py:611
  63.3 1.2 %collective-permute-done.12.r3 = bf16[2,32,512]{2,1,0:T(8,128)(2,1)S(1)} collective-permute-done((bf16[2,32,512]{2,1,0:T(8,128)(2,1)S(1)}, bf16[2,32,512]{2,1,0:T(8,128)(2,1)S(1)}, u32[]{:S(2)}, u32[]{:S(2)}) %collective-permute-start.12) | collective-permute-done | bytes 65568 | tf_op jit(solution)/shard_map/ppermute | solution.py:611
  66.1 2.4 %collective-permute-done.13.received = bf16[32,512]{1,0:T(8,128)(2,1)S(1)} collective-permute-done((bf16[32,512]{1,0:T(8,128)(2,1)S(1)}, bf16[32,512]{1,0:T(8,128)(2,1)S(1)}, u32[]{:S(2)}, u32[]{:S(2)}) %collective-permute-start.13) | collective-permute-done | bytes 32800 | tf_op jit(solution)/shard_map/ppermute | solution.py:607
  69.2 2.2 %unpack.1 = (bf16[8,32,1024]{2,1,0:T(8,128)(2,1)}, bf16[8,32,1024]{2,1,0:T(8,128)(2,1)}, bf16[8,8]{1,0:T(8,128)(2,1)}, bf16[8,8]{1,0:T(8,128)(2,1)}) custom-call(s32[8]{0:T(128)S(1)} %copy-done.6, bf16[16,520,128]{2,1,0:T(8,128)(2,1)S(1)} %all-to-all-done.received, bf16[8,32,1024]{2,1,0:T(8,128)(2,1)S(1)} %copy-done, bf16[8,32,1024]{2,1,0:T(8,128)(2,1)S(1)} %copy-done.1, ...), custom_call_target="tpu_custom_call" | custom-call | flops 1048576 | bytes 4194304 | tf_op jit(solution)/shard_map/unpack/pallas_call | solution.py:236
  (31 shorter events, 5.2 us)
Async XLA Ops:
  0.6 14.6 %copy-start.5 = (f32[128]{0:T(128)S(1)}, f32[128]{0:T(128)}, u32[]{:S(2)}) copy-start(f32[128]{0:T(128)} %param.14) | copy-start | bytes 1540
  3.2 36.1 %copy-start = (bf16[8,32,1024]{2,1,0:T(8,128)(2,1)S(1)}, bf16[8,32,1024]{2,1,0:T(8,128)(2,1)}, u32[]{:S(2)}) copy-start(bf16[8,32,1024]{2,1,0:T(8,128)(2,1)} %keys.5) | copy-start | bytes 1572868
  3.2 36.1 %copy-start.1 = (bf16[8,32,1024]{2,1,0:T(8,128)(2,1)S(1)}, bf16[8,32,1024]{2,1,0:T(8,128)(2,1)}, u32[]{:S(2)}) copy-start(bf16[8,32,1024]{2,1,0:T(8,128)(2,1)} %values.5) | copy-start | bytes 1572868
  3.3 36.1 %copy-start.2 = (bf16[8,1,8]{2,0,1:T(8,128)(2,1)S(1)}, bf16[8,1,8]{2,0,1:T(8,128)(2,1)}, u32[]{:S(2)}) copy-start(bf16[8,1,8]{2,0,1:T(8,128)(2,1)} %param.19) | copy-start | bytes 388
  3.3 36.1 %copy-start.3 = (bf16[8,1,8]{2,0,1:T(8,128)(2,1)S(1)}, bf16[8,1,8]{2,0,1:T(8,128)(2,1)}, u32[]{:S(2)}) copy-start(bf16[8,1,8]{2,0,1:T(8,128)(2,1)} %param.20) | copy-start | bytes 388
  3.3 36.1 %copy-start.4 = (s32[8]{0:T(128)S(1)}, s32[8]{0:T(128)}, u32[]{:S(2)}) copy-start(s32[8]{0:T(128)} %lengths.1) | copy-start | bytes 100
  3.3 65.9 %all-to-all-start = ((bf16[16,520,128]{2,1,0:T(8,128)(2,1)}), bf16[16,520,128]{2,1,0:T(8,128)(2,1)S(1)}, u32[]{:S(2)}, u32[]{:S(2)}) async-start(bf16[16,520,128]{2,1,0:T(8,128)(2,1)} %get-tuple-element.46), calls=%async_computation | async-start | bytes 4259840 | tf_op jit(solution)/shard_map/all_to_all | solution.py:650
  14.0 25.3 %collective-permute-start.4 = (bf16[528,512]{1,0:T(8,128)(2,1)}, bf16[528,512]{1,0:T(8,128)(2,1)S(1)}, u32[]{:S(2)}, u32[]{:S(2)}) collective-permute-start(bf16[528,512]{1,0:T(8,128)(2,1)} %get-tuple-element.29), channel_id=1, source_target_pairs={{0,2},{1,3},{2,0},{3,1},{4,6},{5,7},{6,4},{7,5},{8,10},{9,11},{10,... | collective-permute-start | bytes 1622024 | tf_op jit(solution)/shard_map/ppermute | solution.py:607
  18.9 1.3 %collective-permute-start = (bf16[32,256]{1,0:T(8,128)(2,1)S(1)}, bf16[32,256]{1,0:T(8,128)(2,1)S(1)}, u32[]{:S(2)}, u32[]{:S(2)}) collective-permute-start(bf16[32,256]{1,0:T(8,128)(2,1)S(1)} %get-tuple-element.28), channel_id=1, source_target_pairs={{0,1},{1,0},{2,3},{3,2},{4,5},{5,4},{6,7},{7,6},{8,9},{9,8},{10,11... | collective-permute-start | bytes 49160 | tf_op jit(solution)/shard_map/ppermute | solution.py:607
  20.2 5.8 %collective-permute-start.1 = (bf16[2,32,256]{2,1,0:T(8,128)(2,1)S(1)}, bf16[2,32,256]{2,1,0:T(8,128)(2,1)S(1)}, u32[]{:S(2)}, u32[]{:S(2)}) collective-permute-start(bf16[2,32,256]{2,1,0:T(8,128)(2,1)S(1)} %pad_maximum_fusion.q0), channel_id=1, source_target_pairs={{0,4},{1,5},{2,6},{3,7},{4,8},{5,9},{6,10},{7,11},{8,12},{9,13},{1... | collective-permute-start | bytes 98312 | tf_op jit(solution)/shard_map/ppermute | solution.py:611
  21.8 5.4 %collective-permute-start.2 = (bf16[2,32,256]{2,1,0:T(8,128)(2,1)S(1)}, bf16[2,32,256]{2,1,0:T(8,128)(2,1)S(1)}, u32[]{:S(2)}, u32[]{:S(2)}) collective-permute-start(bf16[2,32,256]{2,1,0:T(8,128)(2,1)S(1)} %pad_maximum_fusion.q0), channel_id=1, source_target_pairs={{0,8},{1,9},{2,10},{3,11},{4,12},{5,13},{6,14},{7,15},{8,0},{9,1},... | collective-permute-start | bytes 98312 | tf_op jit(solution)/shard_map/ppermute | solution.py:611
  24.7 3.9 %collective-permute-start.3 = (bf16[2,32,256]{2,1,0:T(8,128)(2,1)S(1)}, bf16[2,32,256]{2,1,0:T(8,128)(2,1)S(1)}, u32[]{:S(2)}, u32[]{:S(2)}) collective-permute-start(bf16[2,32,256]{2,1,0:T(8,128)(2,1)S(1)} %pad_maximum_fusion.q0), channel_id=1, source_target_pairs={{0,12},{1,13},{2,14},{3,15},{4,0},{5,1},{6,2},{7,3},{8,4},{9,5},{1... | collective-permute-start | bytes 98312 | tf_op jit(solution)/shard_map/ppermute | solution.py:611
  41.3 4.8 %collective-permute-start.5 = (bf16[160,128]{1,0:T(8,128)(2,1)S(1)}, bf16[160,128]{1,0:T(8,128)(2,1)S(1)}, u32[]{:S(2)}, u32[]{:S(2)}) collective-permute-start(bf16[160,128]{1,0:T(8,128)(2,1)S(1)} %get-tuple-element.31), channel_id=1, source_target_pairs={{0,12},{1,13},{2,14},{3,15},{4,0},{5,1},{6,2},{7,3},{8,4},{9,5},{1... | collective-permute-start | bytes 122888 | tf_op jit(solution)/shard_map/ppermute | solution.py:611
  44.4 5.5 %collective-permute-start.6 = (bf16[160,128]{1,0:T(8,128)(2,1)S(1)}, bf16[160,128]{1,0:T(8,128)(2,1)S(1)}, u32[]{:S(2)}, u32[]{:S(2)}) collective-permute-start(bf16[160,128]{1,0:T(8,128)(2,1)S(1)} %get-tuple-element.32), channel_id=1, source_target_pairs={{0,8},{1,9},{2,10},{3,11},{4,12},{5,13},{6,14},{7,15},{8,0},{9,1},... | collective-permute-start | bytes 122888 | tf_op jit(solution)/shard_map/ppermute | solution.py:611
  45.0 5.3 %collective-permute-start.7 = (bf16[160,128]{1,0:T(8,128)(2,1)S(1)}, bf16[160,128]{1,0:T(8,128)(2,1)S(1)}, u32[]{:S(2)}, u32[]{:S(2)}) collective-permute-start(bf16[160,128]{1,0:T(8,128)(2,1)S(1)} %get-tuple-element.33), channel_id=1, source_target_pairs={{0,4},{1,5},{2,6},{3,7},{4,8},{5,9},{6,10},{7,11},{8,12},{9,13},{1... | collective-permute-start | bytes 122888 | tf_op jit(solution)/shard_map/ppermute | solution.py:611
  50.6 1.3 %collective-permute-start.8 = (bf16[96,128]{1,0:T(8,128)(2,1)S(1)}, bf16[96,128]{1,0:T(8,128)(2,1)S(1)}, u32[]{:S(2)}, u32[]{:S(2)}) collective-permute-start(bf16[96,128]{1,0:T(8,128)(2,1)S(1)} %get-tuple-element.35), channel_id=1, source_target_pairs={{0,1},{1,0},{2,3},{3,2},{4,5},{5,4},{6,7},{7,6},{8,9},{9,8},{10,11... | collective-permute-start | bytes 73736 | tf_op jit(solution)/shard_map/ppermute | solution.py:607
  51.9 17.3 %copy-start.6 = (s32[8]{0:T(128)S(1)}, s32[8]{0:T(128)}, u32[]{:S(2)}) copy-start(s32[8]{0:T(128)} %get-tuple-element.45.plan) | copy-start | bytes 100
  54.2 2.5 %collective-permute-start.9 = (bf16[8,32,512]{2,1,0:T(8,128)(2,1)S(1)}, bf16[8,32,512]{2,1,0:T(8,128)(2,1)S(1)}, u32[]{:S(2)}, u32[]{:S(2)}) collective-permute-start(bf16[8,32,512]{2,1,0:T(8,128)(2,1)S(1)} %get-tuple-element.37), channel_id=1, source_target_pairs={{0,1},{1,0},{2,3},{3,2},{4,5},{5,4},{6,7},{7,6},{8,9},{9,8},{10,11... | collective-permute-start | bytes 786440 | tf_op jit(solution)/shard_map/ppermute | solution.py:607
  56.8 5.0 %collective-permute-start.10 = (bf16[2,32,512]{2,1,0:T(8,128)(2,1)S(1)}, bf16[2,32,512]{2,1,0:T(8,128)(2,1)S(1)}, u32[]{:S(2)}, u32[]{:S(2)}) collective-permute-start(bf16[2,32,512]{2,1,0:T(8,128)(2,1)S(1)} %get-tuple-element.39), channel_id=1, source_target_pairs={{0,12},{1,13},{2,14},{3,15},{4,0},{5,1},{6,2},{7,3},{8,4},{9,5},{1... | collective-permute-start | bytes 196616 | tf_op jit(solution)/shard_map/ppermute | solution.py:611
  57.4 5.9 %collective-permute-start.11 = (bf16[2,32,512]{2,1,0:T(8,128)(2,1)S(1)}, bf16[2,32,512]{2,1,0:T(8,128)(2,1)S(1)}, u32[]{:S(2)}, u32[]{:S(2)}) collective-permute-start(bf16[2,32,512]{2,1,0:T(8,128)(2,1)S(1)} %get-tuple-element.40), channel_id=1, source_target_pairs={{0,8},{1,9},{2,10},{3,11},{4,12},{5,13},{6,14},{7,15},{8,0},{9,1},... | collective-permute-start | bytes 196616 | tf_op jit(solution)/shard_map/ppermute | solution.py:611
  58.6 5.9 %collective-permute-start.12 = (bf16[2,32,512]{2,1,0:T(8,128)(2,1)S(1)}, bf16[2,32,512]{2,1,0:T(8,128)(2,1)S(1)}, u32[]{:S(2)}, u32[]{:S(2)}) collective-permute-start(bf16[2,32,512]{2,1,0:T(8,128)(2,1)S(1)} %get-tuple-element.41), channel_id=1, source_target_pairs={{0,4},{1,5},{2,6},{3,7},{4,8},{5,9},{6,10},{7,11},{8,12},{9,13},{1... | collective-permute-start | bytes 196616 | tf_op jit(solution)/shard_map/ppermute | solution.py:611
  64.5 4.0 %collective-permute-start.13 = (bf16[32,512]{1,0:T(8,128)(2,1)S(1)}, bf16[32,512]{1,0:T(8,128)(2,1)S(1)}, u32[]{:S(2)}, u32[]{:S(2)}) collective-permute-start(bf16[32,512]{1,0:T(8,128)(2,1)S(1)} %get-tuple-element.43), channel_id=1, source_target_pairs={{0,2},{1,3},{2,0},{3,1},{4,6},{5,7},{6,4},{7,5},{8,10},{9,11},{10,... | collective-permute-start | bytes 98312 | tf_op jit(solution)/shard_map/ppermute | solution.py:607

commit v5 on v4

--- a/solution.py
+++ b/solution.py
@@ -169,44 +169,46 @@
 def unpack_kernel(
     plan, received, keys, values, key_scales, value_scales,
     new_keys, new_values, new_key_scales, new_value_scales,
-    stage, scr, thin, in_sem, out_sem, thin_sem,
+    stage, scr, thin, out_sem, thin_sem,
 ):
-    def copies(r, inward):
-        pairs = ((keys, new_keys), (values, new_values))
-        if inward:
-            return [
-                pltpu.make_async_copy(old.at[r], stage.at[r, i], in_sem.at[r, i])
-                for i, (old, _) in enumerate(pairs)
-            ]
+    pairs = ((keys, new_keys), (values, new_values))
+
+    def stores(r, kept):
         return [
-            pltpu.make_async_copy(stage.at[r, i], new.at[r], out_sem.at[r, i])
-            for i, (_, new) in enumerate(pairs)
+            pltpu.make_async_copy(old.at[r] if kept else stage.at[r, i], new.at[r], out_sem.at[r, i])
+            for i, (old, new) in enumerate(pairs)
         ]
 
     for r in range(HELD):
 
         @pl.when(plan[r] < 0)
         def _():
-            for copy in copies(r, True):
+            for copy in stores(r, True):
                 copy.start()
 
-    scale_rows(scr, key_scales, value_scales)
     for r in range(HELD):
         source = plan[r]
 
         @pl.when(source >= 0)
         def _():
-            both = received[source, 2 * KVH * SPAN : SLOT, :].astype(F32)
-            scr[r : r + 1, :] = both[0:1, :]
-            scr[HELD + r : HELD + r + 1, :] = both[1:2, :]
             for which in range(2):
                 for c in range(KVH):
                     at_row = (which * KVH + c) * SPAN
                     stage[r, which, :, c * HD : (c + 1) * HD] = received[
                         source, at_row : at_row + SPAN, :
                     ]
-            for copy in copies(r, False):
+            for copy in stores(r, False):
                 copy.start()
+
+    scale_rows(scr, key_scales, value_scales)
+    for r in range(HELD):
+        source = plan[r]
+
+        @pl.when(source >= 0)
+        def _():
+            both = received[source, 2 * KVH * SPAN : SLOT, :].astype(F32)
+            scr[r : r + 1, :] = both[0:1, :]
+            scr[HELD + r : HELD + r + 1, :] = both[1:2, :]
 
     thin[0] = scr[0:HELD, 0:KVH].astype(BF16)
     thin[1] = scr[HELD : 2 * HELD, 0:KVH].astype(BF16)
@@ -217,16 +219,7 @@
     for copy in scales_out:
         copy.start()
     for r in range(HELD):
-
-        @pl.when(plan[r] < 0)
-        def _():
-            for copy in copies(r, True):
-                copy.wait()
-            for copy in copies(r, False):
-                copy.start()
-
-    for r in range(HELD):
-        for copy in copies(r, False):
+        for copy in stores(r, False):
             copy.wait()
     for copy in scales_out:
         copy.wait()
@@ -241,13 +234,12 @@
             shape((HELD, KVH), BF16),
             shape((HELD, KVH), BF16),
         ),
-        in_specs=[SMEM, VMEM, HBM, HBM, VMEM, VMEM],
+        in_specs=[SMEM, VMEM, VMEM, VMEM, VMEM, VMEM],
         out_specs=(HBM, HBM, HBM, HBM),
         scratch_shapes=[
             pltpu.VMEM((HELD, 2, SPAN, KVH * HD), BF16),
             pltpu.VMEM((2 * HELD, HD), F32),
             pltpu.VMEM((2, HELD, KVH), BF16),
-            pltpu.SemaphoreType.DMA((HELD, 2)),
             pltpu.SemaphoreType.DMA((HELD, 2)),
             pltpu.SemaphoreType.DMA((2,)),
         ],
@@ -643,9 +635,7 @@
 ):
     dest = dest_replica.T
     key_scales, value_scales = key_scales[:, 0, :], value_scales[:, 0, :]
-    message, other, plan = front(
-        dest, move_slot, key_codes, value_codes, key_scales, value_scales
-    )
+    message, other, plan = front(dest, move_slot, key_codes, value_codes, key_scales, value_scales)
     other = swap(other, 2)
     received = lax.all_to_all(
         message, "replica", split_axis=0, concat_axis=0, tiled=True

time: 71.7 us -> 71.1 us (level)
  no operation moved by 1% of the time
where the time goes in v5:
time: 71.1 us; the launch traced here: 70.8 us
  waiting for transfers between devices  27.1 us (38%)
  starting transfers between devices  26.9 us (38%)
  Pallas kernels  15.4 us (22%)
  between operations  1.44 us (2%)
    ppermute x5, waiting for transfers between devices, swap(): lax.ppermute(array, 'tensor', [(i, i ^ bits) for i in range(TENSORS)])  15.5 us
    ppermute x9, starting transfers between devices, shift(): lax.ppermute(array, 'tensor', [(i, (i + 4 * rows) % TENSORS) for i in ran...  13.6 us
    ppermute x9, waiting for transfers between devices, shift(): lax.ppermute(array, 'tensor', [(i, (i + 4 * rows) % TENSORS) for i in ran...  11.6 us
    all_to_all x1, starting transfers between devices, local(): lax.all_to_all(message, 'replica', split_axis=0, concat_axis=0, tiled=True)  10.7 us
    pallas_call x1, Pallas kernels, project_query(): pl.pallas_call(query_kernel, out_shape=(shape((ROWS, 2 * HD), BF16), shap...  3.7 us
    pallas_call x1, Pallas kernels, front(): pl.pallas_call(front_kernel, out_shape=(shape((REPLICAS, SLOT, HD), BF16)...  2.58 us
    ppermute x5, starting transfers between devices, swap(): lax.ppermute(array, 'tensor', [(i, i ^ bits) for i in range(TENSORS)])  2.56 us
    pallas_call x1, Pallas kernels, output_other(): pl.pallas_call(output_other_kernel, out_shape=(shape((ROWS, 2 * HD), BF16...  2.28 us
  transfers between devices with their start and end apart: 15, of which 12 were waited for; matrix products, arithmetic and copies ran while one was open for 0% of the time, Pallas kernels for 16%

profile of v5, /device:TPU:68, one launch (start us, length us, event | category | flops | bytes accessed | tf_op | source)
XLA Modules:
  0.0 70.8 jit_solution(5069285966372965749)
XLA Ops:
  0.6 2.6 %front.1 = (bf16[16,520,128]{2,1,0:T(8,128)(2,1)}, bf16[528,512]{1,0:T(8,128)(2,1)}, s32[8]{0:T(128)}) custom-call(s32[6,16]{1,0:T(8,128)} %bitcast.17, s32[1,6]{1,0:T(1,128)} %slots_in.1, bf16[8,32,1024]{2,1,0:T(8,128)(2,1)} %keys.5, bf16[8,32,1024]{2,1,0:T(8,128)(2,1)} %values.5, bf16[8,8]{1,0:T(8,128)(2,1)} %bitcast.8, bf16[8,8]{1,0:T(8,128)(2,1)} %bitcast.11), custom_call_target="tpu_custom_call" | custom-call | flops 1048576 | bytes 4194304 | tf_op jit(solution)/shard_map/front/pallas_call | solution.py:140
  3.3 10.7 %all-to-all-start = ((bf16[16,520,128]{2,1,0:T(8,128)(2,1)}), bf16[16,520,128]{2,1,0:T(8,128)(2,1)S(1)}, u32[]{:S(2)}, u32[]{:S(2)}) async-start(bf16[16,520,128]{2,1,0:T(8,128)(2,1)} %get-tuple-element.46), calls=%async_computation | async-start | bytes 4259840 | tf_op jit(solution)/shard_map/all_to_all | solution.py:640
  14.0 1.2 %collective-permute-start.4 = (bf16[528,512]{1,0:T(8,128)(2,1)}, bf16[528,512]{1,0:T(8,128)(2,1)S(1)}, u32[]{:S(2)}, u32[]{:S(2)}) collective-permute-start(bf16[528,512]{1,0:T(8,128)(2,1)} %get-tuple-element.29), channel_id=1, source_target_pairs={{0,2},{1,3},{2,0},{3,1},{4,6},{5,7},{6,4},{7,5},{8,10},{9,11},{10,... | collective-permute-start | bytes 1622024 | tf_op jit(solution)/shard_map/ppermute | solution.py:599
  15.2 3.7 %query.1 = (bf16[32,256]{1,0:T(8,128)(2,1)S(1)}, bf16[32,512]{1,0:T(8,128)(2,1)S(1)}) custom-call(bf16[32,8192]{1,0:T(8,128)(2,1)} %hidden.1, bf16[8192,256]{1,0:T(8,128)(2,1)} %weight.3, f32[1,128]{1,0:T(1,128)S(1)} %bitcast.15), custom_call_target="tpu_custom_call" | custom-call | flops 4194304 | bytes 5242880 | tf_op jit(solution)/shard_map/query/pallas_call | solution.py:281
  19.0 1.2 %collective-permute-done = bf16[32,256]{1,0:T(8,128)(2,1)S(1)} collective-permute-done((bf16[32,256]{1,0:T(8,128)(2,1)S(1)}, bf16[32,256]{1,0:T(8,128)(2,1)S(1)}, u32[]{:S(2)}, u32[]{:S(2)}) %collective-permute-start) | collective-permute-done | bytes 16416 | tf_op jit(solution)/shard_map/ppermute | solution.py:599
  20.2 1.6 %collective-permute-start.1 = (bf16[2,32,256]{2,1,0:T(8,128)(2,1)S(1)}, bf16[2,32,256]{2,1,0:T(8,128)(2,1)S(1)}, u32[]{:S(2)}, u32[]{:S(2)}) collective-permute-start(bf16[2,32,256]{2,1,0:T(8,128)(2,1)S(1)} %pad_maximum_fusion.q0), channel_id=1, source_target_pairs={{0,4},{1,5},{2,6},{3,7},{4,8},{5,9},{6,10},{7,11},{8,12},{9,13},{1... | collective-permute-start | bytes 98312 | tf_op jit(solution)/shard_map/ppermute | solution.py:603
  21.8 2.9 %collective-permute-start.2 = (bf16[2,32,256]{2,1,0:T(8,128)(2,1)S(1)}, bf16[2,32,256]{2,1,0:T(8,128)(2,1)S(1)}, u32[]{:S(2)}, u32[]{:S(2)}) collective-permute-start(bf16[2,32,256]{2,1,0:T(8,128)(2,1)S(1)} %pad_maximum_fusion.q0), channel_id=1, source_target_pairs={{0,8},{1,9},{2,10},{3,11},{4,12},{5,13},{6,14},{7,15},{8,0},{9,1},... | collective-permute-start | bytes 98312 | tf_op jit(solution)/shard_map/ppermute | solution.py:603
  24.7 1.3 %collective-permute-start.3 = (bf16[2,32,256]{2,1,0:T(8,128)(2,1)S(1)}, bf16[2,32,256]{2,1,0:T(8,128)(2,1)S(1)}, u32[]{:S(2)}, u32[]{:S(2)}) collective-permute-start(bf16[2,32,256]{2,1,0:T(8,128)(2,1)S(1)} %pad_maximum_fusion.q0), channel_id=1, source_target_pairs={{0,12},{1,13},{2,14},{3,15},{4,0},{5,1},{6,2},{7,3},{8,4},{9,5},{1... | collective-permute-start | bytes 98312 | tf_op jit(solution)/shard_map/ppermute | solution.py:603
  26.0 1.2 %collective-permute-done.2.q2 = bf16[2,32,256]{2,1,0:T(8,128)(2,1)S(1)} collective-permute-done((bf16[2,32,256]{2,1,0:T(8,128)(2,1)S(1)}, bf16[2,32,256]{2,1,0:T(8,128)(2,1)S(1)}, u32[]{:S(2)}, u32[]{:S(2)}) %collective-permute-start.2) | collective-permute-done | bytes 32800 | tf_op jit(solution)/shard_map/ppermute | solution.py:603
  27.2 1.4 %collective-permute-done.3.q3 = bf16[2,32,256]{2,1,0:T(8,128)(2,1)S(1)} collective-permute-done((bf16[2,32,256]{2,1,0:T(8,128)(2,1)S(1)}, bf16[2,32,256]{2,1,0:T(8,128)(2,1)S(1)}, u32[]{:S(2)}, u32[]{:S(2)}) %collective-permute-start.3) | collective-permute-done | bytes 32800 | tf_op jit(solution)/shard_map/ppermute | solution.py:603
  28.6 10.8 %collective-permute-done.4.other = bf16[528,512]{1,0:T(8,128)(2,1)S(1)} collective-permute-done((bf16[528,512]{1,0:T(8,128)(2,1)}, bf16[528,512]{1,0:T(8,128)(2,1)S(1)}, u32[]{:S(2)}, u32[]{:S(2)}) %collective-permute-start.4) | collective-permute-done | bytes 540704 | tf_op jit(solution)/shard_map/ppermute | solution.py:599
  39.4 1.9 %attend.1 = (bf16[160,128]{1,0:T(8,128)(2,1)S(1)}, bf16[160,128]{1,0:T(8,128)(2,1)S(1)}, bf16[160,128]{1,0:T(8,128)(2,1)S(1)}, bf16[160,128]{1,0:T(8,128)(2,1)S(1)}) custom-call(s32[8]{0:T(128)S(1)} %copy-done.4, bf16[2,32,256]{2,1,0:T(8,128)(2,1)S(1)} %pad_maximum_fusion.q0, bf16[2,32,256]{2,1,0:T(8,128)(2,1)S(1)} %collective-permute-done.1.q1, ...), custom_call_target="tpu_custom_call" | custom-call | flops 4194304 | bytes 2097152 | tf_op jit(solution)/shard_map/attend/pallas_call | solution.py:408
  41.3 3.1 %collective-permute-start.5 = (bf16[160,128]{1,0:T(8,128)(2,1)S(1)}, bf16[160,128]{1,0:T(8,128)(2,1)S(1)}, u32[]{:S(2)}, u32[]{:S(2)}) collective-permute-start(bf16[160,128]{1,0:T(8,128)(2,1)S(1)} %get-tuple-element.31), channel_id=1, source_target_pairs={{0,12},{1,13},{2,14},{3,15},{4,0},{5,1},{6,2},{7,3},{8,4},{9,5},{1... | collective-permute-start | bytes 122888 | tf_op jit(solution)/shard_map/ppermute | solution.py:603
  46.0 3.8 %collective-permute-done.6.p2 = bf16[160,128]{1,0:T(8,128)(2,1)S(1)} collective-permute-done((bf16[160,128]{1,0:T(8,128)(2,1)S(1)}, bf16[160,128]{1,0:T(8,128)(2,1)S(1)}, u32[]{:S(2)}, u32[]{:S(2)}) %collective-permute-start.6) | collective-permute-done | bytes 40992 | tf_op jit(solution)/shard_map/ppermute | solution.py:603
  50.7 1.2 %collective-permute-done.8.p1 = bf16[96,128]{1,0:T(8,128)(2,1)S(1)} collective-permute-done((bf16[96,128]{1,0:T(8,128)(2,1)S(1)}, bf16[96,128]{1,0:T(8,128)(2,1)S(1)}, u32[]{:S(2)}, u32[]{:S(2)}) %collective-permute-start.8) | collective-permute-done | bytes 24608 | tf_op jit(solution)/shard_map/ppermute | solution.py:599
  51.9 2.3 %output_other.1 = (bf16[32,256]{1,0:T(8,128)(2,1)S(1)}, bf16[8,32,512]{2,1,0:T(8,128)(2,1)S(1)}) custom-call(bf16[96,128]{1,0:T(8,128)(2,1)S(1)} %get-tuple-element.34.p0, bf16[96,128]{1,0:T(8,128)(2,1)S(1)} %collective-permute-done.8.p1, bf16[256,8192]{1,0:T(8,128)(2,1)} %weight.5), custom_call_target="tpu_custom_call" | custom-call | flops 4194304 | bytes 2097152 | tf_op jit(solution)/shard_map/output_other/pallas_call | solution.py:508
  54.4 2.3 %output_own.1.own = f32[8,32,512]{2,1,0:T(8,128)S(1)} custom-call(bf16[32,256]{1,0:T(8,128)(2,1)S(1)} %get-tuple-element.36.attended, bf16[256,8192]{1,0:T(8,128)(2,1)} %weight.5), custom_call_target="tpu_custom_call" | custom-call | flops 4194304 | bytes 2097152 | tf_op jit(solution)/shard_map/output_own/pallas_call | solution.py:524
  57.4 1.2 %collective-permute-start.11 = (bf16[2,32,512]{2,1,0:T(8,128)(2,1)S(1)}, bf16[2,32,512]{2,1,0:T(8,128)(2,1)S(1)}, u32[]{:S(2)}, u32[]{:S(2)}) collective-permute-start(bf16[2,32,512]{2,1,0:T(8,128)(2,1)S(1)} %get-tuple-element.40), channel_id=1, source_target_pairs={{0,8},{1,9},{2,10},{3,11},{4,12},{5,13},{6,14},{7,15},{8,0},{9,1},... | collective-permute-start | bytes 196616 | tf_op jit(solution)/shard_map/ppermute | solution.py:603
  58.6 1.3 %collective-permute-start.12 = (bf16[2,32,512]{2,1,0:T(8,128)(2,1)S(1)}, bf16[2,32,512]{2,1,0:T(8,128)(2,1)S(1)}, u32[]{:S(2)}, u32[]{:S(2)}) collective-permute-start(bf16[2,32,512]{2,1,0:T(8,128)(2,1)S(1)} %get-tuple-element.41), channel_id=1, source_target_pairs={{0,4},{1,5},{2,6},{3,7},{4,8},{5,9},{6,10},{7,11},{8,12},{9,13},{1... | collective-permute-start | bytes 196616 | tf_op jit(solution)/shard_map/ppermute | solution.py:603
  59.8 2.0 %collective-permute-done.10.r1 = bf16[2,32,512]{2,1,0:T(8,128)(2,1)S(1)} collective-permute-done((bf16[2,32,512]{2,1,0:T(8,128)(2,1)S(1)}, bf16[2,32,512]{2,1,0:T(8,128)(2,1)S(1)}, u32[]{:S(2)}, u32[]{:S(2)}) %collective-permute-start.10) | collective-permute-done | bytes 65568 | tf_op jit(solution)/shard_map/ppermute | solution.py:603
  61.8 1.5 %collective-permute-done.11.r2 = bf16[2,32,512]{2,1,0:T(8,128)(2,1)S(1)} collective-permute-done((bf16[2,32,512]{2,1,0:T(8,128)(2,1)S(1)}, bf16[2,32,512]{2,1,0:T(8,128)(2,1)S(1)}, u32[]{:S(2)}, u32[]{:S(2)}) %collective-permute-start.11) | collective-permute-done | bytes 65568 | tf_op jit(solution)/shard_map/ppermute | solution.py:603
  63.3 1.2 %collective-permute-done.12.r3 = bf16[2,32,512]{2,1,0:T(8,128)(2,1)S(1)} collective-permute-done((bf16[2,32,512]{2,1,0:T(8,128)(2,1)S(1)}, bf16[2,32,512]{2,1,0:T(8,128)(2,1)S(1)}, u32[]{:S(2)}, u32[]{:S(2)}) %collective-permute-start.12) | collective-permute-done | bytes 65568 | tf_op jit(solution)/shard_map/ppermute | solution.py:603
  66.1 2.4 %collective-permute-done.13.received = bf16[32,512]{1,0:T(8,128)(2,1)S(1)} collective-permute-done((bf16[32,512]{1,0:T(8,128)(2,1)S(1)}, bf16[32,512]{1,0:T(8,128)(2,1)S(1)}, u32[]{:S(2)}, u32[]{:S(2)}) %collective-permute-start.13) | collective-permute-done | bytes 32800 | tf_op jit(solution)/shard_map/ppermute | solution.py:599
  69.2 1.7 %unpack.1 = (bf16[8,32,1024]{2,1,0:T(8,128)(2,1)}, bf16[8,32,1024]{2,1,0:T(8,128)(2,1)}, bf16[8,8]{1,0:T(8,128)(2,1)}, bf16[8,8]{1,0:T(8,128)(2,1)}) custom-call(s32[8]{0:T(128)S(1)} %copy-done.6, bf16[16,520,128]{2,1,0:T(8,128)(2,1)S(1)} %all-to-all-done.received, bf16[8,32,1024]{2,1,0:T(8,128)(2,1)S(1)} %copy-done, bf16[8,32,1024]{2,1,0:T(8,128)(2,1)S(1)} %copy-done.1, ...), custom_call_target="tpu_custom_call" | custom-call | flops 1048576 | bytes 4194304 | tf_op jit(solution)/shard_map/unpack/pallas_call | solution.py:229
  (31 shorter events, 5.2 us)
Async XLA Ops:
  0.6 14.6 %copy-start.5 = (f32[128]{0:T(128)S(1)}, f32[128]{0:T(128)}, u32[]{:S(2)}) copy-start(f32[128]{0:T(128)} %param.14) | copy-start | bytes 1540
  3.2 36.1 %copy-start = (bf16[8,32,1024]{2,1,0:T(8,128)(2,1)S(1)}, bf16[8,32,1024]{2,1,0:T(8,128)(2,1)}, u32[]{:S(2)}) copy-start(bf16[8,32,1024]{2,1,0:T(8,128)(2,1)} %keys.5) | copy-start | bytes 1572868
  3.2 36.1 %copy-start.1 = (bf16[8,32,1024]{2,1,0:T(8,128)(2,1)S(1)}, bf16[8,32,1024]{2,1,0:T(8,128)(2,1)}, u32[]{:S(2)}) copy-start(bf16[8,32,1024]{2,1,0:T(8,128)(2,1)} %values.5) | copy-start | bytes 1572868
  3.3 36.1 %copy-start.2 = (bf16[8,1,8]{2,0,1:T(8,128)(2,1)S(1)}, bf16[8,1,8]{2,0,1:T(8,128)(2,1)}, u32[]{:S(2)}) copy-start(bf16[8,1,8]{2,0,1:T(8,128)(2,1)} %param.19) | copy-start | bytes 388
  3.3 36.1 %copy-start.3 = (bf16[8,1,8]{2,0,1:T(8,128)(2,1)S(1)}, bf16[8,1,8]{2,0,1:T(8,128)(2,1)}, u32[]{:S(2)}) copy-start(bf16[8,1,8]{2,0,1:T(8,128)(2,1)} %param.20) | copy-start | bytes 388
  3.3 36.1 %copy-start.4 = (s32[8]{0:T(128)S(1)}, s32[8]{0:T(128)}, u32[]{:S(2)}) copy-start(s32[8]{0:T(128)} %lengths.1) | copy-start | bytes 100
  3.3 65.9 %all-to-all-start = ((bf16[16,520,128]{2,1,0:T(8,128)(2,1)}), bf16[16,520,128]{2,1,0:T(8,128)(2,1)S(1)}, u32[]{:S(2)}, u32[]{:S(2)}) async-start(bf16[16,520,128]{2,1,0:T(8,128)(2,1)} %get-tuple-element.46), calls=%async_computation | async-start | bytes 4259840 | tf_op jit(solution)/shard_map/all_to_all | solution.py:640
  14.0 25.3 %collective-permute-start.4 = (bf16[528,512]{1,0:T(8,128)(2,1)}, bf16[528,512]{1,0:T(8,128)(2,1)S(1)}, u32[]{:S(2)}, u32[]{:S(2)}) collective-permute-start(bf16[528,512]{1,0:T(8,128)(2,1)} %get-tuple-element.29), channel_id=1, source_target_pairs={{0,2},{1,3},{2,0},{3,1},{4,6},{5,7},{6,4},{7,5},{8,10},{9,11},{10,... | collective-permute-start | bytes 1622024 | tf_op jit(solution)/shard_map/ppermute | solution.py:599
  18.9 1.3 %collective-permute-start = (bf16[32,256]{1,0:T(8,128)(2,1)S(1)}, bf16[32,256]{1,0:T(8,128)(2,1)S(1)}, u32[]{:S(2)}, u32[]{:S(2)}) collective-permute-start(bf16[32,256]{1,0:T(8,128)(2,1)S(1)} %get-tuple-element.28), channel_id=1, source_target_pairs={{0,1},{1,0},{2,3},{3,2},{4,5},{5,4},{6,7},{7,6},{8,9},{9,8},{10,11... | collective-permute-start | bytes 49160 | tf_op jit(solution)/shard_map/ppermute | solution.py:599
  20.2 5.8 %collective-permute-start.1 = (bf16[2,32,256]{2,1,0:T(8,128)(2,1)S(1)}, bf16[2,32,256]{2,1,0:T(8,128)(2,1)S(1)}, u32[]{:S(2)}, u32[]{:S(2)}) collective-permute-start(bf16[2,32,256]{2,1,0:T(8,128)(2,1)S(1)} %pad_maximum_fusion.q0), channel_id=1, source_target_pairs={{0,4},{1,5},{2,6},{3,7},{4,8},{5,9},{6,10},{7,11},{8,12},{9,13},{1... | collective-permute-start | bytes 98312 | tf_op jit(solution)/shard_map/ppermute | solution.py:603
  21.8 5.4 %collective-permute-start.2 = (bf16[2,32,256]{2,1,0:T(8,128)(2,1)S(1)}, bf16[2,32,256]{2,1,0:T(8,128)(2,1)S(1)}, u32[]{:S(2)}, u32[]{:S(2)}) collective-permute-start(bf16[2,32,256]{2,1,0:T(8,128)(2,1)S(1)} %pad_maximum_fusion.q0), channel_id=1, source_target_pairs={{0,8},{1,9},{2,10},{3,11},{4,12},{5,13},{6,14},{7,15},{8,0},{9,1},... | collective-permute-start | bytes 98312 | tf_op jit(solution)/shard_map/ppermute | solution.py:603
  24.7 3.9 %collective-permute-start.3 = (bf16[2,32,256]{2,1,0:T(8,128)(2,1)S(1)}, bf16[2,32,256]{2,1,0:T(8,128)(2,1)S(1)}, u32[]{:S(2)}, u32[]{:S(2)}) collective-permute-start(bf16[2,32,256]{2,1,0:T(8,128)(2,1)S(1)} %pad_maximum_fusion.q0), channel_id=1, source_target_pairs={{0,12},{1,13},{2,14},{3,15},{4,0},{5,1},{6,2},{7,3},{8,4},{9,5},{1... | collective-permute-start | bytes 98312 | tf_op jit(solution)/shard_map/ppermute | solution.py:603
  41.3 4.8 %collective-permute-start.5 = (bf16[160,128]{1,0:T(8,128)(2,1)S(1)}, bf16[160,128]{1,0:T(8,128)(2,1)S(1)}, u32[]{:S(2)}, u32[]{:S(2)}) collective-permute-start(bf16[160,128]{1,0:T(8,128)(2,1)S(1)} %get-tuple-element.31), channel_id=1, source_target_pairs={{0,12},{1,13},{2,14},{3,15},{4,0},{5,1},{6,2},{7,3},{8,4},{9,5},{1... | collective-permute-start | bytes 122888 | tf_op jit(solution)/shard_map/ppermute | solution.py:603
  44.4 5.5 %collective-permute-start.6 = (bf16[160,128]{1,0:T(8,128)(2,1)S(1)}, bf16[160,128]{1,0:T(8,128)(2,1)S(1)}, u32[]{:S(2)}, u32[]{:S(2)}) collective-permute-start(bf16[160,128]{1,0:T(8,128)(2,1)S(1)} %get-tuple-element.32), channel_id=1, source_target_pairs={{0,8},{1,9},{2,10},{3,11},{4,12},{5,13},{6,14},{7,15},{8,0},{9,1},... | collective-permute-start | bytes 122888 | tf_op jit(solution)/shard_map/ppermute | solution.py:603
  45.0 5.3 %collective-permute-start.7 = (bf16[160,128]{1,0:T(8,128)(2,1)S(1)}, bf16[160,128]{1,0:T(8,128)(2,1)S(1)}, u32[]{:S(2)}, u32[]{:S(2)}) collective-permute-start(bf16[160,128]{1,0:T(8,128)(2,1)S(1)} %get-tuple-element.33), channel_id=1, source_target_pairs={{0,4},{1,5},{2,6},{3,7},{4,8},{5,9},{6,10},{7,11},{8,12},{9,13},{1... | collective-permute-start | bytes 122888 | tf_op jit(solution)/shard_map/ppermute | solution.py:603
  50.6 1.3 %collective-permute-start.8 = (bf16[96,128]{1,0:T(8,128)(2,1)S(1)}, bf16[96,128]{1,0:T(8,128)(2,1)S(1)}, u32[]{:S(2)}, u32[]{:S(2)}) collective-permute-start(bf16[96,128]{1,0:T(8,128)(2,1)S(1)} %get-tuple-element.35), channel_id=1, source_target_pairs={{0,1},{1,0},{2,3},{3,2},{4,5},{5,4},{6,7},{7,6},{8,9},{9,8},{10,11... | collective-permute-start | bytes 73736 | tf_op jit(solution)/shard_map/ppermute | solution.py:599
  51.9 17.3 %copy-start.6 = (s32[8]{0:T(128)S(1)}, s32[8]{0:T(128)}, u32[]{:S(2)}) copy-start(s32[8]{0:T(128)} %get-tuple-element.45.plan) | copy-start | bytes 100
  54.2 2.5 %collective-permute-start.9 = (bf16[8,32,512]{2,1,0:T(8,128)(2,1)S(1)}, bf16[8,32,512]{2,1,0:T(8,128)(2,1)S(1)}, u32[]{:S(2)}, u32[]{:S(2)}) collective-permute-start(bf16[8,32,512]{2,1,0:T(8,128)(2,1)S(1)} %get-tuple-element.37), channel_id=1, source_target_pairs={{0,1},{1,0},{2,3},{3,2},{4,5},{5,4},{6,7},{7,6},{8,9},{9,8},{10,11... | collective-permute-start | bytes 786440 | tf_op jit(solution)/shard_map/ppermute | solution.py:599
  56.8 5.0 %collective-permute-start.10 = (bf16[2,32,512]{2,1,0:T(8,128)(2,1)S(1)}, bf16[2,32,512]{2,1,0:T(8,128)(2,1)S(1)}, u32[]{:S(2)}, u32[]{:S(2)}) collective-permute-start(bf16[2,32,512]{2,1,0:T(8,128)(2,1)S(1)} %get-tuple-element.39), channel_id=1, source_target_pairs={{0,12},{1,13},{2,14},{3,15},{4,0},{5,1},{6,2},{7,3},{8,4},{9,5},{1... | collective-permute-start | bytes 196616 | tf_op jit(solution)/shard_map/ppermute | solution.py:603
  57.4 5.9 %collective-permute-start.11 = (bf16[2,32,512]{2,1,0:T(8,128)(2,1)S(1)}, bf16[2,32,512]{2,1,0:T(8,128)(2,1)S(1)}, u32[]{:S(2)}, u32[]{:S(2)}) collective-permute-start(bf16[2,32,512]{2,1,0:T(8,128)(2,1)S(1)} %get-tuple-element.40), channel_id=1, source_target_pairs={{0,8},{1,9},{2,10},{3,11},{4,12},{5,13},{6,14},{7,15},{8,0},{9,1},... | collective-permute-start | bytes 196616 | tf_op jit(solution)/shard_map/ppermute | solution.py:603
  58.6 5.9 %collective-permute-start.12 = (bf16[2,32,512]{2,1,0:T(8,128)(2,1)S(1)}, bf16[2,32,512]{2,1,0:T(8,128)(2,1)S(1)}, u32[]{:S(2)}, u32[]{:S(2)}) collective-permute-start(bf16[2,32,512]{2,1,0:T(8,128)(2,1)S(1)} %get-tuple-element.41), channel_id=1, source_target_pairs={{0,4},{1,5},{2,6},{3,7},{4,8},{5,9},{6,10},{7,11},{8,12},{9,13},{1... | collective-permute-start | bytes 196616 | tf_op jit(solution)/shard_map/ppermute | solution.py:603
  64.5 4.0 %collective-permute-start.13 = (bf16[32,512]{1,0:T(8,128)(2,1)S(1)}, bf16[32,512]{1,0:T(8,128)(2,1)S(1)}, u32[]{:S(2)}, u32[]{:S(2)}) collective-permute-start(bf16[32,512]{1,0:T(8,128)(2,1)S(1)} %get-tuple-element.43), channel_id=1, source_target_pairs={{0,2},{1,3},{2,0},{3,1},{4,6},{5,7},{6,4},{7,5},{8,10},{9,11},{10,... | collective-permute-start | bytes 98312 | tf_op jit(solution)/shard_map/ppermute | solution.py:599

commit v6 on v5

--- a/solution.py
+++ b/solution.py
@@ -98,9 +98,6 @@
     plan_copy.start()
     scale_rows(scr, scales.at[0], scales.at[1])
     row = iota((8, HD), 0)
-    for r in range(HELD):
-        for copy in loads(r):
-            copy.wait()
     stores = []
     for j in range(MOVE):
         s = slots[0, j]
@@ -110,13 +107,21 @@
             jnp.where(row == 1, scr[pl.ds(HELD + s, 1), :], 0.0),
         )
         stage[j, 2 * KVH * SPAN : SLOT, :] = both.astype(BF16)
-        for which in range(2):
+        for which, copy in enumerate(loads(s)):
+            copy.wait()
             for c in range(KVH):
                 at_row = (which * KVH + c) * SPAN
                 stage[j, at_row : at_row + SPAN, :] = held[s, which, :, c * HD : (c + 1) * HD]
         copy = pltpu.make_async_copy(stage.at[j], message.at[dest[j, here]], out_sem.at[j])
         copy.start()
         stores.append(copy)
+    for r in range(HELD):
+
+        @pl.when(plan[r] < 0)
+        def _():
+            for copy in loads(r):
+                copy.wait()
+
     for i in range(KVH // 2):
         start = pl.multiple_of((2 * i + 1 - x) * HD, HD)
         for which in range(2):

time: 71.1 us -> 71 us (level)
  no operation moved by 1% of the time
where the time goes in v6:
time: 71 us; the launch traced here: 70.8 us
  waiting for transfers between devices  27.1 us (38%)
  starting transfers between devices  26.8 us (38%)
  Pallas kernels  15.4 us (22%)
  between operations  1.44 us (2%)
    ppermute x5, waiting for transfers between devices, swap(): lax.ppermute(array, 'tensor', [(i, i ^ bits) for i in range(TENSORS)])  15.5 us
    ppermute x9, starting transfers between devices, shift(): lax.ppermute(array, 'tensor', [(i, (i + 4 * rows) % TENSORS) for i in ran...  13.6 us
    ppermute x9, waiting for transfers between devices, shift(): lax.ppermute(array, 'tensor', [(i, (i + 4 * rows) % TENSORS) for i in ran...  11.6 us
    all_to_all x1, starting transfers between devices, local(): lax.all_to_all(message, 'replica', split_axis=0, concat_axis=0, tiled=True)  10.6 us
    pallas_call x1, Pallas kernels, project_query(): pl.pallas_call(query_kernel, out_shape=(shape((ROWS, 2 * HD), BF16), shap...  3.7 us
    pallas_call x1, Pallas kernels, front(): pl.pallas_call(front_kernel, out_shape=(shape((REPLICAS, SLOT, HD), BF16)...  2.64 us
    ppermute x5, starting transfers between devices, swap(): lax.ppermute(array, 'tensor', [(i, i ^ bits) for i in range(TENSORS)])  2.55 us
    pallas_call x1, Pallas kernels, output_other(): pl.pallas_call(output_other_kernel, out_shape=(shape((ROWS, 2 * HD), BF16...  2.28 us
  transfers between devices with their start and end apart: 15, of which 12 were waited for; matrix products, arithmetic and copies ran while one was open for 0% of the time, Pallas kernels for 16%

profile of v6, /device:TPU:68, one launch (start us, length us, event | category | flops | bytes accessed | tf_op | source)
XLA Modules:
  0.0 70.8 jit_solution(9758787033037730012)
XLA Ops:
  0.6 2.6 %front.1 = (bf16[16,520,128]{2,1,0:T(8,128)(2,1)}, bf16[528,512]{1,0:T(8,128)(2,1)}, s32[8]{0:T(128)}) custom-call(s32[6,16]{1,0:T(8,128)} %bitcast.17, s32[1,6]{1,0:T(1,128)} %slots_in.1, bf16[8,32,1024]{2,1,0:T(8,128)(2,1)} %keys.5, bf16[8,32,1024]{2,1,0:T(8,128)(2,1)} %values.5, bf16[8,8]{1,0:T(8,128)(2,1)} %bitcast.8, bf16[8,8]{1,0:T(8,128)(2,1)} %bitcast.11), custom_call_target="tpu_custom_call" | custom-call | flops 1048576 | bytes 4194304 | tf_op jit(solution)/shard_map/front/pallas_call | solution.py:145
  3.3 10.6 %all-to-all-start = ((bf16[16,520,128]{2,1,0:T(8,128)(2,1)}), bf16[16,520,128]{2,1,0:T(8,128)(2,1)S(1)}, u32[]{:S(2)}, u32[]{:S(2)}) async-start(bf16[16,520,128]{2,1,0:T(8,128)(2,1)} %get-tuple-element.46), calls=%async_computation | async-start | bytes 4259840 | tf_op jit(solution)/shard_map/all_to_all | solution.py:645
  13.9 1.2 %collective-permute-start.4 = (bf16[528,512]{1,0:T(8,128)(2,1)}, bf16[528,512]{1,0:T(8,128)(2,1)S(1)}, u32[]{:S(2)}, u32[]{:S(2)}) collective-permute-start(bf16[528,512]{1,0:T(8,128)(2,1)} %get-tuple-element.29), channel_id=1, source_target_pairs={{0,2},{1,3},{2,0},{3,1},{4,6},{5,7},{6,4},{7,5},{8,10},{9,11},{10,... | collective-permute-start | bytes 1622024 | tf_op jit(solution)/shard_map/ppermute | solution.py:604
  15.1 3.7 %query.1 = (bf16[32,256]{1,0:T(8,128)(2,1)S(1)}, bf16[32,512]{1,0:T(8,128)(2,1)S(1)}) custom-call(bf16[32,8192]{1,0:T(8,128)(2,1)} %hidden.1, bf16[8192,256]{1,0:T(8,128)(2,1)} %weight.3, f32[1,128]{1,0:T(1,128)S(1)} %bitcast.15), custom_call_target="tpu_custom_call" | custom-call | flops 4194304 | bytes 5242880 | tf_op jit(solution)/shard_map/query/pallas_call | solution.py:286
  19.0 1.2 %collective-permute-done = bf16[32,256]{1,0:T(8,128)(2,1)S(1)} collective-permute-done((bf16[32,256]{1,0:T(8,128)(2,1)S(1)}, bf16[32,256]{1,0:T(8,128)(2,1)S(1)}, u32[]{:S(2)}, u32[]{:S(2)}) %collective-permute-start) | collective-permute-done | bytes 16416 | tf_op jit(solution)/shard_map/ppermute | solution.py:604
  20.1 1.6 %collective-permute-start.1 = (bf16[2,32,256]{2,1,0:T(8,128)(2,1)S(1)}, bf16[2,32,256]{2,1,0:T(8,128)(2,1)S(1)}, u32[]{:S(2)}, u32[]{:S(2)}) collective-permute-start(bf16[2,32,256]{2,1,0:T(8,128)(2,1)S(1)} %pad_maximum_fusion.q0), channel_id=1, source_target_pairs={{0,4},{1,5},{2,6},{3,7},{4,8},{5,9},{6,10},{7,11},{8,12},{9,13},{1... | collective-permute-start | bytes 98312 | tf_op jit(solution)/shard_map/ppermute | solution.py:608
  21.7 2.9 %collective-permute-start.2 = (bf16[2,32,256]{2,1,0:T(8,128)(2,1)S(1)}, bf16[2,32,256]{2,1,0:T(8,128)(2,1)S(1)}, u32[]{:S(2)}, u32[]{:S(2)}) collective-permute-start(bf16[2,32,256]{2,1,0:T(8,128)(2,1)S(1)} %pad_maximum_fusion.q0), channel_id=1, source_target_pairs={{0,8},{1,9},{2,10},{3,11},{4,12},{5,13},{6,14},{7,15},{8,0},{9,1},... | collective-permute-start | bytes 98312 | tf_op jit(solution)/shard_map/ppermute | solution.py:608
  24.6 1.3 %collective-permute-start.3 = (bf16[2,32,256]{2,1,0:T(8,128)(2,1)S(1)}, bf16[2,32,256]{2,1,0:T(8,128)(2,1)S(1)}, u32[]{:S(2)}, u32[]{:S(2)}) collective-permute-start(bf16[2,32,256]{2,1,0:T(8,128)(2,1)S(1)} %pad_maximum_fusion.q0), channel_id=1, source_target_pairs={{0,12},{1,13},{2,14},{3,15},{4,0},{5,1},{6,2},{7,3},{8,4},{9,5},{1... | collective-permute-start | bytes 98312 | tf_op jit(solution)/shard_map/ppermute | solution.py:608
  26.0 1.2 %collective-permute-done.2.q2 = bf16[2,32,256]{2,1,0:T(8,128)(2,1)S(1)} collective-permute-done((bf16[2,32,256]{2,1,0:T(8,128)(2,1)S(1)}, bf16[2,32,256]{2,1,0:T(8,128)(2,1)S(1)}, u32[]{:S(2)}, u32[]{:S(2)}) %collective-permute-start.2) | collective-permute-done | bytes 32800 | tf_op jit(solution)/shard_map/ppermute | solution.py:608
  27.1 1.4 %collective-permute-done.3.q3 = bf16[2,32,256]{2,1,0:T(8,128)(2,1)S(1)} collective-permute-done((bf16[2,32,256]{2,1,0:T(8,128)(2,1)S(1)}, bf16[2,32,256]{2,1,0:T(8,128)(2,1)S(1)}, u32[]{:S(2)}, u32[]{:S(2)}) %collective-permute-start.3) | collective-permute-done | bytes 32800 | tf_op jit(solution)/shard_map/ppermute | solution.py:608
  28.5 10.8 %collective-permute-done.4.other = bf16[528,512]{1,0:T(8,128)(2,1)S(1)} collective-permute-done((bf16[528,512]{1,0:T(8,128)(2,1)}, bf16[528,512]{1,0:T(8,128)(2,1)S(1)}, u32[]{:S(2)}, u32[]{:S(2)}) %collective-permute-start.4) | collective-permute-done | bytes 540704 | tf_op jit(solution)/shard_map/ppermute | solution.py:604
  39.3 1.9 %attend.1 = (bf16[160,128]{1,0:T(8,128)(2,1)S(1)}, bf16[160,128]{1,0:T(8,128)(2,1)S(1)}, bf16[160,128]{1,0:T(8,128)(2,1)S(1)}, bf16[160,128]{1,0:T(8,128)(2,1)S(1)}) custom-call(s32[8]{0:T(128)S(1)} %copy-done.4, bf16[2,32,256]{2,1,0:T(8,128)(2,1)S(1)} %pad_maximum_fusion.q0, bf16[2,32,256]{2,1,0:T(8,128)(2,1)S(1)} %collective-permute-done.1.q1, ...), custom_call_target="tpu_custom_call" | custom-call | flops 4194304 | bytes 2097152 | tf_op jit(solution)/shard_map/attend/pallas_call | solution.py:413
  41.2 3.1 %collective-permute-start.5 = (bf16[160,128]{1,0:T(8,128)(2,1)S(1)}, bf16[160,128]{1,0:T(8,128)(2,1)S(1)}, u32[]{:S(2)}, u32[]{:S(2)}) collective-permute-start(bf16[160,128]{1,0:T(8,128)(2,1)S(1)} %get-tuple-element.31), channel_id=1, source_target_pairs={{0,12},{1,13},{2,14},{3,15},{4,0},{5,1},{6,2},{7,3},{8,4},{9,5},{1... | collective-permute-start | bytes 122888 | tf_op jit(solution)/shard_map/ppermute | solution.py:608
  46.0 3.8 %collective-permute-done.6.p2 = bf16[160,128]{1,0:T(8,128)(2,1)S(1)} collective-permute-done((bf16[160,128]{1,0:T(8,128)(2,1)S(1)}, bf16[160,128]{1,0:T(8,128)(2,1)S(1)}, u32[]{:S(2)}, u32[]{:S(2)}) %collective-permute-start.6) | collective-permute-done | bytes 40992 | tf_op jit(solution)/shard_map/ppermute | solution.py:608
  50.6 1.2 %collective-permute-done.8.p1 = bf16[96,128]{1,0:T(8,128)(2,1)S(1)} collective-permute-done((bf16[96,128]{1,0:T(8,128)(2,1)S(1)}, bf16[96,128]{1,0:T(8,128)(2,1)S(1)}, u32[]{:S(2)}, u32[]{:S(2)}) %collective-permute-start.8) | collective-permute-done | bytes 24608 | tf_op jit(solution)/shard_map/ppermute | solution.py:604
  51.8 2.3 %output_other.1 = (bf16[32,256]{1,0:T(8,128)(2,1)S(1)}, bf16[8,32,512]{2,1,0:T(8,128)(2,1)S(1)}) custom-call(bf16[96,128]{1,0:T(8,128)(2,1)S(1)} %get-tuple-element.34.p0, bf16[96,128]{1,0:T(8,128)(2,1)S(1)} %collective-permute-done.8.p1, bf16[256,8192]{1,0:T(8,128)(2,1)} %weight.5), custom_call_target="tpu_custom_call" | custom-call | flops 4194304 | bytes 2097152 | tf_op jit(solution)/shard_map/output_other/pallas_call | solution.py:513
  54.3 2.3 %output_own.1.own = f32[8,32,512]{2,1,0:T(8,128)S(1)} custom-call(bf16[32,256]{1,0:T(8,128)(2,1)S(1)} %get-tuple-element.36.attended, bf16[256,8192]{1,0:T(8,128)(2,1)} %weight.5), custom_call_target="tpu_custom_call" | custom-call | flops 4194304 | bytes 2097152 | tf_op jit(solution)/shard_map/output_own/pallas_call | solution.py:529
  57.3 1.2 %collective-permute-start.11 = (bf16[2,32,512]{2,1,0:T(8,128)(2,1)S(1)}, bf16[2,32,512]{2,1,0:T(8,128)(2,1)S(1)}, u32[]{:S(2)}, u32[]{:S(2)}) collective-permute-start(bf16[2,32,512]{2,1,0:T(8,128)(2,1)S(1)} %get-tuple-element.40), channel_id=1, source_target_pairs={{0,8},{1,9},{2,10},{3,11},{4,12},{5,13},{6,14},{7,15},{8,0},{9,1},... | collective-permute-start | bytes 196616 | tf_op jit(solution)/shard_map/ppermute | solution.py:608
  58.5 1.3 %collective-permute-start.12 = (bf16[2,32,512]{2,1,0:T(8,128)(2,1)S(1)}, bf16[2,32,512]{2,1,0:T(8,128)(2,1)S(1)}, u32[]{:S(2)}, u32[]{:S(2)}) collective-permute-start(bf16[2,32,512]{2,1,0:T(8,128)(2,1)S(1)} %get-tuple-element.41), channel_id=1, source_target_pairs={{0,4},{1,5},{2,6},{3,7},{4,8},{5,9},{6,10},{7,11},{8,12},{9,13},{1... | collective-permute-start | bytes 196616 | tf_op jit(solution)/shard_map/ppermute | solution.py:608
  59.8 2.0 %collective-permute-done.10.r1 = bf16[2,32,512]{2,1,0:T(8,128)(2,1)S(1)} collective-permute-done((bf16[2,32,512]{2,1,0:T(8,128)(2,1)S(1)}, bf16[2,32,512]{2,1,0:T(8,128)(2,1)S(1)}, u32[]{:S(2)}, u32[]{:S(2)}) %collective-permute-start.10) | collective-permute-done | bytes 65568 | tf_op jit(solution)/shard_map/ppermute | solution.py:608
  61.7 1.5 %collective-permute-done.11.r2 = bf16[2,32,512]{2,1,0:T(8,128)(2,1)S(1)} collective-permute-done((bf16[2,32,512]{2,1,0:T(8,128)(2,1)S(1)}, bf16[2,32,512]{2,1,0:T(8,128)(2,1)S(1)}, u32[]{:S(2)}, u32[]{:S(2)}) %collective-permute-start.11) | collective-permute-done | bytes 65568 | tf_op jit(solution)/shard_map/ppermute | solution.py:608
  63.2 1.2 %collective-permute-done.12.r3 = bf16[2,32,512]{2,1,0:T(8,128)(2,1)S(1)} collective-permute-done((bf16[2,32,512]{2,1,0:T(8,128)(2,1)S(1)}, bf16[2,32,512]{2,1,0:T(8,128)(2,1)S(1)}, u32[]{:S(2)}, u32[]{:S(2)}) %collective-permute-start.12) | collective-permute-done | bytes 65568 | tf_op jit(solution)/shard_map/ppermute | solution.py:608
  66.0 2.4 %collective-permute-done.13.received = bf16[32,512]{1,0:T(8,128)(2,1)S(1)} collective-permute-done((bf16[32,512]{1,0:T(8,128)(2,1)S(1)}, bf16[32,512]{1,0:T(8,128)(2,1)S(1)}, u32[]{:S(2)}, u32[]{:S(2)}) %collective-permute-start.13) | collective-permute-done | bytes 32800 | tf_op jit(solution)/shard_map/ppermute | solution.py:604
  69.1 1.7 %unpack.1 = (bf16[8,32,1024]{2,1,0:T(8,128)(2,1)}, bf16[8,32,1024]{2,1,0:T(8,128)(2,1)}, bf16[8,8]{1,0:T(8,128)(2,1)}, bf16[8,8]{1,0:T(8,128)(2,1)}) custom-call(s32[8]{0:T(128)S(1)} %copy-done.6, bf16[16,520,128]{2,1,0:T(8,128)(2,1)S(1)} %all-to-all-done.received, bf16[8,32,1024]{2,1,0:T(8,128)(2,1)S(1)} %copy-done, bf16[8,32,1024]{2,1,0:T(8,128)(2,1)S(1)} %copy-done.1, ...), custom_call_target="tpu_custom_call" | custom-call | flops 1048576 | bytes 4194304 | tf_op jit(solution)/shard_map/unpack/pallas_call | solution.py:234
  (31 shorter events, 5.1 us)
Async XLA Ops:
  0.6 14.5 %copy-start.5 = (f32[128]{0:T(128)S(1)}, f32[128]{0:T(128)}, u32[]{:S(2)}) copy-start(f32[128]{0:T(128)} %param.14) | copy-start | bytes 1540
  3.3 36.0 %copy-start = (bf16[8,32,1024]{2,1,0:T(8,128)(2,1)S(1)}, bf16[8,32,1024]{2,1,0:T(8,128)(2,1)}, u32[]{:S(2)}) copy-start(bf16[8,32,1024]{2,1,0:T(8,128)(2,1)} %keys.5) | copy-start | bytes 1572868
  3.3 36.0 %copy-start.1 = (bf16[8,32,1024]{2,1,0:T(8,128)(2,1)S(1)}, bf16[8,32,1024]{2,1,0:T(8,128)(2,1)}, u32[]{:S(2)}) copy-start(bf16[8,32,1024]{2,1,0:T(8,128)(2,1)} %values.5) | copy-start | bytes 1572868
  3.3 36.0 %copy-start.2 = (bf16[8,1,8]{2,0,1:T(8,128)(2,1)S(1)}, bf16[8,1,8]{2,0,1:T(8,128)(2,1)}, u32[]{:S(2)}) copy-start(bf16[8,1,8]{2,0,1:T(8,128)(2,1)} %param.19) | copy-start | bytes 388
  3.3 36.0 %copy-start.3 = (bf16[8,1,8]{2,0,1:T(8,128)(2,1)S(1)}, bf16[8,1,8]{2,0,1:T(8,128)(2,1)}, u32[]{:S(2)}) copy-start(bf16[8,1,8]{2,0,1:T(8,128)(2,1)} %param.20) | copy-start | bytes 388
  3.3 36.0 %copy-start.4 = (s32[8]{0:T(128)S(1)}, s32[8]{0:T(128)}, u32[]{:S(2)}) copy-start(s32[8]{0:T(128)} %lengths.1) | copy-start | bytes 100
  3.3 65.8 %all-to-all-start = ((bf16[16,520,128]{2,1,0:T(8,128)(2,1)}), bf16[16,520,128]{2,1,0:T(8,128)(2,1)S(1)}, u32[]{:S(2)}, u32[]{:S(2)}) async-start(bf16[16,520,128]{2,1,0:T(8,128)(2,1)} %get-tuple-element.46), calls=%async_computation | async-start | bytes 4259840 | tf_op jit(solution)/shard_map/all_to_all | solution.py:645
  13.9 25.3 %collective-permute-start.4 = (bf16[528,512]{1,0:T(8,128)(2,1)}, bf16[528,512]{1,0:T(8,128)(2,1)S(1)}, u32[]{:S(2)}, u32[]{:S(2)}) collective-permute-start(bf16[528,512]{1,0:T(8,128)(2,1)} %get-tuple-element.29), channel_id=1, source_target_pairs={{0,2},{1,3},{2,0},{3,1},{4,6},{5,7},{6,4},{7,5},{8,10},{9,11},{10,... | collective-permute-start | bytes 1622024 | tf_op jit(solution)/shard_map/ppermute | solution.py:604
  18.9 1.3 %collective-permute-start = (bf16[32,256]{1,0:T(8,128)(2,1)S(1)}, bf16[32,256]{1,0:T(8,128)(2,1)S(1)}, u32[]{:S(2)}, u32[]{:S(2)}) collective-permute-start(bf16[32,256]{1,0:T(8,128)(2,1)S(1)} %get-tuple-element.28), channel_id=1, source_target_pairs={{0,1},{1,0},{2,3},{3,2},{4,5},{5,4},{6,7},{7,6},{8,9},{9,8},{10,11... | collective-permute-start | bytes 49160 | tf_op jit(solution)/shard_map/ppermute | solution.py:604
  20.1 5.8 %collective-permute-start.1 = (bf16[2,32,256]{2,1,0:T(8,128)(2,1)S(1)}, bf16[2,32,256]{2,1,0:T(8,128)(2,1)S(1)}, u32[]{:S(2)}, u32[]{:S(2)}) collective-permute-start(bf16[2,32,256]{2,1,0:T(8,128)(2,1)S(1)} %pad_maximum_fusion.q0), channel_id=1, source_target_pairs={{0,4},{1,5},{2,6},{3,7},{4,8},{5,9},{6,10},{7,11},{8,12},{9,13},{1... | collective-permute-start | bytes 98312 | tf_op jit(solution)/shard_map/ppermute | solution.py:608
  21.7 5.4 %collective-permute-start.2 = (bf16[2,32,256]{2,1,0:T(8,128)(2,1)S(1)}, bf16[2,32,256]{2,1,0:T(8,128)(2,1)S(1)}, u32[]{:S(2)}, u32[]{:S(2)}) collective-permute-start(bf16[2,32,256]{2,1,0:T(8,128)(2,1)S(1)} %pad_maximum_fusion.q0), channel_id=1, source_target_pairs={{0,8},{1,9},{2,10},{3,11},{4,12},{5,13},{6,14},{7,15},{8,0},{9,1},... | collective-permute-start | bytes 98312 | tf_op jit(solution)/shard_map/ppermute | solution.py:608
  24.6 3.9 %collective-permute-start.3 = (bf16[2,32,256]{2,1,0:T(8,128)(2,1)S(1)}, bf16[2,32,256]{2,1,0:T(8,128)(2,1)S(1)}, u32[]{:S(2)}, u32[]{:S(2)}) collective-permute-start(bf16[2,32,256]{2,1,0:T(8,128)(2,1)S(1)} %pad_maximum_fusion.q0), channel_id=1, source_target_pairs={{0,12},{1,13},{2,14},{3,15},{4,0},{5,1},{6,2},{7,3},{8,4},{9,5},{1... | collective-permute-start | bytes 98312 | tf_op jit(solution)/shard_map/ppermute | solution.py:608
  41.2 4.8 %collective-permute-start.5 = (bf16[160,128]{1,0:T(8,128)(2,1)S(1)}, bf16[160,128]{1,0:T(8,128)(2,1)S(1)}, u32[]{:S(2)}, u32[]{:S(2)}) collective-permute-start(bf16[160,128]{1,0:T(8,128)(2,1)S(1)} %get-tuple-element.31), channel_id=1, source_target_pairs={{0,12},{1,13},{2,14},{3,15},{4,0},{5,1},{6,2},{7,3},{8,4},{9,5},{1... | collective-permute-start | bytes 122888 | tf_op jit(solution)/shard_map/ppermute | solution.py:608
  44.3 5.5 %collective-permute-start.6 = (bf16[160,128]{1,0:T(8,128)(2,1)S(1)}, bf16[160,128]{1,0:T(8,128)(2,1)S(1)}, u32[]{:S(2)}, u32[]{:S(2)}) collective-permute-start(bf16[160,128]{1,0:T(8,128)(2,1)S(1)} %get-tuple-element.32), channel_id=1, source_target_pairs={{0,8},{1,9},{2,10},{3,11},{4,12},{5,13},{6,14},{7,15},{8,0},{9,1},... | collective-permute-start | bytes 122888 | tf_op jit(solution)/shard_map/ppermute | solution.py:608
  44.9 5.3 %collective-permute-start.7 = (bf16[160,128]{1,0:T(8,128)(2,1)S(1)}, bf16[160,128]{1,0:T(8,128)(2,1)S(1)}, u32[]{:S(2)}, u32[]{:S(2)}) collective-permute-start(bf16[160,128]{1,0:T(8,128)(2,1)S(1)} %get-tuple-element.33), channel_id=1, source_target_pairs={{0,4},{1,5},{2,6},{3,7},{4,8},{5,9},{6,10},{7,11},{8,12},{9,13},{1... | collective-permute-start | bytes 122888 | tf_op jit(solution)/shard_map/ppermute | solution.py:608
  50.5 1.3 %collective-permute-start.8 = (bf16[96,128]{1,0:T(8,128)(2,1)S(1)}, bf16[96,128]{1,0:T(8,128)(2,1)S(1)}, u32[]{:S(2)}, u32[]{:S(2)}) collective-permute-start(bf16[96,128]{1,0:T(8,128)(2,1)S(1)} %get-tuple-element.35), channel_id=1, source_target_pairs={{0,1},{1,0},{2,3},{3,2},{4,5},{5,4},{6,7},{7,6},{8,9},{9,8},{10,11... | collective-permute-start | bytes 73736 | tf_op jit(solution)/shard_map/ppermute | solution.py:604
  51.8 17.3 %copy-start.6 = (s32[8]{0:T(128)S(1)}, s32[8]{0:T(128)}, u32[]{:S(2)}) copy-start(s32[8]{0:T(128)} %get-tuple-element.45.plan) | copy-start | bytes 100
  54.1 2.5 %collective-permute-start.9 = (bf16[8,32,512]{2,1,0:T(8,128)(2,1)S(1)}, bf16[8,32,512]{2,1,0:T(8,128)(2,1)S(1)}, u32[]{:S(2)}, u32[]{:S(2)}) collective-permute-start(bf16[8,32,512]{2,1,0:T(8,128)(2,1)S(1)} %get-tuple-element.37), channel_id=1, source_target_pairs={{0,1},{1,0},{2,3},{3,2},{4,5},{5,4},{6,7},{7,6},{8,9},{9,8},{10,11... | collective-permute-start | bytes 786440 | tf_op jit(solution)/shard_map/ppermute | solution.py:604
  56.7 5.0 %collective-permute-start.10 = (bf16[2,32,512]{2,1,0:T(8,128)(2,1)S(1)}, bf16[2,32,512]{2,1,0:T(8,128)(2,1)S(1)}, u32[]{:S(2)}, u32[]{:S(2)}) collective-permute-start(bf16[2,32,512]{2,1,0:T(8,128)(2,1)S(1)} %get-tuple-element.39), channel_id=1, source_target_pairs={{0,12},{1,13},{2,14},{3,15},{4,0},{5,1},{6,2},{7,3},{8,4},{9,5},{1... | collective-permute-start | bytes 196616 | tf_op jit(solution)/shard_map/ppermute | solution.py:608
  57.3 5.9 %collective-permute-start.11 = (bf16[2,32,512]{2,1,0:T(8,128)(2,1)S(1)}, bf16[2,32,512]{2,1,0:T(8,128)(2,1)S(1)}, u32[]{:S(2)}, u32[]{:S(2)}) collective-permute-start(bf16[2,32,512]{2,1,0:T(8,128)(2,1)S(1)} %get-tuple-element.40), channel_id=1, source_target_pairs={{0,8},{1,9},{2,10},{3,11},{4,12},{5,13},{6,14},{7,15},{8,0},{9,1},... | collective-permute-start | bytes 196616 | tf_op jit(solution)/shard_map/ppermute | solution.py:608
  58.5 5.9 %collective-permute-start.12 = (bf16[2,32,512]{2,1,0:T(8,128)(2,1)S(1)}, bf16[2,32,512]{2,1,0:T(8,128)(2,1)S(1)}, u32[]{:S(2)}, u32[]{:S(2)}) collective-permute-start(bf16[2,32,512]{2,1,0:T(8,128)(2,1)S(1)} %get-tuple-element.41), channel_id=1, source_target_pairs={{0,4},{1,5},{2,6},{3,7},{4,8},{5,9},{6,10},{7,11},{8,12},{9,13},{1... | collective-permute-start | bytes 196616 | tf_op jit(solution)/shard_map/ppermute | solution.py:608
  64.5 4.0 %collective-permute-start.13 = (bf16[32,512]{1,0:T(8,128)(2,1)S(1)}, bf16[32,512]{1,0:T(8,128)(2,1)S(1)}, u32[]{:S(2)}, u32[]{:S(2)}) collective-permute-start(bf16[32,512]{1,0:T(8,128)(2,1)S(1)} %get-tuple-element.43), channel_id=1, source_target_pairs={{0,2},{1,3},{2,0},{3,1},{4,6},{5,7},{6,4},{7,5},{8,10},{9,11},{10,... | collective-permute-start | bytes 98312 | tf_op jit(solution)/shard_map/ppermute | solution.py:604
